TPU v7x, 512 devices: a whole 4x4x16 slice. The times are simulated.
512 devices in a mesh: section: 16 (over x_lo, y, core), shard: 32 (over z, x_hi).
Axes of the slice: x: 4 (x_hi: 2, x_lo: 2; x = x_hi * 2 + x_lo), y: 4, z: 16, core: 2. Of those that a mesh axis runs over, the one named last changes fastest.
Arguments:
- train_weights: float32 [16, 16384, 1024], P('section', 'shard'), may hold values from -0.046875 to 0.046875
- section_to_group: int32 [16], replicated, may hold values from 0 to 15, each once
- hidden: bfloat16 [2048, 16384], P(('section', 'shard')), may hold values from -6 to 6
- queries: bfloat16 [8192, 2048], P(('section', 'shard')), may hold values from -100 to 100
- kv_cache: bfloat16 [8192, 128, 256], P(('section', 'shard')), may hold values from -5 to 5
- lengths: int32 [2048], P('section'), may hold values from 2 to 127, as said below
Outputs:
- context: bfloat16 [8192, 2048], P(('section', 'shard'))
- layer_out: bfloat16 [16, 4, 256, 16384], P('section', None, 'shard')
Inputs may be any that keep to these rules, and one draw needn't show every extreme that they name: `section_to_group`: a permutation: each rollout group runs exactly one trainer section's layer. `lengths`: every row has at least two cached tokens; some row of every device has 127.
All inputs are finite; a program needn't handle non-finite values.
Results may differ from a plain program's by a relative error of at most 0.006.
Values may be sent and summed in bfloat16 or wider, within the bound.
No kernel may reach another device: no remote copies, remote signals or barrier semaphores. Data moves between devices by JAX's collectives and lax.ppermute only.
A program may use at most 64 MiB of HBM per device.

v0:
```python
import math

import jax
import jax.numpy as jnp
from jax import lax
from jax.sharding import PartitionSpec as P

D = 16384
HD = 128
QPK = 16
KVH = 4
LEN = 128
ROWS = 128


def route(blocks, source):
    spread = lax.all_to_all(blocks, "section", split_axis=2, concat_axis=0, tiled=True)
    picked = jnp.take(spread, source, axis=0)
    return lax.all_to_all(picked, "section", split_axis=0, concat_axis=2, tiled=True)


def attend(query_rows, cache_rows, fresh_rows, row_lengths):
    score_scale = 1.0 / math.sqrt(HD)
    cached_keys = cache_rows[:, :, :HD]
    cached_values = cache_rows[:, :, HD:]
    key_new = fresh_rows[:, :HD]
    value_new = fresh_rows[:, HD:]
    scores = (
        jnp.einsum("rhd,rtd->rht", query_rows, cached_keys, preferred_element_type=jnp.float32)
        * score_scale
    )
    valid = jnp.arange(LEN)[None, None, :] < row_lengths[:, None, None]
    scores = jnp.where(valid, scores, -1e30)
    fresh_score = (
        jnp.einsum("rhd,rd->rh", query_rows, key_new, preferred_element_type=jnp.float32)
        * score_scale
    )
    highest = jnp.maximum(jnp.max(scores, axis=-1), fresh_score)
    weights = jnp.where(valid, jnp.exp(scores - highest[..., None]), 0.0)
    fresh_weight = jnp.exp(fresh_score - highest)
    total = jnp.sum(weights, axis=-1) + fresh_weight
    probs = (weights / total[..., None]).astype(jnp.bfloat16)
    fresh_prob = (fresh_weight / total).astype(jnp.bfloat16)
    context = jnp.einsum("rht,rtd->rhd", probs, cached_values, preferred_element_type=jnp.float32)
    context = (
        context
        + fresh_prob.astype(jnp.float32)[..., None] * value_new.astype(jnp.float32)[:, None, :]
    )
    return context.reshape(context.shape[0], QPK * HD).astype(jnp.bfloat16)


def body(train_weights, section_to_group, hidden, queries, kv_cache, lengths):
    shards = lax.axis_size("shard")
    per_head = shards // KVH
    row_block = ROWS // per_head
    piece_cols = 2 * HD // shards
    source = jnp.argsort(section_to_group)
    flipped = train_weights[0].astype(jnp.bfloat16).T
    slice_rows = flipped.shape[1]
    routed = route(flipped[None], source)[0]
    pieces = routed.reshape(KVH, shards, piece_cols, slice_rows).transpose(1, 0, 2, 3)
    column_block = lax.all_to_all(pieces, "shard", split_axis=0, concat_axis=3, tiled=True)
    column_block = column_block.reshape(KVH * piece_cols, D)
    product = lax.dot_general(
        lax.all_gather(hidden, "shard", axis=0, tiled=True),
        column_block,
        (((1,), (1,)), ((), ())),
        preferred_element_type=jnp.float32,
    )
    fresh_cols = product.astype(jnp.bfloat16)
    arranged = fresh_cols.reshape(per_head, row_block, KVH, piece_cols).transpose(2, 0, 1, 3)
    arranged = arranged.reshape(shards, row_block, piece_cols)
    fresh = lax.all_to_all(arranged, "shard", split_axis=0, concat_axis=2, tiled=True)[0]
    position = lax.axis_index("shard")
    block_index = position % per_head
    row_lengths = lax.dynamic_slice_in_dim(lengths, block_index * row_block, row_block, 0)
    query_rows = queries.reshape(row_block, QPK, HD)
    context = attend(query_rows, kv_cache, fresh, row_lengths)
    layer_out = column_block.reshape(1, KVH, piece_cols, D)
    return (context, layer_out)


def solution(mesh):
    return jax.shard_map(
        body,
        mesh=mesh,
        in_specs=(
            P("section", "shard", None),
            P(),
            P(("section", "shard"), None),
            P(("section", "shard"), None),
            P(("section", "shard"), None, None),
            P("section"),
        ),
        out_specs=(P(("section", "shard"), None), P("section", None, "shard", None)),
        check_vma=False,
    )
```

profile of v0, /device:TPU:2, one launch (start us, length us, event | category | flops | bytes accessed | tf_op | source)
XLA Modules:
  0.0 233.2 jit_solution(13555757295215974813)
XLA Ops:
  7.2 0.0 all-gather.3.cloned.1.call-start
  7.2 0.7 all-gather.3.cloned.1.call-update
  7.9 1.8 copy.26
  9.7 2.0 copy.27
  11.7 0.0 copy-start.2
  11.7 0.5 broadcast.33
  12.2 6.8 %reduce = bf16[512,1024]{1,0:T(8,128)(2,1)S(1)} reduce(bf16[512,1,1024]{2,1,0:T(2,128)(2,1)S(1)} %bitcast.62, bf16[]{:T(256)} %broadcast.33), dimensions={1}, to_apply=%bitcast.49.reduce_sub_computation | reduce | bytes 2097154
  19.0 1.6 reshape.69
  20.6 9.4 %all-to-all-start = ((bf16[16,2,16384]{2,1,0:T(2,128)(2,1)}), bf16[16,2,16384]{2,1,0:T(2,128)(2,1)S(1)}, u32[]{:S(2)}, u32[]{:S(2)}) async-start(bf16[16,2,16384]{2,1,0:T(2,128)(2,1)} %reshape.69), calls=%async_computation | async-start | bytes 2097152 | tf_op jit(solution)/shard_map/all_to_all | solution.py:17
  29.9 0.0 copy-done.2
  29.9 1.2 sort.17
  31.2 15.2 %all-to-all-done = bf16[16,2,16384]{2,1,0:T(2,128)(2,1)S(1)} async-done(((bf16[16,2,16384]{2,1,0:T(2,128)(2,1)}), bf16[16,2,16384]{2,1,0:T(2,128)(2,1)S(1)}, u32[]{:S(2)}, u32[]{:S(2)}) %all-to-all-start) | async-done | bytes 1048608 | tf_op jit(solution)/shard_map/all_to_all | solution.py:17
  46.4 1.0 reshape.70
  47.5 0.4 copy.36
  47.9 0.6 gather_fusion
  48.5 0.2 broadcast_select_fusion
  48.7 19.1 %all_to_all.66 = bf16[16,1024,32]{1,2,0:T(8,128)(2,1)S(1)} all-to-all(bf16[16,1024,32]{1,2,0:T(8,128)(2,1)S(1)} %broadcast_select_fusion), channel_id=1, replica_groups=mesh['section'=16,'shard'=32] {'section'}, dimensions={0} | all-to-all | bytes 2097152 | tf_op jit(solution)/shard_map/all_to_all | solution.py:19
  67.8 4.8 %copy.28 = bf16[1,1024,16,32]{3,2,1,0:T(8,128)(2,1)} copy(bf16[1,1024,16,32]{1,3,2,0:T(8,128)(2,1)S(1)} %bitcast.65) | data formatting | bytes 2097152 | tf_op jit(solution)/shard_map/all_to_all | solution.py:19
  72.5 0.0 copy-start.1
  72.5 0.0 copy-start.3
  72.5 6.0 %reshape_squeeze.3 = bf16[4,32,8,512]{3,2,1,0:T(8,128)(2,1)S(1)} reshape(bf16[1,1024,16,32]{3,2,1,0:T(8,128)(2,1)} %copy.28) | data formatting | bytes 2097152 | tf_op jit(solution)/shard_map/reshape;squeeze | solution.py:61
  78.5 1.1 copy.29
  79.6 13.8 %all-to-all-start.2 = ((bf16[32,4,8,512]{3,2,1,0:T(8,128)(2,1)}), bf16[32,4,8,512]{3,2,1,0:T(8,128)(2,1)S(1)}, u32[]{:S(2)}, u32[]{:S(2)}) async-start(bf16[32,4,8,512]{3,2,1,0:T(8,128)(2,1)} %copy.29), calls=%async_computation.2 | async-start | bytes 2097152 | tf_op jit(solution)/shard_map/all_to_all | solution.py:62
  93.4 0.0 copy-done.1
  93.4 0.0 copy-done.3
  93.5 0.1 dynamic_slice.3
  93.5 0.1 iota_compare_fusion
  93.6 61.1 %all-to-all-done.2 = bf16[32,4,8,512]{3,2,1,0:T(8,128)(2,1)S(1)} async-done(((bf16[32,4,8,512]{3,2,1,0:T(8,128)(2,1)}), bf16[32,4,8,512]{3,2,1,0:T(8,128)(2,1)S(1)}, u32[]{:S(2)}, u32[]{:S(2)}) %all-to-all-start.2) | async-done | bytes 1048608 | tf_op jit(solution)/shard_map/all_to_all | solution.py:62
  154.7 0.6 copy.44
  155.3 0.6 copy.40
  155.9 32.8 %all-gather.3.cloned.1.call-done = bf16[32,4,16384]{2,1,0:T(4,128)(2,1)} async-done(((bf16[1,4,16384]{2,1,0:T(4,128)(2,1)}), bf16[32,4,16384]{2,1,0:T(4,128)(2,1)}) %all-gather.3.cloned.1.call-update) | async-done | bytes 4194320 | tf_op jit(solution)/shard_map/all_gather | solution.py:65
  188.7 6.9 %reshape.66 = bf16[128,16384]{1,0:T(8,128)(2,1)} reshape(bf16[32,4,16384]{2,1,0:T(4,128)(2,1)} %all-gather.3.cloned.1.call-done) | data formatting | bytes 8388608
  195.6 0.0 copy-start
  195.6 3.8 %fusion.2 = bf16[128,32]{0,1:T(8,128)(2,1)S(1)} fusion(bf16[32,16384]{1,0:T(8,128)(2,1)S(1)} %bitcast.64, bf16[128,16384]{1,0:T(8,128)(2,1)} %reshape.66), kind=kOutput, calls=%fused_computation.6 | convolution fusion | flops 134221824 | bytes 5251072 | tf_op jit(solution)/shard_map/dot_general | solution.py:64
  199.4 0.1 reshape.54
  199.5 0.6 copy.31
  200.2 9.4 %all-to-all-start.3 = ((bf16[32,16,8]{1,2,0:T(8,128)(2,1)}), bf16[32,16,8]{1,2,0:T(8,128)(2,1)S(1)}, u32[]{:S(2)}, u32[]{:S(2)}) async-start(bf16[32,16,8]{1,2,0:T(8,128)(2,1)} %bitcast.13), calls=%async_computation.3 | async-start | bytes 131072 | tf_op jit(solution)/shard_map/all_to_all | solution.py:73
  209.6 0.0 copy-done
  209.6 0.5 fusion.13
  210.0 1.1 copy.38
  211.1 13.7 %all-to-all-done.3 = bf16[32,16,8]{1,2,0:T(8,128)(2,1)S(1)} async-done(((bf16[32,16,8]{1,2,0:T(8,128)(2,1)}), bf16[32,16,8]{1,2,0:T(8,128)(2,1)S(1)}, u32[]{:S(2)}, u32[]{:S(2)}) %all-to-all-start.3) | async-done | bytes 8224 | tf_op jit(solution)/shard_map/all_to_all | solution.py:73
  224.8 0.1 copy.34
  224.9 0.2 fusion.14
  225.0 0.1 copy.37
  225.1 0.2 fusion.5
  225.4 0.3 fusion.1
  225.7 0.7 copy.45
  (9 shorter events, 0.1 us)
Async XLA Ops:
  7.2 181.6 %all-gather.3.cloned.1.call-start = ((), (), s32[]{:S(2)}) async-start(), calls=%async_computation.4 | async-start | bytes 4325376 | tf_op jit(solution)/shard_map/all_gather | solution.py:65
  11.7 18.3 %copy-start.2 = (s32[16]{0:T(128)S(1)}, s32[16]{0:T(128)}, u32[]{:S(2)}) copy-start(s32[16]{0:T(128)} %param.7) | copy-start | bytes 196
  20.6 25.9 %all-to-all-start = ((bf16[16,2,16384]{2,1,0:T(2,128)(2,1)}), bf16[16,2,16384]{2,1,0:T(2,128)(2,1)S(1)}, u32[]{:S(2)}, u32[]{:S(2)}) async-start(bf16[16,2,16384]{2,1,0:T(2,128)(2,1)} %reshape.69), calls=%async_computation | async-start | bytes 2097152 | tf_op jit(solution)/shard_map/all_to_all | solution.py:17
  72.5 20.9 %copy-start.1 = (bf16[16,2048]{1,0:T(8,128)(2,1)S(1)}, bf16[16,2048]{1,0:T(8,128)(2,1)}, u32[]{:S(2)}) copy-start(bf16[16,2048]{1,0:T(8,128)(2,1)} %param.9) | copy-start | bytes 196612
  72.5 20.9 %copy-start.3 = (s32[128]{0:T(128)S(1)}, s32[128]{0:T(128)}, u32[]{:S(2)}) copy-start(s32[128]{0:T(128)} %param.11) | copy-start | bytes 1540
  79.6 75.1 %all-to-all-start.2 = ((bf16[32,4,8,512]{3,2,1,0:T(8,128)(2,1)}), bf16[32,4,8,512]{3,2,1,0:T(8,128)(2,1)S(1)}, u32[]{:S(2)}, u32[]{:S(2)}) async-start(bf16[32,4,8,512]{3,2,1,0:T(8,128)(2,1)} %copy.29), calls=%async_computation.2 | async-start | bytes 2097152 | tf_op jit(solution)/shard_map/all_to_all | solution.py:62
  195.6 13.9 %copy-start = (bf16[16,128,256]{2,1,0:T(8,128)(2,1)S(1)}, bf16[16,128,256]{2,1,0:T(8,128)(2,1)}, u32[]{:S(2)}) copy-start(bf16[16,128,256]{2,1,0:T(8,128)(2,1)} %param.10) | copy-start | bytes 3145732
  200.2 24.6 %all-to-all-start.3 = ((bf16[32,16,8]{1,2,0:T(8,128)(2,1)}), bf16[32,16,8]{1,2,0:T(8,128)(2,1)S(1)}, u32[]{:S(2)}, u32[]{:S(2)}) async-start(bf16[32,16,8]{1,2,0:T(8,128)(2,1)} %bitcast.13), calls=%async_computation.3 | async-start | bytes 131072 | tf_op jit(solution)/shard_map/all_to_all | solution.py:73
Sparse Core Ops, SparseCore 0:
  11.1 177.6 all-gather.2
where the time goes:
time: 234 us; the launch traced here: 233 us
  waiting for transfers between devices  124 us (53%)
  starting transfers between devices  32.6 us (14%)
  local copies, waits for them, and re-layouts  30.5 us (13%)
  blocking collectives  19.1 us (8%)
  between operations  14.2 us (6%)
  other arithmetic  8.54 us (4%)
  matrix products  4.7 us (2%)
    all_to_all x1, waiting for transfers between devices, body(): lax.all_to_all(pieces, 'shard', split_axis=0, concat_axis=3, tiled=True)  61.1 us
    all_gather x1, waiting for transfers between devices, body(): lax.all_gather(hidden, 'shard', axis=0, tiled=True)  32.8 us
    all_to_all x1, blocking collectives, route(): lax.all_to_all(picked, 'section', split_axis=0, concat_axis=2, tiled=True)  19.1 us
    all_to_all x1, waiting for transfers between devices, route(): lax.all_to_all(blocks, 'section', split_axis=2, concat_axis=0, tiled=True)  15.2 us
    all_to_all x1, starting transfers between devices, body(): lax.all_to_all(pieces, 'shard', split_axis=0, concat_axis=3, tiled=True)  13.8 us
    all_to_all x1, waiting for transfers between devices, body(): lax.all_to_all(arranged, 'shard', split_axis=0, concat_axis=2, tiled=True)  13.7 us
    unnamed x18, local copies, waits for them, and re-layouts  13.5 us
    all_to_all x1, starting transfers between devices, body(): lax.all_to_all(arranged, 'shard', split_axis=0, concat_axis=2, tiled=True)  9.39 us
  transfers between devices with their start and end apart: 4, of which 4 were waited for; matrix products, arithmetic and copies ran while one was open for 13% of the time, Pallas kernels for 0%

commit v1 on v0

--- a/solution.py
+++ b/solution.py
@@ -13,10 +13,8 @@
 ROWS = 128
 
 
-def route(blocks, source):
-    spread = lax.all_to_all(blocks, "section", split_axis=2, concat_axis=0, tiled=True)
-    picked = jnp.take(spread, source, axis=0)
-    return lax.all_to_all(picked, "section", split_axis=0, concat_axis=2, tiled=True)
+def exchange(blocks, axis):
+    return lax.all_to_all(blocks, axis, split_axis=0, concat_axis=0, tiled=True)
 
 
 def attend(query_rows, cache_rows, fresh_rows, row_lengths):
@@ -51,32 +49,39 @@
 
 def body(train_weights, section_to_group, hidden, queries, kv_cache, lengths):
     shards = lax.axis_size("shard")
+    sections = lax.axis_size("section")
     per_head = shards // KVH
     row_block = ROWS // per_head
     piece_cols = 2 * HD // shards
-    source = jnp.argsort(section_to_group)
+    slice_rows = train_weights.shape[1]
+    groups = jnp.arange(sections, dtype=jnp.int32)
+    source = jnp.sum(
+        jnp.where(section_to_group[None, :] == groups[:, None], groups[None, :], 0), axis=1
+    )
+    own = hidden.shape[0]
+    inputs = exchange(hidden.reshape(own, shards, slice_rows).transpose(1, 0, 2), "shard")
+    inputs = inputs.reshape(ROWS, slice_rows)
     flipped = train_weights[0].astype(jnp.bfloat16).T
-    slice_rows = flipped.shape[1]
-    routed = route(flipped[None], source)[0]
-    pieces = routed.reshape(KVH, shards, piece_cols, slice_rows).transpose(1, 0, 2, 3)
-    column_block = lax.all_to_all(pieces, "shard", split_axis=0, concat_axis=3, tiled=True)
-    column_block = column_block.reshape(KVH * piece_cols, D)
-    product = lax.dot_general(
-        lax.all_gather(hidden, "shard", axis=0, tiled=True),
-        column_block,
-        (((1,), (1,)), ((), ())),
+    flipped = flipped.reshape(KVH, shards, piece_cols, slice_rows).transpose(1, 0, 2, 3)
+    flipped = flipped.reshape(sections, -1, slice_rows)
+    spread = exchange(flipped, "section")
+    picked = spread.at[source].get(mode="promise_in_bounds")
+    routed = exchange(picked, "section").reshape(shards, KVH, piece_cols, slice_rows)
+    partial = lax.dot_general(
+        inputs,
+        routed.transpose(1, 0, 2, 3).reshape(KVH, 2 * HD, slice_rows),
+        (((1,), (2,)), ((), ())),
         preferred_element_type=jnp.float32,
     )
-    fresh_cols = product.astype(jnp.bfloat16)
-    arranged = fresh_cols.reshape(per_head, row_block, KVH, piece_cols).transpose(2, 0, 1, 3)
-    arranged = arranged.reshape(shards, row_block, piece_cols)
-    fresh = lax.all_to_all(arranged, "shard", split_axis=0, concat_axis=2, tiled=True)[0]
-    position = lax.axis_index("shard")
-    block_index = position % per_head
+    partial = partial.reshape(per_head, row_block, KVH, 2 * HD).transpose(2, 0, 1, 3)
+    partial = exchange(partial.reshape(shards, row_block, 2 * HD), "shard")
+    fresh = jnp.sum(partial, axis=0).astype(jnp.bfloat16)
+    pieces = exchange(routed, "shard")
+    layer_out = pieces.transpose(1, 2, 0, 3).reshape(1, KVH, piece_cols, D)
+    block_index = lax.axis_index("shard") % per_head
     row_lengths = lax.dynamic_slice_in_dim(lengths, block_index * row_block, row_block, 0)
     query_rows = queries.reshape(row_block, QPK, HD)
     context = attend(query_rows, kv_cache, fresh, row_lengths)
-    layer_out = column_block.reshape(1, KVH, piece_cols, D)
     return (context, layer_out)
 
 

time: 234 us -> 179 us (0.76)
  the two profiles are of different devices: /device:TPU:2 before, /device:TPU:36 now
where the time goes in v1:
time: 179 us; the launch traced here: 178 us
  waiting for transfers between devices  80.9 us (45%)
  blocking collectives  58.9 us (33%)
  starting transfers between devices  28.2 us (16%)
  local copies, waits for them, and re-layouts  6.17 us (3%)
  matrix products  2.7 us (2%)
    all_to_all x3, waiting for transfers between devices, exchange(): return lax.all_to_all(blocks, axis, split_axis=0, concat_axis=0, tiled=True)  80.9 us
    all_to_all x2, blocking collectives, exchange(): return lax.all_to_all(blocks, axis, split_axis=0, concat_axis=0, tiled=True)  58.9 us
    all_to_all x3, starting transfers between devices, exchange(): return lax.all_to_all(blocks, axis, split_axis=0, concat_axis=0, tiled=True)  28.2 us
  transfers between devices with their start and end apart: 3, of which 3 were waited for; matrix products, arithmetic and copies ran while one was open for 2% of the time, Pallas kernels for 0%

profile of v1, /device:TPU:36, one launch (start us, length us, event | category | flops | bytes accessed | tf_op | source)
XLA Modules:
  0.0 178.1 jit_solution(15405398352190134446)
XLA Ops:
  0.6 1.8 copy.18
  2.4 0.0 copy-start.2
  2.4 0.1 copy.19
  2.6 21.5 %all_to_all.25 = bf16[16,64,512]{2,1,0:T(8,128)(2,1)S(1)} all-to-all(bf16[16,64,512]{2,1,0:T(8,128)(2,1)S(1)} %bitcast.46), channel_id=1, replica_groups=mesh['section'=16,'shard'=32] {'section'}, dimensions={0} | all-to-all | bytes 2097152 | tf_op jit(solution)/shard_map/all_to_all | solution.py:17
  24.0 17.8 %all-to-all-start.2 = ((bf16[32,4,512]{2,1,0:T(4,128)(2,1)}), bf16[32,4,512]{2,1,0:T(4,128)(2,1)S(1)}, u32[]{:S(2)}, u32[]{:S(2)}) async-start(bf16[32,4,512]{2,1,0:T(4,128)(2,1)} %bitcast.11), calls=%async_computation.2 | async-start | bytes 262144 | tf_op jit(solution)/shard_map/all_to_all | solution.py:17
  41.8 0.0 copy-done.2
  41.8 0.1 select_reduce_fusion
  41.9 1.6 gather_fusion
  43.5 12.5 %all-to-all-done.2 = bf16[32,4,512]{2,1,0:T(4,128)(2,1)S(1)} async-done(((bf16[32,4,512]{2,1,0:T(4,128)(2,1)}), bf16[32,4,512]{2,1,0:T(4,128)(2,1)S(1)}, u32[]{:S(2)}, u32[]{:S(2)}) %all-to-all-start.2) | async-done | bytes 131104 | tf_op jit(solution)/shard_map/all_to_all | solution.py:17
  56.0 4.3 %all-to-all-start.1 = ((bf16[16,64,512]{2,1,0:T(8,128)(2,1)}), bf16[16,64,512]{2,1,0:T(8,128)(2,1)}, u32[]{:S(2)}, u32[]{:S(2)}) async-start(bf16[16,64,512]{2,1,0:T(8,128)(2,1)} %gather_fusion), calls=%async_computation.1 | async-start | bytes 2097152 | tf_op jit(solution)/shard_map/all_to_all | solution.py:17
  60.4 16.5 %all-to-all-done.1 = bf16[16,64,512]{2,1,0:T(8,128)(2,1)} async-done(((bf16[16,64,512]{2,1,0:T(8,128)(2,1)}), bf16[16,64,512]{2,1,0:T(8,128)(2,1)}, u32[]{:S(2)}, u32[]{:S(2)}) %all-to-all-start.1) | async-done | bytes 1048608 | tf_op jit(solution)/shard_map/all_to_all | solution.py:17
  76.9 0.0 copy-start.1
  76.9 0.0 copy-start.3
  76.9 0.0 copy-start
  76.9 1.8 %fusion.2 = f32[4,256,128]{1,2,0:T(8,128)S(1)} fusion(bf16[128,512,1]{1,0,2:T(8,128)(2,1)S(1)} %reshape.94, bf16[4,32,8,512]{3,2,0,1:T(8,128)(2,1)} %bitcast.8), kind=kOutput, calls=%fused_computation.5 | convolution fusion | flops 134217728 | bytes 1703936 | tf_op jit(solution)/shard_map/dot_general | solution.py:70
  78.7 37.5 %all_to_all.26 = f32[32,16,256]{2,1,0:T(8,128)S(1)} all-to-all(f32[32,16,256]{2,1,0:T(8,128)S(1)} %bitcast.47), channel_id=1, replica_groups=mesh['section'=16,'shard'=32] {'shard'}, dimensions={0} | all-to-all | bytes 1048576 | tf_op jit(solution)/shard_map/all_to_all | solution.py:17
  116.2 6.1 %all-to-all-start.4 = ((bf16[32,4,8,512]{3,2,1,0:T(8,128)(2,1)}), bf16[32,4,8,512]{3,2,1,0:T(8,128)(2,1)S(1)}, u32[]{:S(2)}, u32[]{:S(2)}) async-start(bf16[32,4,8,512]{3,2,1,0:T(8,128)(2,1)} %bitcast.7), calls=%async_computation.4 | async-start | bytes 2097152 | tf_op jit(solution)/shard_map/all_to_all | solution.py:17
  122.3 0.0 copy-done.1
  122.3 0.0 copy-done.3
  122.4 0.1 dynamic_slice.3
  122.4 0.1 iota_compare_fusion.1
  122.5 0.0 copy-done
  122.5 0.5 fusion.18
  123.0 0.1 reduce_sum.31
  123.0 0.1 fusion.12
  123.2 0.2 fusion.7
  123.4 0.3 fusion.1
  123.7 0.7 copy.34
  124.4 51.8 %all-to-all-done.4 = bf16[32,4,8,512]{3,2,1,0:T(8,128)(2,1)S(1)} async-done(((bf16[32,4,8,512]{3,2,1,0:T(8,128)(2,1)}), bf16[32,4,8,512]{3,2,1,0:T(8,128)(2,1)S(1)}, u32[]{:S(2)}, u32[]{:S(2)}) %all-to-all-start.4) | async-done | bytes 1048608 | tf_op jit(solution)/shard_map/all_to_all | solution.py:17
  176.2 0.6 copy.22
  176.8 1.3 reshape.85
  (7 shorter events, 0.1 us)
Async XLA Ops:
  2.4 39.4 %copy-start.2 = (s32[16]{0:T(128)S(1)}, s32[16]{0:T(128)}, u32[]{:S(2)}) copy-start(s32[16]{0:T(128)} %param.7) | copy-start | bytes 196
  24.0 32.0 %all-to-all-start.2 = ((bf16[32,4,512]{2,1,0:T(4,128)(2,1)}), bf16[32,4,512]{2,1,0:T(4,128)(2,1)S(1)}, u32[]{:S(2)}, u32[]{:S(2)}) async-start(bf16[32,4,512]{2,1,0:T(4,128)(2,1)} %bitcast.11), calls=%async_computation.2 | async-start | bytes 262144 | tf_op jit(solution)/shard_map/all_to_all | solution.py:17
  56.0 20.9 %all-to-all-start.1 = ((bf16[16,64,512]{2,1,0:T(8,128)(2,1)}), bf16[16,64,512]{2,1,0:T(8,128)(2,1)}, u32[]{:S(2)}, u32[]{:S(2)}) async-start(bf16[16,64,512]{2,1,0:T(8,128)(2,1)} %gather_fusion), calls=%async_computation.1 | async-start | bytes 2097152 | tf_op jit(solution)/shard_map/all_to_all | solution.py:17
  76.9 45.4 %copy-start.1 = (bf16[16,2048]{1,0:T(8,128)(2,1)S(1)}, bf16[16,2048]{1,0:T(8,128)(2,1)}, u32[]{:S(2)}) copy-start(bf16[16,2048]{1,0:T(8,128)(2,1)} %param.9) | copy-start | bytes 196612
  76.9 45.4 %copy-start.3 = (s32[128]{0:T(128)S(1)}, s32[128]{0:T(128)}, u32[]{:S(2)}) copy-start(s32[128]{0:T(128)} %param.11) | copy-start | bytes 1540
  76.9 45.6 %copy-start = (bf16[16,128,256]{2,1,0:T(8,128)(2,1)S(1)}, bf16[16,128,256]{2,1,0:T(8,128)(2,1)}, u32[]{:S(2)}) copy-start(bf16[16,128,256]{2,1,0:T(8,128)(2,1)} %param.10) | copy-start | bytes 3145732
  116.2 60.0 %all-to-all-start.4 = ((bf16[32,4,8,512]{3,2,1,0:T(8,128)(2,1)}), bf16[32,4,8,512]{3,2,1,0:T(8,128)(2,1)S(1)}, u32[]{:S(2)}, u32[]{:S(2)}) async-start(bf16[32,4,8,512]{3,2,1,0:T(8,128)(2,1)} %bitcast.7), calls=%async_computation.4 | async-start | bytes 2097152 | tf_op jit(solution)/shard_map/all_to_all | solution.py:17

commit v2 on v1

--- a/solution.py
+++ b/solution.py
@@ -3,6 +3,8 @@
 import jax
 import jax.numpy as jnp
 from jax import lax
+from jax.experimental import pallas as pl
+from jax.experimental.pallas import tpu as pltpu
 from jax.sharding import PartitionSpec as P
 
 D = 16384
@@ -47,6 +49,49 @@
     return context.reshape(context.shape[0], QPK * HD).astype(jnp.bfloat16)
 
 
+def pack_kernel(inputs_ref, routed_ref, out_ref):
+    head = pl.program_id(0)
+    shards, _, piece, depth = routed_ref.shape
+    half = piece
+    per_head = shards // KVH
+    block = routed_ref[:, 0]
+    out_ref[:, :, pl.ds(pl.multiple_of(head * depth, depth), depth)] = block
+    product = lax.dot_general(
+        inputs_ref[...],
+        block.reshape(2 * HD, depth),
+        (((1,), (1,)), ((), ())),
+        preferred_element_type=jnp.float32,
+    )
+    upper = product.astype(jnp.bfloat16)
+    lower = (product[:, :HD] - upper[:, :HD].astype(jnp.float32)).astype(jnp.bfloat16)
+    base = KVH * depth
+    for i in range(per_head):
+        for j in range(2):
+            rows = slice((2 * i + j) * half, (2 * i + j + 1) * half)
+            start = base + j * 2 * HD
+            out_ref[pl.ds(head * per_head + i, 1), :, start : start + 2 * HD] = upper[rows][None]
+            start = base + 4 * HD + j * HD
+            out_ref[pl.ds(head * per_head + i, 1), :, start : start + HD] = lower[rows][None]
+
+
+def pack(inputs, routed):
+    shards, _, piece, depth = routed.shape
+    width = KVH * depth + 6 * HD
+    return pl.pallas_call(
+        pack_kernel,
+        grid=(KVH,),
+        in_specs=[
+            pl.BlockSpec((ROWS, depth), lambda h: (0, 0)),
+            pl.BlockSpec((shards, 1, piece, depth), lambda h: (0, h, 0, 0)),
+        ],
+        out_specs=pl.BlockSpec((shards, piece, width), lambda h: (0, 0, 0)),
+        out_shape=jax.ShapeDtypeStruct((shards, piece, width), jnp.bfloat16),
+        cost_estimate=pl.CostEstimate(
+            flops=2 * ROWS * KVH * 2 * HD * depth, bytes_accessed=3_000_000, transcendentals=0
+        ),
+    )(inputs, routed)
+
+
 def body(train_weights, section_to_group, hidden, queries, kv_cache, lengths):
     shards = lax.axis_size("shard")
     sections = lax.axis_size("section")
@@ -67,17 +112,14 @@
     spread = exchange(flipped, "section")
     picked = spread.at[source].get(mode="promise_in_bounds")
     routed = exchange(picked, "section").reshape(shards, KVH, piece_cols, slice_rows)
-    partial = lax.dot_general(
-        inputs,
-        routed.transpose(1, 0, 2, 3).reshape(KVH, 2 * HD, slice_rows),
-        (((1,), (2,)), ((), ())),
-        preferred_element_type=jnp.float32,
-    )
-    partial = partial.reshape(per_head, row_block, KVH, 2 * HD).transpose(2, 0, 1, 3)
-    partial = exchange(partial.reshape(shards, row_block, 2 * HD), "shard")
-    fresh = jnp.sum(partial, axis=0).astype(jnp.bfloat16)
-    pieces = exchange(routed, "shard")
-    layer_out = pieces.transpose(1, 2, 0, 3).reshape(1, KVH, piece_cols, D)
+    received = exchange(pack(inputs, routed), "shard")
+    base = KVH * slice_rows
+    layer_out = received[:, :, :base].reshape(shards, piece_cols, KVH, slice_rows)
+    layer_out = layer_out.transpose(2, 1, 0, 3).reshape(1, KVH, piece_cols, D)
+    sums = jnp.sum(received[:, :, base:].astype(jnp.float32), axis=0)
+    upper = jnp.concatenate([sums[:, : 2 * HD], sums[:, 2 * HD : 4 * HD]], axis=0)
+    lower = jnp.concatenate([sums[:, 4 * HD : 5 * HD], sums[:, 5 * HD :]], axis=0)
+    fresh = jnp.concatenate([upper[:, :HD] + lower, upper[:, HD:]], axis=1).astype(jnp.bfloat16)
     block_index = lax.axis_index("shard") % per_head
     row_lengths = lax.dynamic_slice_in_dim(lengths, block_index * row_block, row_block, 0)
     query_rows = queries.reshape(row_block, QPK, HD)

time: 179 us -> 163 us (0.911)
  the two profiles are of different devices: /device:TPU:36 before, /device:TPU:4 now
where the time goes in v2:
time: 163 us
  waiting for transfers between devices  101 us (62%)
  starting transfers between devices  27.2 us (17%)
  blocking collectives  21.5 us (13%)
  local copies, waits for them, and re-layouts  7.09 us (4%)
  Pallas kernels  3.8 us (2%)
    all_to_all x3, waiting for transfers between devices, exchange(): return lax.all_to_all(blocks, axis, split_axis=0, concat_axis=0, tiled=True)  101 us
    all_to_all x3, starting transfers between devices, exchange(): return lax.all_to_all(blocks, axis, split_axis=0, concat_axis=0, tiled=True)  27.2 us
    all_to_all x1, blocking collectives, exchange(): return lax.all_to_all(blocks, axis, split_axis=0, concat_axis=0, tiled=True)  21.5 us
    pallas_call x1, Pallas kernels, pack(): pl.pallas_call(pack_kernel, grid=(KVH,), in_specs=[pl.BlockSpec((ROWS, de...  3.8 us
    unnamed x13, local copies, waits for them, and re-layouts  3.43 us
  transfers between devices with their start and end apart: 3, of which 3 were waited for; matrix products, arithmetic and copies ran while one was open for 2% of the time, Pallas kernels for 0%

profile of v2, /device:TPU:4, one launch (start us, length us, event | category | flops | bytes accessed | tf_op | source)
XLA Modules:
  0.0 162.8 jit_solution(960464285605963305)
XLA Ops:
  0.6 1.8 %copy.15 = bf16[1,512,1024]{1,2,0:T(8,128)(2,1)S(1)} copy(f32[1,512,1024]{2,1,0:T(8,128)} %param.6) | data formatting | bytes 3145728 | tf_op args[0]
  2.4 0.1 copy.16
  2.5 0.0 copy-start.3
  2.6 21.5 %all_to_all.20 = bf16[16,64,512]{2,1,0:T(8,128)(2,1)S(1)} all-to-all(bf16[16,64,512]{2,1,0:T(8,128)(2,1)S(1)} %bitcast.34), channel_id=1, replica_groups=mesh['section'=16,'shard'=32] {'section'}, dimensions={0} | all-to-all | bytes 2097152 | tf_op jit(solution)/shard_map/all_to_all | solution.py:19
  24.0 18.2 %all-to-all-start = ((bf16[32,4,512]{2,1,0:T(4,128)(2,1)}), bf16[32,4,512]{2,1,0:T(4,128)(2,1)S(1)}, u32[]{:S(2)}, u32[]{:S(2)}) async-start(bf16[32,4,512]{2,1,0:T(4,128)(2,1)} %bitcast.1), calls=%async_computation | async-start | bytes 262144 | tf_op jit(solution)/shard_map/all_to_all | solution.py:19
  42.2 0.0 copy-done.3
  42.2 0.1 select_reduce_fusion
  42.4 1.6 gather_fusion
  44.0 13.7 %all-to-all-done = bf16[32,4,512]{2,1,0:T(4,128)(2,1)S(1)} async-done(((bf16[32,4,512]{2,1,0:T(4,128)(2,1)}), bf16[32,4,512]{2,1,0:T(4,128)(2,1)S(1)}, u32[]{:S(2)}, u32[]{:S(2)}) %all-to-all-start) | async-done | bytes 131104 | tf_op jit(solution)/shard_map/all_to_all | solution.py:19
  57.6 3.7 %all-to-all-start.2 = ((bf16[16,64,512]{2,1,0:T(8,128)(2,1)}), bf16[16,64,512]{2,1,0:T(8,128)(2,1)S(1)}, u32[]{:S(2)}, u32[]{:S(2)}) async-start(bf16[16,64,512]{2,1,0:T(8,128)(2,1)} %gather_fusion), calls=%async_computation.2 | async-start | bytes 2097152 | tf_op jit(solution)/shard_map/all_to_all | solution.py:19
  61.3 0.7 reshape.72.inputs_ref
  62.0 15.8 %all-to-all-done.2 = bf16[16,64,512]{2,1,0:T(8,128)(2,1)S(1)} async-done(((bf16[16,64,512]{2,1,0:T(8,128)(2,1)}), bf16[16,64,512]{2,1,0:T(8,128)(2,1)S(1)}, u32[]{:S(2)}, u32[]{:S(2)}) %all-to-all-start.2) | async-done | bytes 1048608 | tf_op jit(solution)/shard_map/all_to_all | solution.py:19
  77.8 0.0 copy-start
  77.8 1.0 copy-done
  78.8 3.8 %shard_map.77 = bf16[32,8,2816]{2,1,0:T(8,128)(2,1)} custom-call(bf16[128,512]{1,0:T(8,128)(2,1)} %reshape.72.inputs_ref, bf16[32,4,8,512]{3,2,1,0:T(8,128)(2,1)} %bitcast.33), custom_call_target="tpu_custom_call" | custom-call | flops 134217728 | bytes 3000000 | tf_op jit(solution)/shard_map/pallas_call | solution.py:80
  82.6 0.0 copy-start.2
  82.6 0.0 copy-start.4
  82.6 0.0 copy-start.1
  82.6 5.3 %all-to-all-start.3 = ((bf16[32,8,2816]{2,1,0:T(8,128)(2,1)}), bf16[32,8,2816]{2,1,0:T(8,128)(2,1)S(1)}, u32[]{:S(2)}, u32[]{:S(2)}) async-start(bf16[32,8,2816]{2,1,0:T(8,128)(2,1)} %shard_map.77), calls=%async_computation.3 | async-start | bytes 2883584 | tf_op jit(solution)/shard_map/all_to_all | solution.py:19
  87.9 0.0 copy-done.2
  87.9 0.0 copy-done.4
  87.9 0.1 dynamic_slice.3
  88.0 0.1 iota_compare_fusion.1
  88.1 0.0 copy-done.1
  88.1 0.5 fusion.23
  88.6 71.6 %all-to-all-done.3 = bf16[32,8,2816]{2,1,0:T(8,128)(2,1)S(1)} async-done(((bf16[32,8,2816]{2,1,0:T(8,128)(2,1)}), bf16[32,8,2816]{2,1,0:T(8,128)(2,1)S(1)}, u32[]{:S(2)}, u32[]{:S(2)}) %all-to-all-start.3) | async-done | bytes 1441824 | tf_op jit(solution)/shard_map/all_to_all | solution.py:19
  160.2 0.1 convert_reduce_fusion
  160.2 0.1 slice.55
  160.4 1.1 copy.17
  161.4 0.1 fusion.13
  161.6 0.2 fusion.4
  161.8 0.3 fusion.1
  162.1 0.7 copy.25
  (9 shorter events, 0.1 us)
Async XLA Ops:
  2.5 39.7 %copy-start.3 = (s32[16]{0:T(128)S(1)}, s32[16]{0:T(128)}, u32[]{:S(2)}) copy-start(s32[16]{0:T(128)} %param.7) | copy-start | bytes 196
  24.0 33.6 %all-to-all-start = ((bf16[32,4,512]{2,1,0:T(4,128)(2,1)}), bf16[32,4,512]{2,1,0:T(4,128)(2,1)S(1)}, u32[]{:S(2)}, u32[]{:S(2)}) async-start(bf16[32,4,512]{2,1,0:T(4,128)(2,1)} %bitcast.1), calls=%async_computation | async-start | bytes 262144 | tf_op jit(solution)/shard_map/all_to_all | solution.py:19
  57.6 20.2 %all-to-all-start.2 = ((bf16[16,64,512]{2,1,0:T(8,128)(2,1)}), bf16[16,64,512]{2,1,0:T(8,128)(2,1)S(1)}, u32[]{:S(2)}, u32[]{:S(2)}) async-start(bf16[16,64,512]{2,1,0:T(8,128)(2,1)} %gather_fusion), calls=%async_computation.2 | async-start | bytes 2097152 | tf_op jit(solution)/shard_map/all_to_all | solution.py:19
  77.8 1.0 copy-start
  82.6 5.3 %copy-start.2 = (bf16[16,2048]{1,0:T(8,128)(2,1)S(1)}, bf16[16,2048]{1,0:T(8,128)(2,1)}, u32[]{:S(2)}) copy-start(bf16[16,2048]{1,0:T(8,128)(2,1)} %param.9) | copy-start | bytes 196612
  82.6 5.4 %copy-start.4 = (s32[128]{0:T(128)S(1)}, s32[128]{0:T(128)}, u32[]{:S(2)}) copy-start(s32[128]{0:T(128)} %param.11) | copy-start | bytes 1540
  82.6 5.5 %copy-start.1 = (bf16[16,128,256]{2,1,0:T(8,128)(2,1)S(1)}, bf16[16,128,256]{2,1,0:T(8,128)(2,1)}, u32[]{:S(2)}) copy-start(bf16[16,128,256]{2,1,0:T(8,128)(2,1)} %param.10) | copy-start | bytes 3145732
  82.6 77.6 %all-to-all-start.3 = ((bf16[32,8,2816]{2,1,0:T(8,128)(2,1)}), bf16[32,8,2816]{2,1,0:T(8,128)(2,1)S(1)}, u32[]{:S(2)}, u32[]{:S(2)}) async-start(bf16[32,8,2816]{2,1,0:T(8,128)(2,1)} %shard_map.77), calls=%async_computation.3 | async-start | bytes 2883584 | tf_op jit(solution)/shard_map/all_to_all | solution.py:19

commit v3 on v2

--- a/solution.py
+++ b/solution.py
@@ -4,8 +4,8 @@
 import jax.numpy as jnp
 from jax import lax
 from jax.experimental import pallas as pl
-from jax.experimental.pallas import tpu as pltpu
 from jax.sharding import PartitionSpec as P
+
 
 D = 16384
 HD = 128
@@ -17,6 +17,26 @@
 
 def exchange(blocks, axis):
     return lax.all_to_all(blocks, axis, split_axis=0, concat_axis=0, tiled=True)
+
+
+def spread_rows(blocks):
+    me = lax.axis_index("shard")
+    shards = blocks.shape[0]
+
+    def send(values, bits):
+        return lax.ppermute(values, "shard", [(i, i ^ bits) for i in range(shards)])
+
+    order = jnp.arange(shards, dtype=jnp.int32).reshape(4, 4, 2).transpose(2, 1, 0).reshape(-1)
+    start = blocks.at[me ^ order].get(mode="promise_in_bounds")
+    start = start.reshape((2, 4, 4) + blocks.shape[1:])
+    side = [start[0], send(start[1], 1)]
+    near = [jnp.stack([v[k] for v in side]) for k in range(4)]
+    near = [near[0]] + [send(near[k], k << 1) for k in range(1, 4)]
+    far = [jnp.stack([v[:, k] for v in near]) for k in range(4)]
+    far = [far[0]] + [send(far[k], k << 3) for k in range(1, 4)]
+    merged = jnp.concatenate(far).reshape((shards,) + blocks.shape[1:])
+    relative = me ^ jnp.arange(shards, dtype=jnp.int32)
+    return merged.at[relative].get(mode="promise_in_bounds")
 
 
 def attend(query_rows, cache_rows, fresh_rows, row_lengths):
@@ -92,7 +112,7 @@
     )(inputs, routed)
 
 
-def body(train_weights, section_to_group, hidden, queries, kv_cache, lengths):
+def step(train_weights, section_to_group, hidden, queries, kv_cache, lengths):
     shards = lax.axis_size("shard")
     sections = lax.axis_size("section")
     per_head = shards // KVH
@@ -104,7 +124,7 @@
         jnp.where(section_to_group[None, :] == groups[:, None], groups[None, :], 0), axis=1
     )
     own = hidden.shape[0]
-    inputs = exchange(hidden.reshape(own, shards, slice_rows).transpose(1, 0, 2), "shard")
+    inputs = spread_rows(hidden.reshape(own, shards, slice_rows).transpose(1, 0, 2))
     inputs = inputs.reshape(ROWS, slice_rows)
     flipped = train_weights[0].astype(jnp.bfloat16).T
     flipped = flipped.reshape(KVH, shards, piece_cols, slice_rows).transpose(1, 0, 2, 3)
@@ -129,7 +149,7 @@
 
 def solution(mesh):
     return jax.shard_map(
-        body,
+        step,
         mesh=mesh,
         in_specs=(
             P("section", "shard", None),

time: 163 us -> 166 us (1.018)
  starting transfers between devices: 27.2 us -> 60 us
  blocking collectives: 21.5 us -> 0 us
  waiting for transfers between devices: 101 us -> 88.6 us
  local copies, waits for them, and re-layouts: 7.09 us -> 10.5 us
    ppermute x0 -> x7, starting transfers between devices: none -> 37.1 us  [send(): return lax.ppermute(values, 'shard', [(i, i ^ bits) for i in range(shards)])]
    all_to_all x1 -> x0, blocking collectives: 21.5 us -> none  [exchange(): return lax.all_to_all(blocks, axis, split_axis=0, concat_axis=0, tiled=True)]
    all_to_all x3, waiting for transfers between devices: 101 us -> 84.7 us  [exchange(): return lax.all_to_all(blocks, axis, split_axis=0, concat_axis=0, tiled=True)]
    all_to_all x3, starting transfers between devices: 27.2 us -> 22.9 us  [exchange(): return lax.all_to_all(blocks, axis, split_axis=0, concat_axis=0, tiled=True)]
    ppermute x0 -> x7, waiting for transfers between devices: none -> 3.91 us  [send(): return lax.ppermute(values, 'shard', [(i, i ^ bits) for i in range(shards)])]
    unnamed x13 -> x20, local copies, waits for them, and re-layouts: 3.43 us -> 4.29 us
  transfers between devices with their start and end apart: 3 -> 10, of which waited for: 3 -> 4; matrix products, arithmetic and copies ran while one was open for 2% -> 4% of each run, Pallas kernels for 0% -> 0%
where the time goes in v3:
time: 166 us
  waiting for transfers between devices  88.6 us (53%)
  starting transfers between devices  60 us (36%)
  local copies, waits for them, and re-layouts  10.5 us (6%)
  Pallas kernels  3.77 us (2%)
    all_to_all x3, waiting for transfers between devices, exchange(): return lax.all_to_all(blocks, axis, split_axis=0, concat_axis=0, tiled=True)  84.7 us
    ppermute x7, starting transfers between devices, send(): return lax.ppermute(values, 'shard', [(i, i ^ bits) for i in range(shards)])  37.1 us
    all_to_all x3, starting transfers between devices, exchange(): return lax.all_to_all(blocks, axis, split_axis=0, concat_axis=0, tiled=True)  22.9 us
    unnamed x20, local copies, waits for them, and re-layouts  4.29 us
    ppermute x7, waiting for transfers between devices, send(): return lax.ppermute(values, 'shard', [(i, i ^ bits) for i in range(shards)])  3.91 us
    pallas_call x1, Pallas kernels, pack(): pl.pallas_call(pack_kernel, grid=(KVH,), in_specs=[pl.BlockSpec((ROWS, de...  3.77 us
  transfers between devices with their start and end apart: 10, of which 4 were waited for; matrix products, arithmetic and copies ran while one was open for 4% of the time, Pallas kernels for 0%

profile of v3, /device:TPU:4, one launch (start us, length us, event | category | flops | bytes accessed | tf_op | source)
XLA Modules:
  0.0 165.6 jit_solution(3276491260762065108)
XLA Ops:
  0.6 0.0 copy-start
  0.7 0.1 xor.31
  0.8 0.8 copy-done
  1.5 0.7 gather_fusion
  2.3 7.8 %collective-permute-start = (bf16[4,4,4,512]{3,2,0,1:T(4,128)(2,1)S(1)}, bf16[4,4,4,512]{3,2,0,1:T(4,128)(2,1)S(1)}, u32[]{:S(2)}, u32[]{:S(2)}) collective-permute-start(bf16[4,4,4,512]{3,2,0,1:T(4,128)(2,1)S(1)} %copy.23), channel_id=1, source_target_pairs={{0,1},{1,0},{2,3},{3,2},{4,5},{5,4},{6,7},{7,6},{8,9},{9,8},{10,11... | collective-permute-start | bytes 196616 | tf_op jit(solution)/shard_map/ppermute | solution.py:27
  10.0 1.8 %copy.27 = bf16[1,512,1024]{1,2,0:T(8,128)(2,1)S(1)} copy(f32[1,512,1024]{2,1,0:T(8,128)} %param.6) | data formatting | bytes 3145728 | tf_op args[0]
  11.8 1.1 copy.28
  12.9 0.0 copy-start.4
  12.9 3.8 %all-to-all-start = ((bf16[16,64,512]{2,1,0:T(8,128)(2,1)}), bf16[16,64,512]{2,1,0:T(8,128)(2,1)S(1)}, u32[]{:S(2)}, u32[]{:S(2)}) async-start(bf16[16,64,512]{2,1,0:T(8,128)(2,1)} %bitcast.31), calls=%async_computation | async-start | bytes 2097152 | tf_op jit(solution)/shard_map/all_to_all | solution.py:19
  16.8 0.0 copy-done.4
  16.8 0.1 select_reduce_fusion
  16.9 0.0 collective-permute-done
  17.1 1.9 %collective-permute-start.1 = (bf16[2,4,4,512]{3,2,0,1:T(4,128)(2,1)S(1)}, bf16[2,4,4,512]{3,2,0,1:T(4,128)(2,1)S(1)}, u32[]{:S(2)}, u32[]{:S(2)}) collective-permute-start(bf16[2,4,4,512]{3,2,0,1:T(4,128)(2,1)S(1)} %pad_maximum_fusion), channel_id=1, source_target_pairs={{0,2},{1,3},{2,0},{3,1},{4,6},{5,7},{6,4},{7,5},{8,10},{9,11},{10,... | collective-permute-start | bytes 98312 | tf_op jit(solution)/shard_map/ppermute | solution.py:27
  19.0 4.2 %collective-permute-start.2 = (bf16[2,4,4,512]{3,2,1,0:T(4,128)(2,1)S(1)}, bf16[2,4,4,512]{3,2,1,0:T(4,128)(2,1)S(1)}, u32[]{:S(2)}, u32[]{:S(2)}) collective-permute-start(bf16[2,4,4,512]{3,2,1,0:T(4,128)(2,1)S(1)} %pad_maximum_fusion.1), channel_id=1, source_target_pairs={{0,4},{1,5},{2,6},{3,7},{4,0},{5,1},{6,2},{7,3},{8,12},{9,13},{10,... | collective-permute-start | bytes 98312 | tf_op jit(solution)/shard_map/ppermute | solution.py:27
  23.3 4.0 %collective-permute-start.3 = (bf16[2,4,4,512]{3,2,0,1:T(4,128)(2,1)S(1)}, bf16[2,4,4,512]{3,2,0,1:T(4,128)(2,1)S(1)}, u32[]{:S(2)}, u32[]{:S(2)}) collective-permute-start(bf16[2,4,4,512]{3,2,0,1:T(4,128)(2,1)S(1)} %pad_maximum_fusion.2), channel_id=1, source_target_pairs={{0,6},{1,7},{2,4},{3,5},{4,2},{5,3},{6,0},{7,1},{8,14},{9,15},{10,... | collective-permute-start | bytes 98312 | tf_op jit(solution)/shard_map/ppermute | solution.py:27
  27.3 0.0 collective-permute-done.1
  27.3 0.0 collective-permute-done.2
  27.3 3.5 %collective-permute-done.3 = bf16[2,4,4,512]{3,2,0,1:T(4,128)(2,1)S(1)} collective-permute-done((bf16[2,4,4,512]{3,2,0,1:T(4,128)(2,1)S(1)}, bf16[2,4,4,512]{3,2,0,1:T(4,128)(2,1)S(1)}, u32[]{:S(2)}, u32[]{:S(2)}) %collective-permute-start.3) | collective-permute-done | bytes 32800 | tf_op jit(solution)/shard_map/ppermute | solution.py:27
  30.9 9.1 %collective-permute-start.4 = (bf16[4,2,4,512]{3,2,1,0:T(4,128)(2,1)S(1)}, bf16[4,2,4,512]{3,2,1,0:T(4,128)(2,1)S(1)}, u32[]{:S(2)}, u32[]{:S(2)}) collective-permute-start(bf16[4,2,4,512]{3,2,1,0:T(4,128)(2,1)S(1)} %pad_maximum_fusion.3), channel_id=1, source_target_pairs={{0,8},{1,9},{2,10},{3,11},{4,12},{5,13},{6,14},{7,15},{8,0},{9,1},... | collective-permute-start | bytes 98312 | tf_op jit(solution)/shard_map/ppermute | solution.py:27
  40.1 8.2 %collective-permute-start.5 = (bf16[4,2,4,512]{3,2,1,0:T(4,128)(2,1)S(1)}, bf16[4,2,4,512]{3,2,1,0:T(4,128)(2,1)S(1)}, u32[]{:S(2)}, u32[]{:S(2)}) collective-permute-start(bf16[4,2,4,512]{3,2,1,0:T(4,128)(2,1)S(1)} %pad_maximum_fusion.4), channel_id=1, source_target_pairs={{0,16},{1,17},{2,18},{3,19},{4,20},{5,21},{6,22},{7,23},{8,24},{9,... | collective-permute-start | bytes 98312 | tf_op jit(solution)/shard_map/ppermute | solution.py:27
  48.3 1.9 %collective-permute-start.6 = (bf16[4,2,4,512]{3,2,1,0:T(4,128)(2,1)S(1)}, bf16[4,2,4,512]{3,2,1,0:T(4,128)(2,1)S(1)}, u32[]{:S(2)}, u32[]{:S(2)}) collective-permute-start(bf16[4,2,4,512]{3,2,1,0:T(4,128)(2,1)S(1)} %pad_maximum_fusion.5), channel_id=1, source_target_pairs={{0,24},{1,25},{2,26},{3,27},{4,28},{5,29},{6,30},{7,31},{8,16},{9,... | collective-permute-start | bytes 98312 | tf_op jit(solution)/shard_map/ppermute | solution.py:27
  50.3 0.0 all-to-all-done
  50.3 1.6 gather_fusion.2
  51.9 5.7 %all-to-all-start.1 = ((bf16[16,64,512]{2,1,0:T(8,128)(2,1)}), bf16[16,64,512]{2,1,0:T(8,128)(2,1)S(1)}, u32[]{:S(2)}, u32[]{:S(2)}) async-start(bf16[16,64,512]{2,1,0:T(8,128)(2,1)} %gather_fusion.2), calls=%async_computation.1 | async-start | bytes 2097152 | tf_op jit(solution)/shard_map/all_to_all | solution.py:19
  57.6 0.0 collective-permute-done.4
  57.7 0.0 collective-permute-done.5
  57.7 0.4 collective-permute-done.6
  58.1 0.7 gather_fusion.1
  58.7 0.7 reshape.177.inputs_ref
  59.4 14.7 %all-to-all-done.1 = bf16[16,64,512]{2,1,0:T(8,128)(2,1)S(1)} async-done(((bf16[16,64,512]{2,1,0:T(8,128)(2,1)}), bf16[16,64,512]{2,1,0:T(8,128)(2,1)S(1)}, u32[]{:S(2)}, u32[]{:S(2)}) %all-to-all-start.1) | async-done | bytes 1048608 | tf_op jit(solution)/shard_map/all_to_all | solution.py:19
  74.1 0.0 copy-start.1
  74.1 1.0 copy-done.1
  75.1 3.8 %shard_map.77 = bf16[32,8,2816]{2,1,0:T(8,128)(2,1)} custom-call(bf16[128,512]{1,0:T(8,128)(2,1)} %reshape.177.inputs_ref, bf16[32,4,8,512]{3,2,1,0:T(8,128)(2,1)} %bitcast.92), custom_call_target="tpu_custom_call" | custom-call | flops 134217728 | bytes 3000000 | tf_op jit(solution)/shard_map/pallas_call | solution.py:100
  78.9 13.4 %all-to-all-start.2 = ((bf16[32,8,2816]{2,1,0:T(8,128)(2,1)}), bf16[32,8,2816]{2,1,0:T(8,128)(2,1)S(1)}, u32[]{:S(2)}, u32[]{:S(2)}) async-start(bf16[32,8,2816]{2,1,0:T(8,128)(2,1)} %shard_map.77), calls=%async_computation.2 | async-start | bytes 2883584 | tf_op jit(solution)/shard_map/all_to_all | solution.py:19
  92.3 0.0 copy-done.3
  92.4 0.0 copy-done.5
  92.4 0.1 dynamic_slice.3
  92.4 0.1 iota_compare_fusion.1
  92.5 0.0 copy-done.2
  92.5 0.5 fusion.32
  93.0 70.0 %all-to-all-done.2 = bf16[32,8,2816]{2,1,0:T(8,128)(2,1)S(1)} async-done(((bf16[32,8,2816]{2,1,0:T(8,128)(2,1)}), bf16[32,8,2816]{2,1,0:T(8,128)(2,1)S(1)}, u32[]{:S(2)}, u32[]{:S(2)}) %all-to-all-start.2) | async-done | bytes 1441824 | tf_op jit(solution)/shard_map/all_to_all | solution.py:19
  163.0 0.1 convert_reduce_fusion
  163.1 0.1 slice.209
  163.2 1.1 copy.29
  164.3 0.1 fusion.17
  164.4 0.2 fusion.4
  164.7 0.3 fusion.1
  165.0 0.7 copy.39
  (38 shorter events, 0.5 us)
Async XLA Ops:
  0.6 0.9 copy-start
  2.3 14.7 %collective-permute-start = (bf16[4,4,4,512]{3,2,0,1:T(4,128)(2,1)S(1)}, bf16[4,4,4,512]{3,2,0,1:T(4,128)(2,1)S(1)}, u32[]{:S(2)}, u32[]{:S(2)}) collective-permute-start(bf16[4,4,4,512]{3,2,0,1:T(4,128)(2,1)S(1)} %copy.23), channel_id=1, source_target_pairs={{0,1},{1,0},{2,3},{3,2},{4,5},{5,4},{6,7},{7,6},{8,9},{9,8},{10,11... | collective-permute-start | bytes 196616 | tf_op jit(solution)/shard_map/ppermute | solution.py:27
  12.9 3.8 %copy-start.4 = (s32[16]{0:T(128)S(1)}, s32[16]{0:T(128)}, u32[]{:S(2)}) copy-start(s32[16]{0:T(128)} %param.7) | copy-start | bytes 196
  12.9 37.3 %all-to-all-start = ((bf16[16,64,512]{2,1,0:T(8,128)(2,1)}), bf16[16,64,512]{2,1,0:T(8,128)(2,1)S(1)}, u32[]{:S(2)}, u32[]{:S(2)}) async-start(bf16[16,64,512]{2,1,0:T(8,128)(2,1)} %bitcast.31), calls=%async_computation | async-start | bytes 2097152 | tf_op jit(solution)/shard_map/all_to_all | solution.py:19
  17.1 10.2 %collective-permute-start.1 = (bf16[2,4,4,512]{3,2,0,1:T(4,128)(2,1)S(1)}, bf16[2,4,4,512]{3,2,0,1:T(4,128)(2,1)S(1)}, u32[]{:S(2)}, u32[]{:S(2)}) collective-permute-start(bf16[2,4,4,512]{3,2,0,1:T(4,128)(2,1)S(1)} %pad_maximum_fusion), channel_id=1, source_target_pairs={{0,2},{1,3},{2,0},{3,1},{4,6},{5,7},{6,4},{7,5},{8,10},{9,11},{10,... | collective-permute-start | bytes 98312 | tf_op jit(solution)/shard_map/ppermute | solution.py:27
  19.0 8.3 %collective-permute-start.2 = (bf16[2,4,4,512]{3,2,1,0:T(4,128)(2,1)S(1)}, bf16[2,4,4,512]{3,2,1,0:T(4,128)(2,1)S(1)}, u32[]{:S(2)}, u32[]{:S(2)}) collective-permute-start(bf16[2,4,4,512]{3,2,1,0:T(4,128)(2,1)S(1)} %pad_maximum_fusion.1), channel_id=1, source_target_pairs={{0,4},{1,5},{2,6},{3,7},{4,0},{5,1},{6,2},{7,3},{8,12},{9,13},{10,... | collective-permute-start | bytes 98312 | tf_op jit(solution)/shard_map/ppermute | solution.py:27
  23.3 7.6 %collective-permute-start.3 = (bf16[2,4,4,512]{3,2,0,1:T(4,128)(2,1)S(1)}, bf16[2,4,4,512]{3,2,0,1:T(4,128)(2,1)S(1)}, u32[]{:S(2)}, u32[]{:S(2)}) collective-permute-start(bf16[2,4,4,512]{3,2,0,1:T(4,128)(2,1)S(1)} %pad_maximum_fusion.2), channel_id=1, source_target_pairs={{0,6},{1,7},{2,4},{3,5},{4,2},{5,3},{6,0},{7,1},{8,14},{9,15},{10,... | collective-permute-start | bytes 98312 | tf_op jit(solution)/shard_map/ppermute | solution.py:27
  30.9 26.7 %collective-permute-start.4 = (bf16[4,2,4,512]{3,2,1,0:T(4,128)(2,1)S(1)}, bf16[4,2,4,512]{3,2,1,0:T(4,128)(2,1)S(1)}, u32[]{:S(2)}, u32[]{:S(2)}) collective-permute-start(bf16[4,2,4,512]{3,2,1,0:T(4,128)(2,1)S(1)} %pad_maximum_fusion.3), channel_id=1, source_target_pairs={{0,8},{1,9},{2,10},{3,11},{4,12},{5,13},{6,14},{7,15},{8,0},{9,1},... | collective-permute-start | bytes 98312 | tf_op jit(solution)/shard_map/ppermute | solution.py:27
  40.1 17.6 %collective-permute-start.5 = (bf16[4,2,4,512]{3,2,1,0:T(4,128)(2,1)S(1)}, bf16[4,2,4,512]{3,2,1,0:T(4,128)(2,1)S(1)}, u32[]{:S(2)}, u32[]{:S(2)}) collective-permute-start(bf16[4,2,4,512]{3,2,1,0:T(4,128)(2,1)S(1)} %pad_maximum_fusion.4), channel_id=1, source_target_pairs={{0,16},{1,17},{2,18},{3,19},{4,20},{5,21},{6,22},{7,23},{8,24},{9,... | collective-permute-start | bytes 98312 | tf_op jit(solution)/shard_map/ppermute | solution.py:27
  48.3 9.7 %collective-permute-start.6 = (bf16[4,2,4,512]{3,2,1,0:T(4,128)(2,1)S(1)}, bf16[4,2,4,512]{3,2,1,0:T(4,128)(2,1)S(1)}, u32[]{:S(2)}, u32[]{:S(2)}) collective-permute-start(bf16[4,2,4,512]{3,2,1,0:T(4,128)(2,1)S(1)} %pad_maximum_fusion.5), channel_id=1, source_target_pairs={{0,24},{1,25},{2,26},{3,27},{4,28},{5,29},{6,30},{7,31},{8,16},{9,... | collective-permute-start | bytes 98312 | tf_op jit(solution)/shard_map/ppermute | solution.py:27
  51.9 22.3 %all-to-all-start.1 = ((bf16[16,64,512]{2,1,0:T(8,128)(2,1)}), bf16[16,64,512]{2,1,0:T(8,128)(2,1)S(1)}, u32[]{:S(2)}, u32[]{:S(2)}) async-start(bf16[16,64,512]{2,1,0:T(8,128)(2,1)} %gather_fusion.2), calls=%async_computation.1 | async-start | bytes 2097152 | tf_op jit(solution)/shard_map/all_to_all | solution.py:19
  74.1 1.0 copy-start.1
  78.9 13.5 %copy-start.3 = (bf16[16,2048]{1,0:T(8,128)(2,1)S(1)}, bf16[16,2048]{1,0:T(8,128)(2,1)}, u32[]{:S(2)}) copy-start(bf16[16,2048]{1,0:T(8,128)(2,1)} %param.9) | copy-start | bytes 196612
  78.9 13.5 %copy-start.5 = (s32[128]{0:T(128)S(1)}, s32[128]{0:T(128)}, u32[]{:S(2)}) copy-start(s32[128]{0:T(128)} %param.11) | copy-start | bytes 1540
  78.9 13.7 %copy-start.2 = (bf16[16,128,256]{2,1,0:T(8,128)(2,1)S(1)}, bf16[16,128,256]{2,1,0:T(8,128)(2,1)}, u32[]{:S(2)}) copy-start(bf16[16,128,256]{2,1,0:T(8,128)(2,1)} %param.10) | copy-start | bytes 3145732
  78.9 84.1 %all-to-all-start.2 = ((bf16[32,8,2816]{2,1,0:T(8,128)(2,1)}), bf16[32,8,2816]{2,1,0:T(8,128)(2,1)S(1)}, u32[]{:S(2)}, u32[]{:S(2)}) async-start(bf16[32,8,2816]{2,1,0:T(8,128)(2,1)} %shard_map.77), calls=%async_computation.2 | async-start | bytes 2883584 | tf_op jit(solution)/shard_map/all_to_all | solution.py:19

commit v4 on v3

--- a/solution.py
+++ b/solution.py
@@ -4,6 +4,7 @@
 import jax.numpy as jnp
 from jax import lax
 from jax.experimental import pallas as pl
+from jax.experimental.pallas import tpu as pltpu
 from jax.sharding import PartitionSpec as P
 
 
@@ -34,9 +35,7 @@
     near = [near[0]] + [send(near[k], k << 1) for k in range(1, 4)]
     far = [jnp.stack([v[:, k] for v in near]) for k in range(4)]
     far = [far[0]] + [send(far[k], k << 3) for k in range(1, 4)]
-    merged = jnp.concatenate(far).reshape((shards,) + blocks.shape[1:])
-    relative = me ^ jnp.arange(shards, dtype=jnp.int32)
-    return merged.at[relative].get(mode="promise_in_bounds")
+    return jnp.concatenate(far).reshape((shards,) + blocks.shape[1:])
 
 
 def attend(query_rows, cache_rows, fresh_rows, row_lengths):
@@ -69,47 +68,100 @@
     return context.reshape(context.shape[0], QPK * HD).astype(jnp.bfloat16)
 
 
-def pack_kernel(inputs_ref, routed_ref, out_ref):
-    head = pl.program_id(0)
-    shards, _, piece, depth = routed_ref.shape
-    half = piece
-    per_head = shards // KVH
-    block = routed_ref[:, 0]
-    out_ref[:, :, pl.ds(pl.multiple_of(head * depth, depth), depth)] = block
-    product = lax.dot_general(
-        inputs_ref[...],
-        block.reshape(2 * HD, depth),
-        (((1,), (1,)), ((), ())),
-        preferred_element_type=jnp.float32,
-    )
-    upper = product.astype(jnp.bfloat16)
-    lower = (product[:, :HD] - upper[:, :HD].astype(jnp.float32)).astype(jnp.bfloat16)
-    base = KVH * depth
-    for i in range(per_head):
-        for j in range(2):
-            rows = slice((2 * i + j) * half, (2 * i + j + 1) * half)
-            start = base + j * 2 * HD
-            out_ref[pl.ds(head * per_head + i, 1), :, start : start + 2 * HD] = upper[rows][None]
-            start = base + 4 * HD + j * HD
-            out_ref[pl.ds(head * per_head + i, 1), :, start : start + HD] = lower[rows][None]
-
-
-def pack(inputs, routed):
-    shards, _, piece, depth = routed.shape
-    width = KVH * depth + 6 * HD
+VMEM = pl.BlockSpec(memory_space=pltpu.VMEM)
+
+
+def flip_kernel(weights_ref, out_ref):
+    step = pl.program_id(0)
+    shards, heads, piece, _ = out_ref.shape
+    rows = weights_ref.shape[1]
+    lanes = pl.ds(pl.multiple_of(step * rows, rows), rows)
+    for h in range(heads):
+        width = shards * piece
+        block = weights_ref[0, :, h * width : (h + 1) * width].astype(jnp.bfloat16)
+        out_ref[:, h, :, lanes] = block.T.reshape(shards, piece, rows)
+
+
+def flip(weights, shards):
+    _, depth, columns = weights.shape
+    piece = columns // KVH // shards
+    rows = 128
+    return pl.pallas_call(
+        flip_kernel,
+        grid=(depth // rows,),
+        in_specs=[pl.BlockSpec((1, rows, columns), lambda i: (0, i, 0))],
+        out_specs=VMEM,
+        out_shape=jax.ShapeDtypeStruct((shards, KVH, piece, depth), jnp.bfloat16),
+        cost_estimate=pl.CostEstimate(flops=2_000_000, bytes_accessed=3_000_000, transcendentals=0),
+        compiler_params=pltpu.CompilerParams(vmem_limit_bytes=12 * 1024 * 1024),
+        name="flip",
+    )(weights)
+
+
+def pick_kernel(group_ref, spread_ref, out_ref):
+    def move(s, carry):
+        out_ref[group_ref[s]] = spread_ref[s]
+        return carry
+
+    lax.fori_loop(0, spread_ref.shape[0], move, 0)
+
+
+def pick(section_to_group, spread):
+    return pl.pallas_call(
+        pick_kernel,
+        in_specs=[pl.BlockSpec(memory_space=pltpu.SMEM), VMEM],
+        out_specs=VMEM,
+        out_shape=jax.ShapeDtypeStruct(spread.shape, spread.dtype),
+        cost_estimate=pl.CostEstimate(flops=1_000_000, bytes_accessed=2_000_000, transcendentals=0),
+        compiler_params=pltpu.CompilerParams(vmem_limit_bytes=12 * 1024 * 1024),
+        name="pick",
+    )(section_to_group, spread)
+
+
+def pack_kernel(me_ref, inputs_ref, routed_ref, out_ref, rows_ref):
+    me = me_ref[0]
+    shards, heads, piece, depth = routed_ref.shape
+    per_head = shards // heads
+    own = inputs_ref.shape[1]
+    for d in range(shards):
+        rows_ref[d * own : (d + 1) * own, :] = inputs_ref[me ^ d].astype(jnp.float32)
+    inputs = rows_ref[...].astype(jnp.bfloat16)
+    base = heads * depth
+    for h in range(heads):
+        block = routed_ref[:, h]
+        out_ref[:, :, h * depth : (h + 1) * depth] = block
+        product = lax.dot_general(
+            inputs,
+            block.reshape(shards * piece, depth),
+            (((1,), (1,)), ((), ())),
+            preferred_element_type=jnp.float32,
+        )
+        upper = product.astype(jnp.bfloat16)
+        lower = (product[:, :HD] - upper[:, :HD].astype(jnp.float32)).astype(jnp.bfloat16)
+        for i in range(per_head):
+            for j in range(2):
+                rows = slice((2 * i + j) * piece, (2 * i + j + 1) * piece)
+                start = base + j * 2 * HD
+                out_ref[h * per_head + i, :, start : start + 2 * HD] = upper[rows]
+                start = base + 4 * HD + j * HD
+                out_ref[h * per_head + i, :, start : start + HD] = lower[rows]
+
+
+def pack(me, inputs, routed):
+    shards, heads, piece, depth = routed.shape
+    width = heads * depth + 6 * HD
     return pl.pallas_call(
         pack_kernel,
-        grid=(KVH,),
-        in_specs=[
-            pl.BlockSpec((ROWS, depth), lambda h: (0, 0)),
-            pl.BlockSpec((shards, 1, piece, depth), lambda h: (0, h, 0, 0)),
-        ],
-        out_specs=pl.BlockSpec((shards, piece, width), lambda h: (0, 0, 0)),
+        in_specs=[pl.BlockSpec(memory_space=pltpu.SMEM), VMEM, VMEM],
+        out_specs=VMEM,
         out_shape=jax.ShapeDtypeStruct((shards, piece, width), jnp.bfloat16),
+        scratch_shapes=[pltpu.VMEM((ROWS, depth), jnp.float32)],
         cost_estimate=pl.CostEstimate(
-            flops=2 * ROWS * KVH * 2 * HD * depth, bytes_accessed=3_000_000, transcendentals=0
+            flops=2 * ROWS * heads * 2 * HD * depth, bytes_accessed=3_000_000, transcendentals=0
         ),
-    )(inputs, routed)
+        compiler_params=pltpu.CompilerParams(vmem_limit_bytes=12 * 1024 * 1024),
+        name="pack",
+    )(me, inputs, routed)
 
 
 def step(train_weights, section_to_group, hidden, queries, kv_cache, lengths):
@@ -119,20 +171,14 @@
     row_block = ROWS // per_head
     piece_cols = 2 * HD // shards
     slice_rows = train_weights.shape[1]
-    groups = jnp.arange(sections, dtype=jnp.int32)
-    source = jnp.sum(
-        jnp.where(section_to_group[None, :] == groups[:, None], groups[None, :], 0), axis=1
-    )
     own = hidden.shape[0]
     inputs = spread_rows(hidden.reshape(own, shards, slice_rows).transpose(1, 0, 2))
-    inputs = inputs.reshape(ROWS, slice_rows)
-    flipped = train_weights[0].astype(jnp.bfloat16).T
-    flipped = flipped.reshape(KVH, shards, piece_cols, slice_rows).transpose(1, 0, 2, 3)
-    flipped = flipped.reshape(sections, -1, slice_rows)
+    flipped = flip(train_weights, shards).reshape(sections, -1, slice_rows)
     spread = exchange(flipped, "section")
-    picked = spread.at[source].get(mode="promise_in_bounds")
+    picked = pick(section_to_group, spread)
     routed = exchange(picked, "section").reshape(shards, KVH, piece_cols, slice_rows)
-    received = exchange(pack(inputs, routed), "shard")
+    me = lax.axis_index("shard").astype(jnp.int32).reshape(1)
+    received = exchange(pack(me, inputs, routed), "shard")
     base = KVH * slice_rows
     layer_out = received[:, :, :base].reshape(shards, piece_cols, KVH, slice_rows)
     layer_out = layer_out.transpose(2, 1, 0, 3).reshape(1, KVH, piece_cols, D)

time: 166 us -> 163 us (0.982)
  local copies, waits for them, and re-layouts: 10.5 us -> 5.31 us
    gather x2 -> x0, local copies, waits for them, and re-layouts: 2.25 us -> none  [the longest x1 1.58 us: step(): picked = spread.at[source].get(mode='promise_in_bounds')]
    unnamed x20 -> x19, local copies, waits for them, and re-layouts: 4.29 us -> 3.13 us
    pallas_call x1 -> x3, Pallas kernels: 3.77 us -> 4.78 us  [the longest x1 1.65 us: pick(): pl.pallas_call(pick_kernel, in_specs=[pl.BlockSpec(memory_space=pltpu.SME...]
  transfers between devices with their start and end apart: 10 -> 10, of which waited for: 4 -> 4; matrix products, arithmetic and copies ran while one was open for 4% -> 1% of each run, Pallas kernels for 0% -> 2%
where the time goes in v4:
time: 163 us
  waiting for transfers between devices  89.9 us (55%)
  starting transfers between devices  60 us (37%)
  local copies, waits for them, and re-layouts  5.31 us (3%)
  Pallas kernels  4.78 us (3%)
    all_to_all x3, waiting for transfers between devices, exchange(): return lax.all_to_all(blocks, axis, split_axis=0, concat_axis=0, tiled=True)  86.1 us
    ppermute x7, starting transfers between devices, send(): return lax.ppermute(values, 'shard', [(i, i ^ bits) for i in range(shards)])  37.1 us
    all_to_all x3, starting transfers between devices, exchange(): return lax.all_to_all(blocks, axis, split_axis=0, concat_axis=0, tiled=True)  22.9 us
    ppermute x7, waiting for transfers between devices, send(): return lax.ppermute(values, 'shard', [(i, i ^ bits) for i in range(shards)])  3.83 us
  transfers between devices with their start and end apart: 10, of which 4 were waited for; matrix products, arithmetic and copies ran while one was open for 1% of the time, Pallas kernels for 2%

profile of v4, /device:TPU:4, one launch (start us, length us, event | category | flops | bytes accessed | tf_op | source)
XLA Modules:
  0.0 162.6 jit_solution(13681959995386051036)
XLA Ops:
  0.6 0.0 copy-start
  0.7 0.1 xor.18
  0.8 0.8 copy-done
  1.5 0.7 gather_fusion
  2.3 7.8 %collective-permute-start = (bf16[4,4,4,512]{3,2,0,1:T(4,128)(2,1)S(1)}, bf16[4,4,4,512]{3,2,0,1:T(4,128)(2,1)S(1)}, u32[]{:S(2)}, u32[]{:S(2)}) collective-permute-start(bf16[4,4,4,512]{3,2,0,1:T(4,128)(2,1)S(1)} %copy.19), channel_id=1, source_target_pairs={{0,1},{1,0},{2,3},{3,2},{4,5},{5,4},{6,7},{7,6},{8,9},{9,8},{10,11... | collective-permute-start | bytes 196616 | tf_op jit(solution)/shard_map/ppermute | solution.py:28
  10.0 0.0 copy-start.1
  10.1 1.6 copy-done.1
  11.6 1.5 flip.1
  13.2 0.0 copy-start.2
  13.2 3.8 %all-to-all-start = ((bf16[16,64,512]{2,1,0:T(8,128)(2,1)}), bf16[16,64,512]{2,1,0:T(8,128)(2,1)S(1)}, u32[]{:S(2)}, u32[]{:S(2)}) async-start(bf16[16,64,512]{2,1,0:T(8,128)(2,1)} %bitcast.27), calls=%async_computation | async-start | bytes 2097152 | tf_op jit(solution)/shard_map/all_to_all | solution.py:20
  17.0 0.0 collective-permute-done
  17.1 1.9 %collective-permute-start.1 = (bf16[2,4,4,512]{3,2,0,1:T(4,128)(2,1)S(1)}, bf16[2,4,4,512]{3,2,0,1:T(4,128)(2,1)S(1)}, u32[]{:S(2)}, u32[]{:S(2)}) collective-permute-start(bf16[2,4,4,512]{3,2,0,1:T(4,128)(2,1)S(1)} %pad_maximum_fusion), channel_id=1, source_target_pairs={{0,2},{1,3},{2,0},{3,1},{4,6},{5,7},{6,4},{7,5},{8,10},{9,11},{10,... | collective-permute-start | bytes 98312 | tf_op jit(solution)/shard_map/ppermute | solution.py:28
  19.1 4.2 %collective-permute-start.2 = (bf16[2,4,4,512]{3,2,1,0:T(4,128)(2,1)S(1)}, bf16[2,4,4,512]{3,2,1,0:T(4,128)(2,1)S(1)}, u32[]{:S(2)}, u32[]{:S(2)}) collective-permute-start(bf16[2,4,4,512]{3,2,1,0:T(4,128)(2,1)S(1)} %pad_maximum_fusion.1), channel_id=1, source_target_pairs={{0,4},{1,5},{2,6},{3,7},{4,0},{5,1},{6,2},{7,3},{8,12},{9,13},{10,... | collective-permute-start | bytes 98312 | tf_op jit(solution)/shard_map/ppermute | solution.py:28
  23.3 4.0 %collective-permute-start.3 = (bf16[2,4,4,512]{3,2,0,1:T(4,128)(2,1)S(1)}, bf16[2,4,4,512]{3,2,0,1:T(4,128)(2,1)S(1)}, u32[]{:S(2)}, u32[]{:S(2)}) collective-permute-start(bf16[2,4,4,512]{3,2,0,1:T(4,128)(2,1)S(1)} %pad_maximum_fusion.2), channel_id=1, source_target_pairs={{0,6},{1,7},{2,4},{3,5},{4,2},{5,3},{6,0},{7,1},{8,14},{9,15},{10,... | collective-permute-start | bytes 98312 | tf_op jit(solution)/shard_map/ppermute | solution.py:28
  27.3 0.0 collective-permute-done.1
  27.3 0.0 collective-permute-done.2
  27.4 3.5 %collective-permute-done.3 = bf16[2,4,4,512]{3,2,0,1:T(4,128)(2,1)S(1)} collective-permute-done((bf16[2,4,4,512]{3,2,0,1:T(4,128)(2,1)S(1)}, bf16[2,4,4,512]{3,2,0,1:T(4,128)(2,1)S(1)}, u32[]{:S(2)}, u32[]{:S(2)}) %collective-permute-start.3) | collective-permute-done | bytes 32800 | tf_op jit(solution)/shard_map/ppermute | solution.py:28
  31.0 9.1 %collective-permute-start.4 = (bf16[4,2,4,512]{3,2,1,0:T(4,128)(2,1)S(1)}, bf16[4,2,4,512]{3,2,1,0:T(4,128)(2,1)S(1)}, u32[]{:S(2)}, u32[]{:S(2)}) collective-permute-start(bf16[4,2,4,512]{3,2,1,0:T(4,128)(2,1)S(1)} %pad_maximum_fusion.3), channel_id=1, source_target_pairs={{0,8},{1,9},{2,10},{3,11},{4,12},{5,13},{6,14},{7,15},{8,0},{9,1},... | collective-permute-start | bytes 98312 | tf_op jit(solution)/shard_map/ppermute | solution.py:28
  40.1 8.2 %collective-permute-start.5 = (bf16[4,2,4,512]{3,2,1,0:T(4,128)(2,1)S(1)}, bf16[4,2,4,512]{3,2,1,0:T(4,128)(2,1)S(1)}, u32[]{:S(2)}, u32[]{:S(2)}) collective-permute-start(bf16[4,2,4,512]{3,2,1,0:T(4,128)(2,1)S(1)} %pad_maximum_fusion.4), channel_id=1, source_target_pairs={{0,16},{1,17},{2,18},{3,19},{4,20},{5,21},{6,22},{7,23},{8,24},{9,... | collective-permute-start | bytes 98312 | tf_op jit(solution)/shard_map/ppermute | solution.py:28
  48.4 1.9 %collective-permute-start.6 = (bf16[4,2,4,512]{3,2,1,0:T(4,128)(2,1)S(1)}, bf16[4,2,4,512]{3,2,1,0:T(4,128)(2,1)S(1)}, u32[]{:S(2)}, u32[]{:S(2)}) collective-permute-start(bf16[4,2,4,512]{3,2,1,0:T(4,128)(2,1)S(1)} %pad_maximum_fusion.5), channel_id=1, source_target_pairs={{0,24},{1,25},{2,26},{3,27},{4,28},{5,29},{6,30},{7,31},{8,16},{9,... | collective-permute-start | bytes 98312 | tf_op jit(solution)/shard_map/ppermute | solution.py:28
  50.3 0.0 all-to-all-done.spread_ref
  50.3 0.0 copy-done.2
  50.3 1.7 %pick.1 = bf16[16,64,512]{2,1,0:T(8,128)(2,1)} custom-call(s32[16]{0:T(128)S(1)} %copy-done.2, bf16[16,64,512]{2,1,0:T(8,128)(2,1)S(1)} %all-to-all-done.spread_ref), custom_call_target="tpu_custom_call" | custom-call | flops 1000000 | bytes 2000000 | tf_op jit(solution)/shard_map/pick/pallas_call | solution.py:110
  52.0 5.7 %all-to-all-start.1 = ((bf16[16,64,512]{2,1,0:T(8,128)(2,1)}), bf16[16,64,512]{2,1,0:T(8,128)(2,1)S(1)}, u32[]{:S(2)}, u32[]{:S(2)}) async-start(bf16[16,64,512]{2,1,0:T(8,128)(2,1)} %pick.1), calls=%async_computation.1 | async-start | bytes 2097152 | tf_op jit(solution)/shard_map/all_to_all | solution.py:20
  57.8 0.0 collective-permute-done.4
  57.8 0.0 collective-permute-done.5
  57.8 0.3 collective-permute-done.6
  58.1 16.1 %all-to-all-done.1 = bf16[16,64,512]{2,1,0:T(8,128)(2,1)S(1)} async-done(((bf16[16,64,512]{2,1,0:T(8,128)(2,1)}), bf16[16,64,512]{2,1,0:T(8,128)(2,1)S(1)}, u32[]{:S(2)}, u32[]{:S(2)}) %all-to-all-start.1) | async-done | bytes 1048608 | tf_op jit(solution)/shard_map/all_to_all | solution.py:20
  74.2 1.6 pack.1
  75.9 0.0 copy-start.4
  75.9 0.0 copy-start.5
  75.9 0.0 copy-start.3
  75.9 13.4 %all-to-all-start.2 = ((bf16[32,8,2816]{2,1,0:T(8,128)(2,1)}), bf16[32,8,2816]{2,1,0:T(8,128)(2,1)S(1)}, u32[]{:S(2)}, u32[]{:S(2)}) async-start(bf16[32,8,2816]{2,1,0:T(8,128)(2,1)} %pack.1), calls=%async_computation.2 | async-start | bytes 2883584 | tf_op jit(solution)/shard_map/all_to_all | solution.py:20
  89.3 0.0 copy-done.4
  89.4 0.0 copy-done.5
  89.4 0.1 dynamic_slice.3
  89.4 0.1 iota_compare_fusion
  89.5 0.0 copy-done.3
  89.5 0.5 fusion.30
  90.0 70.0 %all-to-all-done.2 = bf16[32,8,2816]{2,1,0:T(8,128)(2,1)S(1)} async-done(((bf16[32,8,2816]{2,1,0:T(8,128)(2,1)}), bf16[32,8,2816]{2,1,0:T(8,128)(2,1)S(1)}, u32[]{:S(2)}, u32[]{:S(2)}) %all-to-all-start.2) | async-done | bytes 1441824 | tf_op jit(solution)/shard_map/all_to_all | solution.py:20
  160.0 0.1 convert_reduce_fusion
  160.0 0.1 slice.205
  160.2 1.1 copy.24
  161.3 0.1 fusion.17
  161.4 0.2 fusion.4
  161.6 0.3 fusion.1
  162.0 0.7 copy.35
  (31 shorter events, 0.5 us)
Async XLA Ops:
  0.6 0.9 copy-start
  2.3 14.7 %collective-permute-start = (bf16[4,4,4,512]{3,2,0,1:T(4,128)(2,1)S(1)}, bf16[4,4,4,512]{3,2,0,1:T(4,128)(2,1)S(1)}, u32[]{:S(2)}, u32[]{:S(2)}) collective-permute-start(bf16[4,4,4,512]{3,2,0,1:T(4,128)(2,1)S(1)} %copy.19), channel_id=1, source_target_pairs={{0,1},{1,0},{2,3},{3,2},{4,5},{5,4},{6,7},{7,6},{8,9},{9,8},{10,11... | collective-permute-start | bytes 196616 | tf_op jit(solution)/shard_map/ppermute | solution.py:28
  10.0 1.6 copy-start.1
  13.2 37.2 %copy-start.2 = (s32[16]{0:T(128)S(1)}, s32[16]{0:T(128)}, u32[]{:S(2)}) copy-start(s32[16]{0:T(128)} %group_ref.1) | copy-start | bytes 196
  13.2 37.2 %all-to-all-start = ((bf16[16,64,512]{2,1,0:T(8,128)(2,1)}), bf16[16,64,512]{2,1,0:T(8,128)(2,1)S(1)}, u32[]{:S(2)}, u32[]{:S(2)}) async-start(bf16[16,64,512]{2,1,0:T(8,128)(2,1)} %bitcast.27), calls=%async_computation | async-start | bytes 2097152 | tf_op jit(solution)/shard_map/all_to_all | solution.py:20
  17.1 10.2 %collective-permute-start.1 = (bf16[2,4,4,512]{3,2,0,1:T(4,128)(2,1)S(1)}, bf16[2,4,4,512]{3,2,0,1:T(4,128)(2,1)S(1)}, u32[]{:S(2)}, u32[]{:S(2)}) collective-permute-start(bf16[2,4,4,512]{3,2,0,1:T(4,128)(2,1)S(1)} %pad_maximum_fusion), channel_id=1, source_target_pairs={{0,2},{1,3},{2,0},{3,1},{4,6},{5,7},{6,4},{7,5},{8,10},{9,11},{10,... | collective-permute-start | bytes 98312 | tf_op jit(solution)/shard_map/ppermute | solution.py:28
  19.1 8.3 %collective-permute-start.2 = (bf16[2,4,4,512]{3,2,1,0:T(4,128)(2,1)S(1)}, bf16[2,4,4,512]{3,2,1,0:T(4,128)(2,1)S(1)}, u32[]{:S(2)}, u32[]{:S(2)}) collective-permute-start(bf16[2,4,4,512]{3,2,1,0:T(4,128)(2,1)S(1)} %pad_maximum_fusion.1), channel_id=1, source_target_pairs={{0,4},{1,5},{2,6},{3,7},{4,0},{5,1},{6,2},{7,3},{8,12},{9,13},{10,... | collective-permute-start | bytes 98312 | tf_op jit(solution)/shard_map/ppermute | solution.py:28
  23.3 7.6 %collective-permute-start.3 = (bf16[2,4,4,512]{3,2,0,1:T(4,128)(2,1)S(1)}, bf16[2,4,4,512]{3,2,0,1:T(4,128)(2,1)S(1)}, u32[]{:S(2)}, u32[]{:S(2)}) collective-permute-start(bf16[2,4,4,512]{3,2,0,1:T(4,128)(2,1)S(1)} %pad_maximum_fusion.2), channel_id=1, source_target_pairs={{0,6},{1,7},{2,4},{3,5},{4,2},{5,3},{6,0},{7,1},{8,14},{9,15},{10,... | collective-permute-start | bytes 98312 | tf_op jit(solution)/shard_map/ppermute | solution.py:28
  31.0 26.8 %collective-permute-start.4 = (bf16[4,2,4,512]{3,2,1,0:T(4,128)(2,1)S(1)}, bf16[4,2,4,512]{3,2,1,0:T(4,128)(2,1)S(1)}, u32[]{:S(2)}, u32[]{:S(2)}) collective-permute-start(bf16[4,2,4,512]{3,2,1,0:T(4,128)(2,1)S(1)} %pad_maximum_fusion.3), channel_id=1, source_target_pairs={{0,8},{1,9},{2,10},{3,11},{4,12},{5,13},{6,14},{7,15},{8,0},{9,1},... | collective-permute-start | bytes 98312 | tf_op jit(solution)/shard_map/ppermute | solution.py:28
  40.1 17.7 %collective-permute-start.5 = (bf16[4,2,4,512]{3,2,1,0:T(4,128)(2,1)S(1)}, bf16[4,2,4,512]{3,2,1,0:T(4,128)(2,1)S(1)}, u32[]{:S(2)}, u32[]{:S(2)}) collective-permute-start(bf16[4,2,4,512]{3,2,1,0:T(4,128)(2,1)S(1)} %pad_maximum_fusion.4), channel_id=1, source_target_pairs={{0,16},{1,17},{2,18},{3,19},{4,20},{5,21},{6,22},{7,23},{8,24},{9,... | collective-permute-start | bytes 98312 | tf_op jit(solution)/shard_map/ppermute | solution.py:28
  48.4 9.7 %collective-permute-start.6 = (bf16[4,2,4,512]{3,2,1,0:T(4,128)(2,1)S(1)}, bf16[4,2,4,512]{3,2,1,0:T(4,128)(2,1)S(1)}, u32[]{:S(2)}, u32[]{:S(2)}) collective-permute-start(bf16[4,2,4,512]{3,2,1,0:T(4,128)(2,1)S(1)} %pad_maximum_fusion.5), channel_id=1, source_target_pairs={{0,24},{1,25},{2,26},{3,27},{4,28},{5,29},{6,30},{7,31},{8,16},{9,... | collective-permute-start | bytes 98312 | tf_op jit(solution)/shard_map/ppermute | solution.py:28
  52.0 22.3 %all-to-all-start.1 = ((bf16[16,64,512]{2,1,0:T(8,128)(2,1)}), bf16[16,64,512]{2,1,0:T(8,128)(2,1)S(1)}, u32[]{:S(2)}, u32[]{:S(2)}) async-start(bf16[16,64,512]{2,1,0:T(8,128)(2,1)} %pick.1), calls=%async_computation.1 | async-start | bytes 2097152 | tf_op jit(solution)/shard_map/all_to_all | solution.py:20
  75.9 13.5 %copy-start.4 = (bf16[16,2048]{1,0:T(8,128)(2,1)S(1)}, bf16[16,2048]{1,0:T(8,128)(2,1)}, u32[]{:S(2)}) copy-start(bf16[16,2048]{1,0:T(8,128)(2,1)} %param.9) | copy-start | bytes 196612
  75.9 13.5 %copy-start.5 = (s32[128]{0:T(128)S(1)}, s32[128]{0:T(128)}, u32[]{:S(2)}) copy-start(s32[128]{0:T(128)} %param.11) | copy-start | bytes 1540
  75.9 13.7 %copy-start.3 = (bf16[16,128,256]{2,1,0:T(8,128)(2,1)S(1)}, bf16[16,128,256]{2,1,0:T(8,128)(2,1)}, u32[]{:S(2)}) copy-start(bf16[16,128,256]{2,1,0:T(8,128)(2,1)} %param.10) | copy-start | bytes 3145732
  75.9 84.1 %all-to-all-start.2 = ((bf16[32,8,2816]{2,1,0:T(8,128)(2,1)}), bf16[32,8,2816]{2,1,0:T(8,128)(2,1)S(1)}, u32[]{:S(2)}, u32[]{:S(2)}) async-start(bf16[32,8,2816]{2,1,0:T(8,128)(2,1)} %pack.1), calls=%async_computation.2 | async-start | bytes 2883584 | tf_op jit(solution)/shard_map/all_to_all | solution.py:20

commit v5 on v4

--- a/solution.py
+++ b/solution.py
@@ -118,50 +118,57 @@
     )(section_to_group, spread)
 
 
-def pack_kernel(me_ref, inputs_ref, routed_ref, out_ref, rows_ref):
+def multiply_kernel(me_ref, inputs_ref, routed_ref, out_ref, rows_ref):
     me = me_ref[0]
     shards, heads, piece, depth = routed_ref.shape
     per_head = shards // heads
     own = inputs_ref.shape[1]
+    block_rows = ROWS // per_head
     for d in range(shards):
         rows_ref[d * own : (d + 1) * own, :] = inputs_ref[me ^ d].astype(jnp.float32)
     inputs = rows_ref[...].astype(jnp.bfloat16)
-    base = heads * depth
     for h in range(heads):
-        block = routed_ref[:, h]
-        out_ref[:, :, h * depth : (h + 1) * depth] = block
         product = lax.dot_general(
             inputs,
-            block.reshape(shards * piece, depth),
+            routed_ref[:, h].reshape(shards * piece, depth),
             (((1,), (1,)), ((), ())),
             preferred_element_type=jnp.float32,
         )
-        upper = product.astype(jnp.bfloat16)
-        lower = (product[:, :HD] - upper[:, :HD].astype(jnp.float32)).astype(jnp.bfloat16)
         for i in range(per_head):
-            for j in range(2):
-                rows = slice((2 * i + j) * piece, (2 * i + j + 1) * piece)
-                start = base + j * 2 * HD
-                out_ref[h * per_head + i, :, start : start + 2 * HD] = upper[rows]
-                start = base + 4 * HD + j * HD
-                out_ref[h * per_head + i, :, start : start + HD] = lower[rows]
-
-
-def pack(me, inputs, routed):
-    shards, heads, piece, depth = routed.shape
-    width = heads * depth + 6 * HD
+            r = me ^ (h * per_head + i)
+            out_ref[r & 1, (r >> 1) & 3, r >> 3] = product[i * block_rows : (i + 1) * block_rows]
+
+
+def multiply(me, inputs, routed):
+    shards, heads, _, depth = routed.shape
     return pl.pallas_call(
-        pack_kernel,
+        multiply_kernel,
         in_specs=[pl.BlockSpec(memory_space=pltpu.SMEM), VMEM, VMEM],
         out_specs=VMEM,
-        out_shape=jax.ShapeDtypeStruct((shards, piece, width), jnp.bfloat16),
+        out_shape=jax.ShapeDtypeStruct((2, 4, 4, ROWS * heads // shards, 2 * HD), jnp.float32),
         scratch_shapes=[pltpu.VMEM((ROWS, depth), jnp.float32)],
+        compiler_params=pltpu.CompilerParams(vmem_limit_bytes=12 * 1024 * 1024),
         cost_estimate=pl.CostEstimate(
             flops=2 * ROWS * heads * 2 * HD * depth, bytes_accessed=3_000_000, transcendentals=0
         ),
-        compiler_params=pltpu.CompilerParams(vmem_limit_bytes=12 * 1024 * 1024),
-        name="pack",
+        name="multiply",
     )(me, inputs, routed)
+
+
+def reduce_rows(partial):
+    shards = lax.axis_size("shard")
+
+    def send(values, bits):
+        return lax.ppermute(values, "shard", [(i, i ^ bits) for i in range(shards)])
+
+    partial = partial[0] + send(partial[1], 1)
+    partial = partial[0] + (
+        send(partial[1], 1 << 1) + (send(partial[2], 2 << 1) + send(partial[3], 3 << 1))
+    )
+    partial = partial[0] + (
+        send(partial[1], 1 << 3) + (send(partial[2], 2 << 3) + send(partial[3], 3 << 3))
+    )
+    return partial
 
 
 def step(train_weights, section_to_group, hidden, queries, kv_cache, lengths):
@@ -178,14 +185,9 @@
     picked = pick(section_to_group, spread)
     routed = exchange(picked, "section").reshape(shards, KVH, piece_cols, slice_rows)
     me = lax.axis_index("shard").astype(jnp.int32).reshape(1)
-    received = exchange(pack(me, inputs, routed), "shard")
-    base = KVH * slice_rows
-    layer_out = received[:, :, :base].reshape(shards, piece_cols, KVH, slice_rows)
-    layer_out = layer_out.transpose(2, 1, 0, 3).reshape(1, KVH, piece_cols, D)
-    sums = jnp.sum(received[:, :, base:].astype(jnp.float32), axis=0)
-    upper = jnp.concatenate([sums[:, : 2 * HD], sums[:, 2 * HD : 4 * HD]], axis=0)
-    lower = jnp.concatenate([sums[:, 4 * HD : 5 * HD], sums[:, 5 * HD :]], axis=0)
-    fresh = jnp.concatenate([upper[:, :HD] + lower, upper[:, HD:]], axis=1).astype(jnp.bfloat16)
+    received = exchange(routed, "shard")
+    layer_out = received.transpose(1, 2, 0, 3).reshape(1, KVH, piece_cols, D)
+    fresh = reduce_rows(multiply(me, inputs, routed)).astype(jnp.bfloat16)
     block_index = lax.axis_index("shard") % per_head
     row_lengths = lax.dynamic_slice_in_dim(lengths, block_index * row_block, row_block, 0)
     query_rows = queries.reshape(row_block, QPK, HD)

time: 163 us -> 152 us (0.933)
  the two profiles are of different devices: /device:TPU:4 before, /device:TPU:6 now
where the time goes in v5:
time: 152 us; the launch traced here: 151 us
  starting transfers between devices  90.3 us (59%)
  waiting for transfers between devices  47 us (31%)
  local copies, waits for them, and re-layouts  6.05 us (4%)
  Pallas kernels  4.94 us (3%)
    ppermute x14, starting transfers between devices, send(): return lax.ppermute(values, 'shard', [(i, i ^ bits) for i in range(shards)])  62.5 us
    ppermute x14, waiting for transfers between devices, send(): return lax.ppermute(values, 'shard', [(i, i ^ bits) for i in range(shards)])  42.3 us
    all_to_all x3, starting transfers between devices, exchange(): return lax.all_to_all(blocks, axis, split_axis=0, concat_axis=0, tiled=True)  27.8 us
    all_to_all x3, waiting for transfers between devices, exchange(): return lax.all_to_all(blocks, axis, split_axis=0, concat_axis=0, tiled=True)  4.78 us
    unnamed x19, local copies, waits for them, and re-layouts  3.14 us
  transfers between devices with their start and end apart: 17, of which 7 were waited for; matrix products, arithmetic and copies ran while one was open for 2% of the time, Pallas kernels for 3%

profile of v5, /device:TPU:6, one launch (start us, length us, event | category | flops | bytes accessed | tf_op | source)
XLA Modules:
  0.0 151.0 jit_solution(10103169103203688219)
XLA Ops:
  0.6 0.0 copy-start
  0.7 0.1 xor.18
  0.8 0.8 copy-done
  1.5 0.7 gather_fusion
  2.3 3.3 %collective-permute-start = (bf16[4,4,4,512]{3,2,0,1:T(4,128)(2,1)S(1)}, bf16[4,4,4,512]{3,2,0,1:T(4,128)(2,1)S(1)}, u32[]{:S(2)}, u32[]{:S(2)}) collective-permute-start(bf16[4,4,4,512]{3,2,0,1:T(4,128)(2,1)S(1)} %copy.18), channel_id=1, source_target_pairs={{0,1},{1,0},{2,3},{3,2},{4,5},{5,4},{6,7},{7,6},{8,9},{9,8},{10,11... | collective-permute-start | bytes 196616 | tf_op jit(solution)/shard_map/ppermute | solution.py:28
  5.6 0.0 copy-start.1
  5.6 1.6 %copy-done.1 = f32[1,512,1024]{2,1,0:T(8,128)S(1)} copy-done((f32[1,512,1024]{2,1,0:T(8,128)S(1)}, f32[1,512,1024]{2,1,0:T(8,128)}, u32[]{:S(2)}) %copy-start.1) | copy-done | bytes 2097176
  7.2 1.5 %flip.1 = bf16[32,4,8,512]{3,2,1,0:T(8,128)(2,1)} custom-call(f32[1,512,1024]{2,1,0:T(8,128)S(1)} %copy-done.1), custom_call_target="tpu_custom_call" | custom-call | flops 2000000 | bytes 3000000 | tf_op jit(solution)/shard_map/flip/pallas_call | solution.py:89
  8.7 8.9 %all-to-all-start = ((bf16[16,64,512]{2,1,0:T(8,128)(2,1)}), bf16[16,64,512]{2,1,0:T(8,128)(2,1)S(1)}, u32[]{:S(2)}, u32[]{:S(2)}) async-start(bf16[16,64,512]{2,1,0:T(8,128)(2,1)} %bitcast.27), calls=%async_computation | async-start | bytes 2097152 | tf_op jit(solution)/shard_map/all_to_all | solution.py:20
  17.6 0.0 collective-permute-done
  17.7 1.9 %collective-permute-start.1 = (bf16[2,4,4,512]{3,2,0,1:T(4,128)(2,1)S(1)}, bf16[2,4,4,512]{3,2,0,1:T(4,128)(2,1)S(1)}, u32[]{:S(2)}, u32[]{:S(2)}) collective-permute-start(bf16[2,4,4,512]{3,2,0,1:T(4,128)(2,1)S(1)} %pad_maximum_fusion), channel_id=1, source_target_pairs={{0,2},{1,3},{2,0},{3,1},{4,6},{5,7},{6,4},{7,5},{8,10},{9,11},{10,... | collective-permute-start | bytes 98312 | tf_op jit(solution)/shard_map/ppermute | solution.py:28
  19.7 4.3 %collective-permute-start.2 = (bf16[2,4,4,512]{3,2,1,0:T(4,128)(2,1)S(1)}, bf16[2,4,4,512]{3,2,1,0:T(4,128)(2,1)S(1)}, u32[]{:S(2)}, u32[]{:S(2)}) collective-permute-start(bf16[2,4,4,512]{3,2,1,0:T(4,128)(2,1)S(1)} %pad_maximum_fusion.1), channel_id=1, source_target_pairs={{0,4},{1,5},{2,6},{3,7},{4,0},{5,1},{6,2},{7,3},{8,12},{9,13},{10,... | collective-permute-start | bytes 98312 | tf_op jit(solution)/shard_map/ppermute | solution.py:28
  24.0 3.9 %collective-permute-start.3 = (bf16[2,4,4,512]{3,2,0,1:T(4,128)(2,1)S(1)}, bf16[2,4,4,512]{3,2,0,1:T(4,128)(2,1)S(1)}, u32[]{:S(2)}, u32[]{:S(2)}) collective-permute-start(bf16[2,4,4,512]{3,2,0,1:T(4,128)(2,1)S(1)} %pad_maximum_fusion.2), channel_id=1, source_target_pairs={{0,6},{1,7},{2,4},{3,5},{4,2},{5,3},{6,0},{7,1},{8,14},{9,15},{10,... | collective-permute-start | bytes 98312 | tf_op jit(solution)/shard_map/ppermute | solution.py:28
  28.0 4.8 %all-to-all-done.spread_ref = bf16[16,64,512]{2,1,0:T(8,128)(2,1)S(1)} async-done(((bf16[16,64,512]{2,1,0:T(8,128)(2,1)}), bf16[16,64,512]{2,1,0:T(8,128)(2,1)S(1)}, u32[]{:S(2)}, u32[]{:S(2)}) %all-to-all-start) | async-done | bytes 1048608 | tf_op jit(solution)/shard_map/all_to_all | solution.py:20
  32.8 1.7 %pick.1 = bf16[16,64,512]{2,1,0:T(8,128)(2,1)} custom-call(s32[16]{0:T(128)S(1)} %copy-done.2, bf16[16,64,512]{2,1,0:T(8,128)(2,1)S(1)} %all-to-all-done.spread_ref), custom_call_target="tpu_custom_call" | custom-call | flops 1000000 | bytes 2000000 | tf_op jit(solution)/shard_map/pick/pallas_call | solution.py:110
  34.4 5.6 %all-to-all-start.1 = ((bf16[16,64,512]{2,1,0:T(8,128)(2,1)}), bf16[16,64,512]{2,1,0:T(8,128)(2,1)}, u32[]{:S(2)}, u32[]{:S(2)}) async-start(bf16[16,64,512]{2,1,0:T(8,128)(2,1)} %pick.1), calls=%async_computation.1 | async-start | bytes 2097152 | tf_op jit(solution)/shard_map/all_to_all | solution.py:20
  40.2 6.2 %collective-permute-start.4 = (bf16[4,2,4,512]{3,2,1,0:T(4,128)(2,1)S(1)}, bf16[4,2,4,512]{3,2,1,0:T(4,128)(2,1)S(1)}, u32[]{:S(2)}, u32[]{:S(2)}) collective-permute-start(bf16[4,2,4,512]{3,2,1,0:T(4,128)(2,1)S(1)} %pad_maximum_fusion.3), channel_id=1, source_target_pairs={{0,8},{1,9},{2,10},{3,11},{4,12},{5,13},{6,14},{7,15},{8,0},{9,1},... | collective-permute-start | bytes 98312 | tf_op jit(solution)/shard_map/ppermute | solution.py:28
  46.4 10.9 %collective-permute-start.5 = (bf16[4,2,4,512]{3,2,1,0:T(4,128)(2,1)S(1)}, bf16[4,2,4,512]{3,2,1,0:T(4,128)(2,1)S(1)}, u32[]{:S(2)}, u32[]{:S(2)}) collective-permute-start(bf16[4,2,4,512]{3,2,1,0:T(4,128)(2,1)S(1)} %pad_maximum_fusion.4), channel_id=1, source_target_pairs={{0,16},{1,17},{2,18},{3,19},{4,20},{5,21},{6,22},{7,23},{8,24},{9,... | collective-permute-start | bytes 98312 | tf_op jit(solution)/shard_map/ppermute | solution.py:28
  57.4 1.9 %collective-permute-start.6 = (bf16[4,2,4,512]{3,2,1,0:T(4,128)(2,1)S(1)}, bf16[4,2,4,512]{3,2,1,0:T(4,128)(2,1)S(1)}, u32[]{:S(2)}, u32[]{:S(2)}) collective-permute-start(bf16[4,2,4,512]{3,2,1,0:T(4,128)(2,1)S(1)} %pad_maximum_fusion.5), channel_id=1, source_target_pairs={{0,24},{1,25},{2,26},{3,27},{4,28},{5,29},{6,30},{7,31},{8,16},{9,... | collective-permute-start | bytes 98312 | tf_op jit(solution)/shard_map/ppermute | solution.py:28
  59.3 0.0 all-to-all-done.1
  59.4 0.0 copy-start.5
  59.4 13.3 %all-to-all-start.2 = ((bf16[32,4,8,512]{3,2,1,0:T(8,128)(2,1)}), bf16[32,4,8,512]{3,2,1,0:T(8,128)(2,1)S(1)}, u32[]{:S(2)}, u32[]{:S(2)}) async-start(bf16[32,4,8,512]{3,2,1,0:T(8,128)(2,1)} %bitcast.28.routed_ref), calls=%async_computation.2 | async-start | bytes 2097152 | tf_op jit(solution)/shard_map/all_to_all | solution.py:20
  72.7 0.0 copy-start.4
  72.7 0.0 copy-start.3
  72.7 0.0 collective-permute-done.4
  72.9 1.8 %multiply.23 = f32[2,4,4,16,256]{4,3,2,1,0:T(8,128)S(1)} custom-call(s32[1]{0:T(128)} %bitcast.me_ref, bf16[32,4,512]{2,1,0:T(4,128)(2,1)S(1)} %bitcast.108, bf16[32,4,8,512]{3,2,1,0:T(8,128)(2,1)} %bitcast.28.routed_ref), custom_call_target="tpu_custom_call" | custom-call | flops 134217728 | bytes 3000000 | tf_op jit(solution)/shard_map/multiply/pallas_call | solution.py:144
  74.7 2.1 %collective-permute-start.7 = (f32[4,4,16,256]{3,2,1,0:T(8,128)S(1)}, f32[4,4,16,256]{3,2,1,0:T(8,128)S(1)}, u32[]{:S(2)}, u32[]{:S(2)}) collective-permute-start(f32[4,4,16,256]{3,2,1,0:T(8,128)S(1)} %slice_bitcast_fusion), channel_id=1, source_target_pairs={{0,1},{1,0},{2,3},{3,2},{4,5},{5,4},{6,7},{7,6},{8,9},{9,8},{10,11... | collective-permute-start | bytes 786440 | tf_op jit(solution)/shard_map/ppermute | solution.py:162
  76.8 0.1 dynamic_slice.3
  76.9 9.4 %collective-permute-done.7 = f32[4,4,16,256]{3,2,1,0:T(8,128)S(1)} collective-permute-done((f32[4,4,16,256]{3,2,1,0:T(8,128)S(1)}, f32[4,4,16,256]{3,2,1,0:T(8,128)S(1)}, u32[]{:S(2)}, u32[]{:S(2)}) %collective-permute-start.7) | collective-permute-done | bytes 262176 | tf_op jit(solution)/shard_map/ppermute | solution.py:162
  86.4 6.4 %collective-permute-start.10 = (f32[4,16,256]{2,1,0:T(8,128)S(1)}, f32[4,16,256]{2,1,0:T(8,128)S(1)}, u32[]{:S(2)}, u32[]{:S(2)}) collective-permute-start(f32[4,16,256]{2,1,0:T(8,128)S(1)} %get-tuple-element.2), channel_id=1, source_target_pairs={{0,6},{1,7},{2,4},{3,5},{4,2},{5,3},{6,0},{7,1},{8,14},{9,15},{10,... | collective-permute-start | bytes 196616 | tf_op jit(solution)/shard_map/ppermute | solution.py:162
  92.8 1.9 %collective-permute-start.8 = (f32[4,16,256]{2,1,0:T(8,128)S(1)}, f32[4,16,256]{2,1,0:T(8,128)S(1)}, u32[]{:S(2)}, u32[]{:S(2)}) collective-permute-start(f32[4,16,256]{2,1,0:T(8,128)S(1)} %get-tuple-element.4), channel_id=1, source_target_pairs={{0,2},{1,3},{2,0},{3,1},{4,6},{5,7},{6,4},{7,5},{8,10},{9,11},{10,... | collective-permute-start | bytes 196616 | tf_op jit(solution)/shard_map/ppermute | solution.py:162
  94.7 2.5 %collective-permute-start.9 = (f32[4,16,256]{2,1,0:T(8,128)S(1)}, f32[4,16,256]{2,1,0:T(8,128)S(1)}, u32[]{:S(2)}, u32[]{:S(2)}) collective-permute-start(f32[4,16,256]{2,1,0:T(8,128)S(1)} %get-tuple-element.3), channel_id=1, source_target_pairs={{0,4},{1,5},{2,6},{3,7},{4,0},{5,1},{6,2},{7,3},{8,12},{9,13},{10,... | collective-permute-start | bytes 196616 | tf_op jit(solution)/shard_map/ppermute | solution.py:162
  97.2 0.1 iota_compare_fusion
  97.3 24.2 %collective-permute-done.10 = f32[4,16,256]{2,1,0:T(8,128)S(1)} collective-permute-done((f32[4,16,256]{2,1,0:T(8,128)S(1)}, f32[4,16,256]{2,1,0:T(8,128)S(1)}, u32[]{:S(2)}, u32[]{:S(2)}) %collective-permute-start.10) | collective-permute-done | bytes 65568 | tf_op jit(solution)/shard_map/ppermute | solution.py:162
  121.5 0.2 collective-permute-done.8
  121.7 3.2 %collective-permute-done.9 = f32[4,16,256]{2,1,0:T(8,128)S(1)} collective-permute-done((f32[4,16,256]{2,1,0:T(8,128)S(1)}, f32[4,16,256]{2,1,0:T(8,128)S(1)}, u32[]{:S(2)}, u32[]{:S(2)}) %collective-permute-start.9) | collective-permute-done | bytes 65568 | tf_op jit(solution)/shard_map/ppermute | solution.py:162
  124.9 7.7 %collective-permute-start.11 = (f32[16,256]{1,0:T(8,128)S(1)}, f32[16,256]{1,0:T(8,128)S(1)}, u32[]{:S(2)}, u32[]{:S(2)}) collective-permute-start(f32[16,256]{1,0:T(8,128)S(1)} %get-tuple-element.11), channel_id=1, source_target_pairs={{0,8},{1,9},{2,10},{3,11},{4,12},{5,13},{6,14},{7,15},{8,0},{9,1},... | collective-permute-start | bytes 49160 | tf_op jit(solution)/shard_map/ppermute | solution.py:162
  132.7 5.5 %collective-permute-start.12 = (f32[16,256]{1,0:T(8,128)S(1)}, f32[16,256]{1,0:T(8,128)S(1)}, u32[]{:S(2)}, u32[]{:S(2)}) collective-permute-start(f32[16,256]{1,0:T(8,128)S(1)} %get-tuple-element.10), channel_id=1, source_target_pairs={{0,16},{1,17},{2,18},{3,19},{4,20},{5,21},{6,22},{7,23},{8,24},{9,... | collective-permute-start | bytes 49160 | tf_op jit(solution)/shard_map/ppermute | solution.py:162
  138.2 3.8 %collective-permute-start.13 = (f32[16,256]{1,0:T(8,128)S(1)}, f32[16,256]{1,0:T(8,128)S(1)}, u32[]{:S(2)}, u32[]{:S(2)}) collective-permute-start(f32[16,256]{1,0:T(8,128)S(1)} %get-tuple-element.9), channel_id=1, source_target_pairs={{0,24},{1,25},{2,26},{3,27},{4,28},{5,29},{6,30},{7,31},{8,16},{9,... | collective-permute-start | bytes 49160 | tf_op jit(solution)/shard_map/ppermute | solution.py:162
  142.0 0.5 fusion.26
  142.4 4.7 %collective-permute-done.12 = f32[16,256]{1,0:T(8,128)S(1)} collective-permute-done((f32[16,256]{1,0:T(8,128)S(1)}, f32[16,256]{1,0:T(8,128)S(1)}, u32[]{:S(2)}, u32[]{:S(2)}) %collective-permute-start.12) | collective-permute-done | bytes 16416 | tf_op jit(solution)/shard_map/ppermute | solution.py:162
  147.1 0.6 collective-permute-done.13
  147.7 0.1 fusion.17
  147.9 0.2 fusion.5
  148.1 0.3 fusion.1
  148.4 0.7 copy.34
  149.1 0.6 copy.23
  149.7 1.3 reshape.143
  (46 shorter events, 0.6 us)
Async XLA Ops:
  0.6 0.9 copy-start
  2.3 15.4 %collective-permute-start = (bf16[4,4,4,512]{3,2,0,1:T(4,128)(2,1)S(1)}, bf16[4,4,4,512]{3,2,0,1:T(4,128)(2,1)S(1)}, u32[]{:S(2)}, u32[]{:S(2)}) collective-permute-start(bf16[4,4,4,512]{3,2,0,1:T(4,128)(2,1)S(1)} %copy.18), channel_id=1, source_target_pairs={{0,1},{1,0},{2,3},{3,2},{4,5},{5,4},{6,7},{7,6},{8,9},{9,8},{10,11... | collective-permute-start | bytes 196616 | tf_op jit(solution)/shard_map/ppermute | solution.py:28
  5.6 1.6 %copy-start.1 = (f32[1,512,1024]{2,1,0:T(8,128)S(1)}, f32[1,512,1024]{2,1,0:T(8,128)}, u32[]{:S(2)}) copy-start(f32[1,512,1024]{2,1,0:T(8,128)} %weights_ref.1) | copy-start | bytes 6291460
  8.7 24.1 %copy-start.2 = (s32[16]{0:T(128)S(1)}, s32[16]{0:T(128)}, u32[]{:S(2)}) copy-start(s32[16]{0:T(128)} %group_ref.1) | copy-start | bytes 196
  8.7 24.1 %all-to-all-start = ((bf16[16,64,512]{2,1,0:T(8,128)(2,1)}), bf16[16,64,512]{2,1,0:T(8,128)(2,1)S(1)}, u32[]{:S(2)}, u32[]{:S(2)}) async-start(bf16[16,64,512]{2,1,0:T(8,128)(2,1)} %bitcast.27), calls=%async_computation | async-start | bytes 2097152 | tf_op jit(solution)/shard_map/all_to_all | solution.py:20
  17.7 10.3 %collective-permute-start.1 = (bf16[2,4,4,512]{3,2,0,1:T(4,128)(2,1)S(1)}, bf16[2,4,4,512]{3,2,0,1:T(4,128)(2,1)S(1)}, u32[]{:S(2)}, u32[]{:S(2)}) collective-permute-start(bf16[2,4,4,512]{3,2,0,1:T(4,128)(2,1)S(1)} %pad_maximum_fusion), channel_id=1, source_target_pairs={{0,2},{1,3},{2,0},{3,1},{4,6},{5,7},{6,4},{7,5},{8,10},{9,11},{10,... | collective-permute-start | bytes 98312 | tf_op jit(solution)/shard_map/ppermute | solution.py:28
  19.7 20.4 %collective-permute-start.2 = (bf16[2,4,4,512]{3,2,1,0:T(4,128)(2,1)S(1)}, bf16[2,4,4,512]{3,2,1,0:T(4,128)(2,1)S(1)}, u32[]{:S(2)}, u32[]{:S(2)}) collective-permute-start(bf16[2,4,4,512]{3,2,1,0:T(4,128)(2,1)S(1)} %pad_maximum_fusion.1), channel_id=1, source_target_pairs={{0,4},{1,5},{2,6},{3,7},{4,0},{5,1},{6,2},{7,3},{8,12},{9,13},{10,... | collective-permute-start | bytes 98312 | tf_op jit(solution)/shard_map/ppermute | solution.py:28
  24.0 16.0 %collective-permute-start.3 = (bf16[2,4,4,512]{3,2,0,1:T(4,128)(2,1)S(1)}, bf16[2,4,4,512]{3,2,0,1:T(4,128)(2,1)S(1)}, u32[]{:S(2)}, u32[]{:S(2)}) collective-permute-start(bf16[2,4,4,512]{3,2,0,1:T(4,128)(2,1)S(1)} %pad_maximum_fusion.2), channel_id=1, source_target_pairs={{0,6},{1,7},{2,4},{3,5},{4,2},{5,3},{6,0},{7,1},{8,14},{9,15},{10,... | collective-permute-start | bytes 98312 | tf_op jit(solution)/shard_map/ppermute | solution.py:28
  34.4 24.9 %all-to-all-start.1 = ((bf16[16,64,512]{2,1,0:T(8,128)(2,1)}), bf16[16,64,512]{2,1,0:T(8,128)(2,1)}, u32[]{:S(2)}, u32[]{:S(2)}) async-start(bf16[16,64,512]{2,1,0:T(8,128)(2,1)} %pick.1), calls=%async_computation.1 | async-start | bytes 2097152 | tf_op jit(solution)/shard_map/all_to_all | solution.py:20
  40.2 32.6 %collective-permute-start.4 = (bf16[4,2,4,512]{3,2,1,0:T(4,128)(2,1)S(1)}, bf16[4,2,4,512]{3,2,1,0:T(4,128)(2,1)S(1)}, u32[]{:S(2)}, u32[]{:S(2)}) collective-permute-start(bf16[4,2,4,512]{3,2,1,0:T(4,128)(2,1)S(1)} %pad_maximum_fusion.3), channel_id=1, source_target_pairs={{0,8},{1,9},{2,10},{3,11},{4,12},{5,13},{6,14},{7,15},{8,0},{9,1},... | collective-permute-start | bytes 98312 | tf_op jit(solution)/shard_map/ppermute | solution.py:28
  46.4 26.3 %collective-permute-start.5 = (bf16[4,2,4,512]{3,2,1,0:T(4,128)(2,1)S(1)}, bf16[4,2,4,512]{3,2,1,0:T(4,128)(2,1)S(1)}, u32[]{:S(2)}, u32[]{:S(2)}) collective-permute-start(bf16[4,2,4,512]{3,2,1,0:T(4,128)(2,1)S(1)} %pad_maximum_fusion.4), channel_id=1, source_target_pairs={{0,16},{1,17},{2,18},{3,19},{4,20},{5,21},{6,22},{7,23},{8,24},{9,... | collective-permute-start | bytes 98312 | tf_op jit(solution)/shard_map/ppermute | solution.py:28
  57.4 15.4 %collective-permute-start.6 = (bf16[4,2,4,512]{3,2,1,0:T(4,128)(2,1)S(1)}, bf16[4,2,4,512]{3,2,1,0:T(4,128)(2,1)S(1)}, u32[]{:S(2)}, u32[]{:S(2)}) collective-permute-start(bf16[4,2,4,512]{3,2,1,0:T(4,128)(2,1)S(1)} %pad_maximum_fusion.5), channel_id=1, source_target_pairs={{0,24},{1,25},{2,26},{3,27},{4,28},{5,29},{6,30},{7,31},{8,16},{9,... | collective-permute-start | bytes 98312 | tf_op jit(solution)/shard_map/ppermute | solution.py:28
  59.4 17.5 %copy-start.5 = (s32[128]{0:T(128)S(1)}, s32[128]{0:T(128)}, u32[]{:S(2)}) copy-start(s32[128]{0:T(128)} %param.11) | copy-start | bytes 1540
  59.4 89.7 %all-to-all-start.2 = ((bf16[32,4,8,512]{3,2,1,0:T(8,128)(2,1)}), bf16[32,4,8,512]{3,2,1,0:T(8,128)(2,1)S(1)}, u32[]{:S(2)}, u32[]{:S(2)}) async-start(bf16[32,4,8,512]{3,2,1,0:T(8,128)(2,1)} %bitcast.28.routed_ref), calls=%async_computation.2 | async-start | bytes 2097152 | tf_op jit(solution)/shard_map/all_to_all | solution.py:20
  72.7 24.6 %copy-start.4 = (bf16[16,2048]{1,0:T(8,128)(2,1)S(1)}, bf16[16,2048]{1,0:T(8,128)(2,1)}, u32[]{:S(2)}) copy-start(bf16[16,2048]{1,0:T(8,128)(2,1)} %param.9) | copy-start | bytes 196612
  72.7 69.2 %copy-start.3 = (bf16[16,128,256]{2,1,0:T(8,128)(2,1)S(1)}, bf16[16,128,256]{2,1,0:T(8,128)(2,1)}, u32[]{:S(2)}) copy-start(bf16[16,128,256]{2,1,0:T(8,128)(2,1)} %param.10) | copy-start | bytes 3145732
  74.7 11.7 %collective-permute-start.7 = (f32[4,4,16,256]{3,2,1,0:T(8,128)S(1)}, f32[4,4,16,256]{3,2,1,0:T(8,128)S(1)}, u32[]{:S(2)}, u32[]{:S(2)}) collective-permute-start(f32[4,4,16,256]{3,2,1,0:T(8,128)S(1)} %slice_bitcast_fusion), channel_id=1, source_target_pairs={{0,1},{1,0},{2,3},{3,2},{4,5},{5,4},{6,7},{7,6},{8,9},{9,8},{10,11... | collective-permute-start | bytes 786440 | tf_op jit(solution)/shard_map/ppermute | solution.py:162
  86.4 35.1 %collective-permute-start.10 = (f32[4,16,256]{2,1,0:T(8,128)S(1)}, f32[4,16,256]{2,1,0:T(8,128)S(1)}, u32[]{:S(2)}, u32[]{:S(2)}) collective-permute-start(f32[4,16,256]{2,1,0:T(8,128)S(1)} %get-tuple-element.2), channel_id=1, source_target_pairs={{0,6},{1,7},{2,4},{3,5},{4,2},{5,3},{6,0},{7,1},{8,14},{9,15},{10,... | collective-permute-start | bytes 196616 | tf_op jit(solution)/shard_map/ppermute | solution.py:162
  92.8 28.9 %collective-permute-start.8 = (f32[4,16,256]{2,1,0:T(8,128)S(1)}, f32[4,16,256]{2,1,0:T(8,128)S(1)}, u32[]{:S(2)}, u32[]{:S(2)}) collective-permute-start(f32[4,16,256]{2,1,0:T(8,128)S(1)} %get-tuple-element.4), channel_id=1, source_target_pairs={{0,2},{1,3},{2,0},{3,1},{4,6},{5,7},{6,4},{7,5},{8,10},{9,11},{10,... | collective-permute-start | bytes 196616 | tf_op jit(solution)/shard_map/ppermute | solution.py:162
  94.7 30.1 %collective-permute-start.9 = (f32[4,16,256]{2,1,0:T(8,128)S(1)}, f32[4,16,256]{2,1,0:T(8,128)S(1)}, u32[]{:S(2)}, u32[]{:S(2)}) collective-permute-start(f32[4,16,256]{2,1,0:T(8,128)S(1)} %get-tuple-element.3), channel_id=1, source_target_pairs={{0,4},{1,5},{2,6},{3,7},{4,0},{5,1},{6,2},{7,3},{8,12},{9,13},{10,... | collective-permute-start | bytes 196616 | tf_op jit(solution)/shard_map/ppermute | solution.py:162
  124.9 17.5 %collective-permute-start.11 = (f32[16,256]{1,0:T(8,128)S(1)}, f32[16,256]{1,0:T(8,128)S(1)}, u32[]{:S(2)}, u32[]{:S(2)}) collective-permute-start(f32[16,256]{1,0:T(8,128)S(1)} %get-tuple-element.11), channel_id=1, source_target_pairs={{0,8},{1,9},{2,10},{3,11},{4,12},{5,13},{6,14},{7,15},{8,0},{9,1},... | collective-permute-start | bytes 49160 | tf_op jit(solution)/shard_map/ppermute | solution.py:162
  132.7 14.5 %collective-permute-start.12 = (f32[16,256]{1,0:T(8,128)S(1)}, f32[16,256]{1,0:T(8,128)S(1)}, u32[]{:S(2)}, u32[]{:S(2)}) collective-permute-start(f32[16,256]{1,0:T(8,128)S(1)} %get-tuple-element.10), channel_id=1, source_target_pairs={{0,16},{1,17},{2,18},{3,19},{4,20},{5,21},{6,22},{7,23},{8,24},{9,... | collective-permute-start | bytes 49160 | tf_op jit(solution)/shard_map/ppermute | solution.py:162
  138.2 9.5 %collective-permute-start.13 = (f32[16,256]{1,0:T(8,128)S(1)}, f32[16,256]{1,0:T(8,128)S(1)}, u32[]{:S(2)}, u32[]{:S(2)}) collective-permute-start(f32[16,256]{1,0:T(8,128)S(1)} %get-tuple-element.9), channel_id=1, source_target_pairs={{0,24},{1,25},{2,26},{3,27},{4,28},{5,29},{6,30},{7,31},{8,16},{9,... | collective-permute-start | bytes 49160 | tf_op jit(solution)/shard_map/ppermute | solution.py:162

commit v6 on v5

--- a/solution.py
+++ b/solution.py
@@ -136,7 +136,7 @@
         )
         for i in range(per_head):
             r = me ^ (h * per_head + i)
-            out_ref[r & 1, (r >> 1) & 3, r >> 3] = product[i * block_rows : (i + 1) * block_rows]
+            out_ref[r & 1, r >> 2, (r >> 1) & 1] = product[i * block_rows : (i + 1) * block_rows]
 
 
 def multiply(me, inputs, routed):
@@ -145,7 +145,7 @@
         multiply_kernel,
         in_specs=[pl.BlockSpec(memory_space=pltpu.SMEM), VMEM, VMEM],
         out_specs=VMEM,
-        out_shape=jax.ShapeDtypeStruct((2, 4, 4, ROWS * heads // shards, 2 * HD), jnp.float32),
+        out_shape=jax.ShapeDtypeStruct((2, 8, 2, ROWS * heads // shards, 2 * HD), jnp.float32),
         scratch_shapes=[pltpu.VMEM((ROWS, depth), jnp.float32)],
         compiler_params=pltpu.CompilerParams(vmem_limit_bytes=12 * 1024 * 1024),
         cost_estimate=pl.CostEstimate(
@@ -162,12 +162,9 @@
         return lax.ppermute(values, "shard", [(i, i ^ bits) for i in range(shards)])
 
     partial = partial[0] + send(partial[1], 1)
-    partial = partial[0] + (
-        send(partial[1], 1 << 1) + (send(partial[2], 2 << 1) + send(partial[3], 3 << 1))
-    )
-    partial = partial[0] + (
-        send(partial[1], 1 << 3) + (send(partial[2], 2 << 3) + send(partial[3], 3 << 3))
-    )
+    arrived = [send(partial[k], k << 2) for k in range(1, 8)]
+    partial = sum(arrived, partial[0])
+    partial = partial[0] + send(partial[1], 1 << 1)
     return partial
 
 

time: 152 us -> 154 us (1.013)
  the two profiles are of different devices: /device:TPU:6 before, /device:TPU:40 now
where the time goes in v6:
time: 154 us; the launch traced here: 153 us
  starting transfers between devices  108 us (70%)
  waiting for transfers between devices  31.1 us (20%)
  local copies, waits for them, and re-layouts  6.05 us (4%)
  Pallas kernels  4.95 us (3%)
    ppermute x16, starting transfers between devices, send(): return lax.ppermute(values, 'shard', [(i, i ^ bits) for i in range(shards)])  83.2 us
    ppermute x16, waiting for transfers between devices, send(): return lax.ppermute(values, 'shard', [(i, i ^ bits) for i in range(shards)])  27.5 us
    all_to_all x3, starting transfers between devices, exchange(): return lax.all_to_all(blocks, axis, split_axis=0, concat_axis=0, tiled=True)  25.2 us
    all_to_all x3, waiting for transfers between devices, exchange(): return lax.all_to_all(blocks, axis, split_axis=0, concat_axis=0, tiled=True)  3.55 us
    unnamed x19, local copies, waits for them, and re-layouts  3.14 us
  transfers between devices with their start and end apart: 19, of which 6 were waited for; matrix products, arithmetic and copies ran while one was open for 2% of the time, Pallas kernels for 3%

profile of v6, /device:TPU:40, one launch (start us, length us, event | category | flops | bytes accessed | tf_op | source)
XLA Modules:
  0.0 153.2 jit_solution(3177566735687000158)
XLA Ops:
  0.6 0.0 copy-start
  0.7 0.1 xor.18
  0.8 0.8 copy-done
  1.5 0.7 gather_fusion
  2.3 4.9 %collective-permute-start = (bf16[4,4,4,512]{3,2,0,1:T(4,128)(2,1)S(1)}, bf16[4,4,4,512]{3,2,0,1:T(4,128)(2,1)S(1)}, u32[]{:S(2)}, u32[]{:S(2)}) collective-permute-start(bf16[4,4,4,512]{3,2,0,1:T(4,128)(2,1)S(1)} %copy.18), channel_id=1, source_target_pairs={{0,1},{1,0},{2,3},{3,2},{4,5},{5,4},{6,7},{7,6},{8,9},{9,8},{10,11... | collective-permute-start | bytes 196616 | tf_op jit(solution)/shard_map/ppermute | solution.py:28
  7.2 0.0 copy-start.1
  7.2 1.6 %copy-done.1 = f32[1,512,1024]{2,1,0:T(8,128)S(1)} copy-done((f32[1,512,1024]{2,1,0:T(8,128)S(1)}, f32[1,512,1024]{2,1,0:T(8,128)}, u32[]{:S(2)}) %copy-start.1) | copy-done | bytes 2097176
  8.8 1.5 flip.1
  10.3 5.1 %all-to-all-start = ((bf16[16,64,512]{2,1,0:T(8,128)(2,1)}), bf16[16,64,512]{2,1,0:T(8,128)(2,1)S(1)}, u32[]{:S(2)}, u32[]{:S(2)}) async-start(bf16[16,64,512]{2,1,0:T(8,128)(2,1)} %bitcast.27), calls=%async_computation | async-start | bytes 2097152 | tf_op jit(solution)/shard_map/all_to_all | solution.py:20
  15.5 3.3 %collective-permute-start.1 = (bf16[2,4,4,512]{3,2,0,1:T(4,128)(2,1)S(1)}, bf16[2,4,4,512]{3,2,0,1:T(4,128)(2,1)S(1)}, u32[]{:S(2)}, u32[]{:S(2)}) collective-permute-start(bf16[2,4,4,512]{3,2,0,1:T(4,128)(2,1)S(1)} %pad_maximum_fusion), channel_id=1, source_target_pairs={{0,2},{1,3},{2,0},{3,1},{4,6},{5,7},{6,4},{7,5},{8,10},{9,11},{10,... | collective-permute-start | bytes 98312 | tf_op jit(solution)/shard_map/ppermute | solution.py:28
  18.9 3.9 %collective-permute-start.2 = (bf16[2,4,4,512]{3,2,1,0:T(4,128)(2,1)S(1)}, bf16[2,4,4,512]{3,2,1,0:T(4,128)(2,1)S(1)}, u32[]{:S(2)}, u32[]{:S(2)}) collective-permute-start(bf16[2,4,4,512]{3,2,1,0:T(4,128)(2,1)S(1)} %pad_maximum_fusion.1), channel_id=1, source_target_pairs={{0,4},{1,5},{2,6},{3,7},{4,0},{5,1},{6,2},{7,3},{8,12},{9,13},{10,... | collective-permute-start | bytes 98312 | tf_op jit(solution)/shard_map/ppermute | solution.py:28
  22.9 2.4 %collective-permute-start.3 = (bf16[2,4,4,512]{3,2,0,1:T(4,128)(2,1)S(1)}, bf16[2,4,4,512]{3,2,0,1:T(4,128)(2,1)S(1)}, u32[]{:S(2)}, u32[]{:S(2)}) collective-permute-start(bf16[2,4,4,512]{3,2,0,1:T(4,128)(2,1)S(1)} %pad_maximum_fusion.2), channel_id=1, source_target_pairs={{0,6},{1,7},{2,4},{3,5},{4,2},{5,3},{6,0},{7,1},{8,14},{9,15},{10,... | collective-permute-start | bytes 98312 | tf_op jit(solution)/shard_map/ppermute | solution.py:28
  25.3 3.5 %all-to-all-done.spread_ref = bf16[16,64,512]{2,1,0:T(8,128)(2,1)S(1)} async-done(((bf16[16,64,512]{2,1,0:T(8,128)(2,1)}), bf16[16,64,512]{2,1,0:T(8,128)(2,1)S(1)}, u32[]{:S(2)}, u32[]{:S(2)}) %all-to-all-start) | async-done | bytes 1048608 | tf_op jit(solution)/shard_map/all_to_all | solution.py:20
  28.8 1.7 %pick.1 = bf16[16,64,512]{2,1,0:T(8,128)(2,1)} custom-call(s32[16]{0:T(128)S(1)} %copy-done.2, bf16[16,64,512]{2,1,0:T(8,128)(2,1)S(1)} %all-to-all-done.spread_ref), custom_call_target="tpu_custom_call" | custom-call | flops 1000000 | bytes 2000000 | tf_op jit(solution)/shard_map/pick/pallas_call | solution.py:110
  30.5 7.3 %all-to-all-start.1 = ((bf16[16,64,512]{2,1,0:T(8,128)(2,1)}), bf16[16,64,512]{2,1,0:T(8,128)(2,1)}, u32[]{:S(2)}, u32[]{:S(2)}) async-start(bf16[16,64,512]{2,1,0:T(8,128)(2,1)} %pick.1), calls=%async_computation.1 | async-start | bytes 2097152 | tf_op jit(solution)/shard_map/all_to_all | solution.py:20
  37.8 0.0 collective-permute-done.2
  37.8 0.0 collective-permute-done.3
  37.9 9.1 %collective-permute-start.4 = (bf16[4,2,4,512]{3,2,1,0:T(4,128)(2,1)S(1)}, bf16[4,2,4,512]{3,2,1,0:T(4,128)(2,1)S(1)}, u32[]{:S(2)}, u32[]{:S(2)}) collective-permute-start(bf16[4,2,4,512]{3,2,1,0:T(4,128)(2,1)S(1)} %pad_maximum_fusion.3), channel_id=1, source_target_pairs={{0,8},{1,9},{2,10},{3,11},{4,12},{5,13},{6,14},{7,15},{8,0},{9,1},... | collective-permute-start | bytes 98312 | tf_op jit(solution)/shard_map/ppermute | solution.py:28
  47.0 10.0 %collective-permute-start.5 = (bf16[4,2,4,512]{3,2,1,0:T(4,128)(2,1)S(1)}, bf16[4,2,4,512]{3,2,1,0:T(4,128)(2,1)S(1)}, u32[]{:S(2)}, u32[]{:S(2)}) collective-permute-start(bf16[4,2,4,512]{3,2,1,0:T(4,128)(2,1)S(1)} %pad_maximum_fusion.4), channel_id=1, source_target_pairs={{0,16},{1,17},{2,18},{3,19},{4,20},{5,21},{6,22},{7,23},{8,24},{9,... | collective-permute-start | bytes 98312 | tf_op jit(solution)/shard_map/ppermute | solution.py:28
  57.1 1.9 %collective-permute-start.6 = (bf16[4,2,4,512]{3,2,1,0:T(4,128)(2,1)S(1)}, bf16[4,2,4,512]{3,2,1,0:T(4,128)(2,1)S(1)}, u32[]{:S(2)}, u32[]{:S(2)}) collective-permute-start(bf16[4,2,4,512]{3,2,1,0:T(4,128)(2,1)S(1)} %pad_maximum_fusion.5), channel_id=1, source_target_pairs={{0,24},{1,25},{2,26},{3,27},{4,28},{5,29},{6,30},{7,31},{8,16},{9,... | collective-permute-start | bytes 98312 | tf_op jit(solution)/shard_map/ppermute | solution.py:28
  59.1 12.8 %all-to-all-start.2 = ((bf16[32,4,8,512]{3,2,1,0:T(8,128)(2,1)}), bf16[32,4,8,512]{3,2,1,0:T(8,128)(2,1)S(1)}, u32[]{:S(2)}, u32[]{:S(2)}) async-start(bf16[32,4,8,512]{3,2,1,0:T(8,128)(2,1)} %bitcast.28.routed_ref), calls=%async_computation.2 | async-start | bytes 2097152 | tf_op jit(solution)/shard_map/all_to_all | solution.py:20
  71.9 0.0 copy-start.5
  71.9 0.0 copy-start.4
  71.9 0.0 copy-start.3
  72.1 1.8 %multiply.23 = f32[2,8,2,16,256]{4,3,2,1,0:T(8,128)S(1)} custom-call(s32[1]{0:T(128)} %bitcast.me_ref, bf16[32,4,512]{2,1,0:T(4,128)(2,1)S(1)} %bitcast.124, bf16[32,4,8,512]{3,2,1,0:T(8,128)(2,1)} %bitcast.28.routed_ref), custom_call_target="tpu_custom_call" | custom-call | flops 134217728 | bytes 3000000 | tf_op jit(solution)/shard_map/multiply/pallas_call | solution.py:144
  73.9 4.9 %collective-permute-start.7 = (f32[8,2,16,256]{3,2,1,0:T(8,128)S(1)}, f32[8,2,16,256]{3,2,1,0:T(8,128)S(1)}, u32[]{:S(2)}, u32[]{:S(2)}) collective-permute-start(f32[8,2,16,256]{3,2,1,0:T(8,128)S(1)} %slice_bitcast_fusion), channel_id=1, source_target_pairs={{0,1},{1,0},{2,3},{3,2},{4,5},{5,4},{6,7},{7,6},{8,9},{9,8},{10,11... | collective-permute-start | bytes 786440 | tf_op jit(solution)/shard_map/ppermute | solution.py:162
  78.8 7.1 %collective-permute-done.7 = f32[8,2,16,256]{3,2,1,0:T(8,128)S(1)} collective-permute-done((f32[8,2,16,256]{3,2,1,0:T(8,128)S(1)}, f32[8,2,16,256]{3,2,1,0:T(8,128)S(1)}, u32[]{:S(2)}, u32[]{:S(2)}) %collective-permute-start.7) | collective-permute-done | bytes 262176 | tf_op jit(solution)/shard_map/ppermute | solution.py:162
  85.9 10.2 %collective-permute-start.10 = (f32[2,16,256]{2,1,0:T(8,128)S(1)}, f32[2,16,256]{2,1,0:T(8,128)S(1)}, u32[]{:S(2)}, u32[]{:S(2)}) collective-permute-start(f32[2,16,256]{2,1,0:T(8,128)S(1)} %get-tuple-element.7), channel_id=1, source_target_pairs={{0,12},{1,13},{2,14},{3,15},{4,8},{5,9},{6,10},{7,11},{8,4},{9,5},... | collective-permute-start | bytes 98312 | tf_op jit(solution)/shard_map/ppermute | solution.py:162
  96.1 4.6 %collective-permute-start.11 = (f32[2,16,256]{2,1,0:T(8,128)S(1)}, f32[2,16,256]{2,1,0:T(8,128)S(1)}, u32[]{:S(2)}, u32[]{:S(2)}) collective-permute-start(f32[2,16,256]{2,1,0:T(8,128)S(1)} %get-tuple-element.6), channel_id=1, source_target_pairs={{0,16},{1,17},{2,18},{3,19},{4,20},{5,21},{6,22},{7,23},{8,24},{9,... | collective-permute-start | bytes 98312 | tf_op jit(solution)/shard_map/ppermute | solution.py:162
  100.8 0.1 dynamic_slice.3
  100.9 5.8 %collective-permute-start.12 = (f32[2,16,256]{2,1,0:T(8,128)S(1)}, f32[2,16,256]{2,1,0:T(8,128)S(1)}, u32[]{:S(2)}, u32[]{:S(2)}) collective-permute-start(f32[2,16,256]{2,1,0:T(8,128)S(1)} %get-tuple-element.5), channel_id=1, source_target_pairs={{0,20},{1,21},{2,22},{3,23},{4,16},{5,17},{6,18},{7,19},{8,28},{9,... | collective-permute-start | bytes 98312 | tf_op jit(solution)/shard_map/ppermute | solution.py:162
  106.7 9.3 %collective-permute-start.13 = (f32[2,16,256]{2,1,0:T(8,128)S(1)}, f32[2,16,256]{2,1,0:T(8,128)S(1)}, u32[]{:S(2)}, u32[]{:S(2)}) collective-permute-start(f32[2,16,256]{2,1,0:T(8,128)S(1)} %get-tuple-element.4), channel_id=1, source_target_pairs={{0,24},{1,25},{2,26},{3,27},{4,28},{5,29},{6,30},{7,31},{8,16},{9,... | collective-permute-start | bytes 98312 | tf_op jit(solution)/shard_map/ppermute | solution.py:162
  116.0 2.8 %collective-permute-start.14 = (f32[2,16,256]{2,1,0:T(8,128)S(1)}, f32[2,16,256]{2,1,0:T(8,128)S(1)}, u32[]{:S(2)}, u32[]{:S(2)}) collective-permute-start(f32[2,16,256]{2,1,0:T(8,128)S(1)} %get-tuple-element.3), channel_id=1, source_target_pairs={{0,28},{1,29},{2,30},{3,31},{4,24},{5,25},{6,26},{7,27},{8,20},{9,... | collective-permute-start | bytes 98312 | tf_op jit(solution)/shard_map/ppermute | solution.py:162
  118.8 3.8 %collective-permute-done.10 = f32[2,16,256]{2,1,0:T(8,128)S(1)} collective-permute-done((f32[2,16,256]{2,1,0:T(8,128)S(1)}, f32[2,16,256]{2,1,0:T(8,128)S(1)}, u32[]{:S(2)}, u32[]{:S(2)}) %collective-permute-start.10) | collective-permute-done | bytes 32800 | tf_op jit(solution)/shard_map/ppermute | solution.py:162
  122.6 6.3 %collective-permute-start.8 = (f32[2,16,256]{2,1,0:T(8,128)S(1)}, f32[2,16,256]{2,1,0:T(8,128)S(1)}, u32[]{:S(2)}, u32[]{:S(2)}) collective-permute-start(f32[2,16,256]{2,1,0:T(8,128)S(1)} %get-tuple-element.2), channel_id=1, source_target_pairs={{0,4},{1,5},{2,6},{3,7},{4,0},{5,1},{6,2},{7,3},{8,12},{9,13},{10,... | collective-permute-start | bytes 98312 | tf_op jit(solution)/shard_map/ppermute | solution.py:162
  128.8 5.7 %collective-permute-done.11 = f32[2,16,256]{2,1,0:T(8,128)S(1)} collective-permute-done((f32[2,16,256]{2,1,0:T(8,128)S(1)}, f32[2,16,256]{2,1,0:T(8,128)S(1)}, u32[]{:S(2)}, u32[]{:S(2)}) %collective-permute-start.11) | collective-permute-done | bytes 32800 | tf_op jit(solution)/shard_map/ppermute | solution.py:162
  134.6 1.9 %collective-permute-start.9 = (f32[2,16,256]{2,1,0:T(8,128)S(1)}, f32[2,16,256]{2,1,0:T(8,128)S(1)}, u32[]{:S(2)}, u32[]{:S(2)}) collective-permute-start(f32[2,16,256]{2,1,0:T(8,128)S(1)} %get-tuple-element.8), channel_id=1, source_target_pairs={{0,8},{1,9},{2,10},{3,11},{4,12},{5,13},{6,14},{7,15},{8,0},{9,1},... | collective-permute-start | bytes 98312 | tf_op jit(solution)/shard_map/ppermute | solution.py:162
  136.5 0.1 iota_compare_fusion
  136.6 7.7 %collective-permute-done.9 = f32[2,16,256]{2,1,0:T(8,128)S(1)} collective-permute-done((f32[2,16,256]{2,1,0:T(8,128)S(1)}, f32[2,16,256]{2,1,0:T(8,128)S(1)}, u32[]{:S(2)}, u32[]{:S(2)}) %collective-permute-start.9) | collective-permute-done | bytes 32800 | tf_op jit(solution)/shard_map/ppermute | solution.py:162
  144.3 1.9 %collective-permute-start.15 = (f32[16,256]{1,0:T(8,128)S(1)}, f32[16,256]{1,0:T(8,128)S(1)}, u32[]{:S(2)}, u32[]{:S(2)}) collective-permute-start(f32[16,256]{1,0:T(8,128)S(1)} %slice_bitcast_fusion.10), channel_id=1, source_target_pairs={{0,2},{1,3},{2,0},{3,1},{4,6},{5,7},{6,4},{7,5},{8,10},{9,11},{10,... | collective-permute-start | bytes 49160 | tf_op jit(solution)/shard_map/ppermute | solution.py:162
  146.2 0.5 fusion.32
  146.7 3.2 %collective-permute-done.15 = f32[16,256]{1,0:T(8,128)S(1)} collective-permute-done((f32[16,256]{1,0:T(8,128)S(1)}, f32[16,256]{1,0:T(8,128)S(1)}, u32[]{:S(2)}, u32[]{:S(2)}) %collective-permute-start.15) | collective-permute-done | bytes 16416 | tf_op jit(solution)/shard_map/ppermute | solution.py:162
  149.9 0.1 fusion.23
  150.1 0.2 fusion.5
  150.3 0.3 fusion.1
  150.6 0.7 copy.34
  151.3 0.6 copy.23
  151.9 1.3 reshape.143
  (50 shorter events, 0.6 us)
Async XLA Ops:
  0.6 0.9 copy-start
  2.3 13.2 %collective-permute-start = (bf16[4,4,4,512]{3,2,0,1:T(4,128)(2,1)S(1)}, bf16[4,4,4,512]{3,2,0,1:T(4,128)(2,1)S(1)}, u32[]{:S(2)}, u32[]{:S(2)}) collective-permute-start(bf16[4,4,4,512]{3,2,0,1:T(4,128)(2,1)S(1)} %copy.18), channel_id=1, source_target_pairs={{0,1},{1,0},{2,3},{3,2},{4,5},{5,4},{6,7},{7,6},{8,9},{9,8},{10,11... | collective-permute-start | bytes 196616 | tf_op jit(solution)/shard_map/ppermute | solution.py:28
  7.2 1.6 %copy-start.1 = (f32[1,512,1024]{2,1,0:T(8,128)S(1)}, f32[1,512,1024]{2,1,0:T(8,128)}, u32[]{:S(2)}) copy-start(f32[1,512,1024]{2,1,0:T(8,128)} %weights_ref.1) | copy-start | bytes 6291460
  10.3 18.5 %copy-start.2 = (s32[16]{0:T(128)S(1)}, s32[16]{0:T(128)}, u32[]{:S(2)}) copy-start(s32[16]{0:T(128)} %group_ref.1) | copy-start | bytes 196
  10.3 18.5 %all-to-all-start = ((bf16[16,64,512]{2,1,0:T(8,128)(2,1)}), bf16[16,64,512]{2,1,0:T(8,128)(2,1)S(1)}, u32[]{:S(2)}, u32[]{:S(2)}) async-start(bf16[16,64,512]{2,1,0:T(8,128)(2,1)} %bitcast.27), calls=%async_computation | async-start | bytes 2097152 | tf_op jit(solution)/shard_map/all_to_all | solution.py:20
  15.5 9.7 %collective-permute-start.1 = (bf16[2,4,4,512]{3,2,0,1:T(4,128)(2,1)S(1)}, bf16[2,4,4,512]{3,2,0,1:T(4,128)(2,1)S(1)}, u32[]{:S(2)}, u32[]{:S(2)}) collective-permute-start(bf16[2,4,4,512]{3,2,0,1:T(4,128)(2,1)S(1)} %pad_maximum_fusion), channel_id=1, source_target_pairs={{0,2},{1,3},{2,0},{3,1},{4,6},{5,7},{6,4},{7,5},{8,10},{9,11},{10,... | collective-permute-start | bytes 98312 | tf_op jit(solution)/shard_map/ppermute | solution.py:28
  18.9 18.9 %collective-permute-start.2 = (bf16[2,4,4,512]{3,2,1,0:T(4,128)(2,1)S(1)}, bf16[2,4,4,512]{3,2,1,0:T(4,128)(2,1)S(1)}, u32[]{:S(2)}, u32[]{:S(2)}) collective-permute-start(bf16[2,4,4,512]{3,2,1,0:T(4,128)(2,1)S(1)} %pad_maximum_fusion.1), channel_id=1, source_target_pairs={{0,4},{1,5},{2,6},{3,7},{4,0},{5,1},{6,2},{7,3},{8,12},{9,13},{10,... | collective-permute-start | bytes 98312 | tf_op jit(solution)/shard_map/ppermute | solution.py:28
  22.9 15.0 %collective-permute-start.3 = (bf16[2,4,4,512]{3,2,0,1:T(4,128)(2,1)S(1)}, bf16[2,4,4,512]{3,2,0,1:T(4,128)(2,1)S(1)}, u32[]{:S(2)}, u32[]{:S(2)}) collective-permute-start(bf16[2,4,4,512]{3,2,0,1:T(4,128)(2,1)S(1)} %pad_maximum_fusion.2), channel_id=1, source_target_pairs={{0,6},{1,7},{2,4},{3,5},{4,2},{5,3},{6,0},{7,1},{8,14},{9,15},{10,... | collective-permute-start | bytes 98312 | tf_op jit(solution)/shard_map/ppermute | solution.py:28
  30.5 28.6 %all-to-all-start.1 = ((bf16[16,64,512]{2,1,0:T(8,128)(2,1)}), bf16[16,64,512]{2,1,0:T(8,128)(2,1)}, u32[]{:S(2)}, u32[]{:S(2)}) async-start(bf16[16,64,512]{2,1,0:T(8,128)(2,1)} %pick.1), calls=%async_computation.1 | async-start | bytes 2097152 | tf_op jit(solution)/shard_map/all_to_all | solution.py:20
  37.9 34.0 %collective-permute-start.4 = (bf16[4,2,4,512]{3,2,1,0:T(4,128)(2,1)S(1)}, bf16[4,2,4,512]{3,2,1,0:T(4,128)(2,1)S(1)}, u32[]{:S(2)}, u32[]{:S(2)}) collective-permute-start(bf16[4,2,4,512]{3,2,1,0:T(4,128)(2,1)S(1)} %pad_maximum_fusion.3), channel_id=1, source_target_pairs={{0,8},{1,9},{2,10},{3,11},{4,12},{5,13},{6,14},{7,15},{8,0},{9,1},... | collective-permute-start | bytes 98312 | tf_op jit(solution)/shard_map/ppermute | solution.py:28
  47.0 24.9 %collective-permute-start.5 = (bf16[4,2,4,512]{3,2,1,0:T(4,128)(2,1)S(1)}, bf16[4,2,4,512]{3,2,1,0:T(4,128)(2,1)S(1)}, u32[]{:S(2)}, u32[]{:S(2)}) collective-permute-start(bf16[4,2,4,512]{3,2,1,0:T(4,128)(2,1)S(1)} %pad_maximum_fusion.4), channel_id=1, source_target_pairs={{0,16},{1,17},{2,18},{3,19},{4,20},{5,21},{6,22},{7,23},{8,24},{9,... | collective-permute-start | bytes 98312 | tf_op jit(solution)/shard_map/ppermute | solution.py:28
  57.1 14.9 %collective-permute-start.6 = (bf16[4,2,4,512]{3,2,1,0:T(4,128)(2,1)S(1)}, bf16[4,2,4,512]{3,2,1,0:T(4,128)(2,1)S(1)}, u32[]{:S(2)}, u32[]{:S(2)}) collective-permute-start(bf16[4,2,4,512]{3,2,1,0:T(4,128)(2,1)S(1)} %pad_maximum_fusion.5), channel_id=1, source_target_pairs={{0,24},{1,25},{2,26},{3,27},{4,28},{5,29},{6,30},{7,31},{8,16},{9,... | collective-permute-start | bytes 98312 | tf_op jit(solution)/shard_map/ppermute | solution.py:28
  59.1 92.2 %all-to-all-start.2 = ((bf16[32,4,8,512]{3,2,1,0:T(8,128)(2,1)}), bf16[32,4,8,512]{3,2,1,0:T(8,128)(2,1)S(1)}, u32[]{:S(2)}, u32[]{:S(2)}) async-start(bf16[32,4,8,512]{3,2,1,0:T(8,128)(2,1)} %bitcast.28.routed_ref), calls=%async_computation.2 | async-start | bytes 2097152 | tf_op jit(solution)/shard_map/all_to_all | solution.py:20
  71.9 28.9 %copy-start.5 = (s32[128]{0:T(128)S(1)}, s32[128]{0:T(128)}, u32[]{:S(2)}) copy-start(s32[128]{0:T(128)} %param.11) | copy-start | bytes 1540
  71.9 64.7 %copy-start.4 = (bf16[16,2048]{1,0:T(8,128)(2,1)S(1)}, bf16[16,2048]{1,0:T(8,128)(2,1)}, u32[]{:S(2)}) copy-start(bf16[16,2048]{1,0:T(8,128)(2,1)} %param.9) | copy-start | bytes 196612
  71.9 74.3 %copy-start.3 = (bf16[16,128,256]{2,1,0:T(8,128)(2,1)S(1)}, bf16[16,128,256]{2,1,0:T(8,128)(2,1)}, u32[]{:S(2)}) copy-start(bf16[16,128,256]{2,1,0:T(8,128)(2,1)} %param.10) | copy-start | bytes 3145732
  73.9 12.0 %collective-permute-start.7 = (f32[8,2,16,256]{3,2,1,0:T(8,128)S(1)}, f32[8,2,16,256]{3,2,1,0:T(8,128)S(1)}, u32[]{:S(2)}, u32[]{:S(2)}) collective-permute-start(f32[8,2,16,256]{3,2,1,0:T(8,128)S(1)} %slice_bitcast_fusion), channel_id=1, source_target_pairs={{0,1},{1,0},{2,3},{3,2},{4,5},{5,4},{6,7},{7,6},{8,9},{9,8},{10,11... | collective-permute-start | bytes 786440 | tf_op jit(solution)/shard_map/ppermute | solution.py:162
  85.9 36.6 %collective-permute-start.10 = (f32[2,16,256]{2,1,0:T(8,128)S(1)}, f32[2,16,256]{2,1,0:T(8,128)S(1)}, u32[]{:S(2)}, u32[]{:S(2)}) collective-permute-start(f32[2,16,256]{2,1,0:T(8,128)S(1)} %get-tuple-element.7), channel_id=1, source_target_pairs={{0,12},{1,13},{2,14},{3,15},{4,8},{5,9},{6,10},{7,11},{8,4},{9,5},... | collective-permute-start | bytes 98312 | tf_op jit(solution)/shard_map/ppermute | solution.py:162
  96.1 38.4 %collective-permute-start.11 = (f32[2,16,256]{2,1,0:T(8,128)S(1)}, f32[2,16,256]{2,1,0:T(8,128)S(1)}, u32[]{:S(2)}, u32[]{:S(2)}) collective-permute-start(f32[2,16,256]{2,1,0:T(8,128)S(1)} %get-tuple-element.6), channel_id=1, source_target_pairs={{0,16},{1,17},{2,18},{3,19},{4,20},{5,21},{6,22},{7,23},{8,24},{9,... | collective-permute-start | bytes 98312 | tf_op jit(solution)/shard_map/ppermute | solution.py:162
  100.9 35.7 %collective-permute-start.12 = (f32[2,16,256]{2,1,0:T(8,128)S(1)}, f32[2,16,256]{2,1,0:T(8,128)S(1)}, u32[]{:S(2)}, u32[]{:S(2)}) collective-permute-start(f32[2,16,256]{2,1,0:T(8,128)S(1)} %get-tuple-element.5), channel_id=1, source_target_pairs={{0,20},{1,21},{2,22},{3,23},{4,16},{5,17},{6,18},{7,19},{8,28},{9,... | collective-permute-start | bytes 98312 | tf_op jit(solution)/shard_map/ppermute | solution.py:162
  106.7 29.9 %collective-permute-start.13 = (f32[2,16,256]{2,1,0:T(8,128)S(1)}, f32[2,16,256]{2,1,0:T(8,128)S(1)}, u32[]{:S(2)}, u32[]{:S(2)}) collective-permute-start(f32[2,16,256]{2,1,0:T(8,128)S(1)} %get-tuple-element.4), channel_id=1, source_target_pairs={{0,24},{1,25},{2,26},{3,27},{4,28},{5,29},{6,30},{7,31},{8,16},{9,... | collective-permute-start | bytes 98312 | tf_op jit(solution)/shard_map/ppermute | solution.py:162
  116.0 20.6 %collective-permute-start.14 = (f32[2,16,256]{2,1,0:T(8,128)S(1)}, f32[2,16,256]{2,1,0:T(8,128)S(1)}, u32[]{:S(2)}, u32[]{:S(2)}) collective-permute-start(f32[2,16,256]{2,1,0:T(8,128)S(1)} %get-tuple-element.3), channel_id=1, source_target_pairs={{0,28},{1,29},{2,30},{3,31},{4,24},{5,25},{6,26},{7,27},{8,20},{9,... | collective-permute-start | bytes 98312 | tf_op jit(solution)/shard_map/ppermute | solution.py:162
  122.6 14.0 %collective-permute-start.8 = (f32[2,16,256]{2,1,0:T(8,128)S(1)}, f32[2,16,256]{2,1,0:T(8,128)S(1)}, u32[]{:S(2)}, u32[]{:S(2)}) collective-permute-start(f32[2,16,256]{2,1,0:T(8,128)S(1)} %get-tuple-element.2), channel_id=1, source_target_pairs={{0,4},{1,5},{2,6},{3,7},{4,0},{5,1},{6,2},{7,3},{8,12},{9,13},{10,... | collective-permute-start | bytes 98312 | tf_op jit(solution)/shard_map/ppermute | solution.py:162
  134.6 9.7 %collective-permute-start.9 = (f32[2,16,256]{2,1,0:T(8,128)S(1)}, f32[2,16,256]{2,1,0:T(8,128)S(1)}, u32[]{:S(2)}, u32[]{:S(2)}) collective-permute-start(f32[2,16,256]{2,1,0:T(8,128)S(1)} %get-tuple-element.8), channel_id=1, source_target_pairs={{0,8},{1,9},{2,10},{3,11},{4,12},{5,13},{6,14},{7,15},{8,0},{9,1},... | collective-permute-start | bytes 98312 | tf_op jit(solution)/shard_map/ppermute | solution.py:162
  144.3 5.6 %collective-permute-start.15 = (f32[16,256]{1,0:T(8,128)S(1)}, f32[16,256]{1,0:T(8,128)S(1)}, u32[]{:S(2)}, u32[]{:S(2)}) collective-permute-start(f32[16,256]{1,0:T(8,128)S(1)} %slice_bitcast_fusion.10), channel_id=1, source_target_pairs={{0,2},{1,3},{2,0},{3,1},{4,6},{5,7},{6,4},{7,5},{8,10},{9,11},{10,... | collective-permute-start | bytes 49160 | tf_op jit(solution)/shard_map/ppermute | solution.py:162

commit v7 on v6

--- a/solution.py
+++ b/solution.py
@@ -73,13 +73,13 @@
 
 def flip_kernel(weights_ref, out_ref):
     step = pl.program_id(0)
-    shards, heads, piece, _ = out_ref.shape
+    shards, piece, width = out_ref.shape
     rows = weights_ref.shape[1]
-    lanes = pl.ds(pl.multiple_of(step * rows, rows), rows)
-    for h in range(heads):
-        width = shards * piece
-        block = weights_ref[0, :, h * width : (h + 1) * width].astype(jnp.bfloat16)
-        out_ref[:, h, :, lanes] = block.T.reshape(shards, piece, rows)
+    for h in range(KVH):
+        lanes = pl.ds(pl.multiple_of(h * (width // KVH) + step * rows, rows), rows)
+        columns = shards * piece
+        block = weights_ref[0, :, h * columns : (h + 1) * columns].astype(jnp.bfloat16)
+        out_ref[:, :, lanes] = block.T.reshape(shards, piece, rows)
 
 
 def flip(weights, shards):
@@ -91,9 +91,9 @@
         grid=(depth // rows,),
         in_specs=[pl.BlockSpec((1, rows, columns), lambda i: (0, i, 0))],
         out_specs=VMEM,
-        out_shape=jax.ShapeDtypeStruct((shards, KVH, piece, depth), jnp.bfloat16),
+        out_shape=jax.ShapeDtypeStruct((shards, piece, KVH * depth), jnp.bfloat16),
         cost_estimate=pl.CostEstimate(flops=2_000_000, bytes_accessed=3_000_000, transcendentals=0),
-        compiler_params=pltpu.CompilerParams(vmem_limit_bytes=12 * 1024 * 1024),
+        compiler_params=pltpu.CompilerParams(vmem_limit_bytes=62 * 1024 * 1024),
         name="flip",
     )(weights)
 
@@ -120,7 +120,8 @@
 
 def multiply_kernel(me_ref, inputs_ref, routed_ref, out_ref, rows_ref):
     me = me_ref[0]
-    shards, heads, piece, depth = routed_ref.shape
+    shards, piece, width = routed_ref.shape
+    heads, depth = KVH, width // KVH
     per_head = shards // heads
     own = inputs_ref.shape[1]
     block_rows = ROWS // per_head
@@ -130,7 +131,7 @@
     for h in range(heads):
         product = lax.dot_general(
             inputs,
-            routed_ref[:, h].reshape(shards * piece, depth),
+            routed_ref[:, :, h * depth : (h + 1) * depth].reshape(shards * piece, depth),
             (((1,), (1,)), ((), ())),
             preferred_element_type=jnp.float32,
         )
@@ -140,7 +141,8 @@
 
 
 def multiply(me, inputs, routed):
-    shards, heads, _, depth = routed.shape
+    shards, _, width = routed.shape
+    heads, depth = KVH, width // KVH
     return pl.pallas_call(
         multiply_kernel,
         in_specs=[pl.BlockSpec(memory_space=pltpu.SMEM), VMEM, VMEM],
@@ -177,13 +179,15 @@
     slice_rows = train_weights.shape[1]
     own = hidden.shape[0]
     inputs = spread_rows(hidden.reshape(own, shards, slice_rows).transpose(1, 0, 2))
-    flipped = flip(train_weights, shards).reshape(sections, -1, slice_rows)
+    flipped = flip(train_weights, shards)
+    flipped = flipped.reshape(sections, -1, KVH * slice_rows)
     spread = exchange(flipped, "section")
     picked = pick(section_to_group, spread)
-    routed = exchange(picked, "section").reshape(shards, KVH, piece_cols, slice_rows)
+    routed = exchange(picked, "section").reshape(shards, piece_cols, KVH * slice_rows)
     me = lax.axis_index("shard").astype(jnp.int32).reshape(1)
     received = exchange(routed, "shard")
-    layer_out = received.transpose(1, 2, 0, 3).reshape(1, KVH, piece_cols, D)
+    layer_out = received.reshape(shards, piece_cols, KVH, slice_rows)
+    layer_out = layer_out.transpose(2, 1, 0, 3).reshape(1, KVH, piece_cols, D)
     fresh = reduce_rows(multiply(me, inputs, routed)).astype(jnp.bfloat16)
     block_index = lax.axis_index("shard") % per_head
     row_lengths = lax.dynamic_slice_in_dim(lengths, block_index * row_block, row_block, 0)

time: 154 us -> 154 us (level)
  local copies, waits for them, and re-layouts: 6.05 us -> 3.64 us
  Pallas kernels: 4.95 us -> 6.96 us
    pallas_call x1, Pallas kernels: 1.51 us -> 3.53 us  [flip(): pl.pallas_call(flip_kernel, grid=(depth // rows,), in_specs=[pl.BlockSpec...]
    unnamed x19 -> x17, local copies, waits for them, and re-layouts: 3.14 us -> 1.55 us
  transfers between devices with their start and end apart: 19 -> 19, of which waited for: 6 -> 6; matrix products, arithmetic and copies ran while one was open for 2% -> 2% of each run, Pallas kernels for 3% -> 5%
where the time goes in v7:
time: 154 us; the launch traced here: 153 us
  starting transfers between devices  108 us (70%)
  waiting for transfers between devices  31.1 us (20%)
  Pallas kernels  6.96 us (5%)
  local copies, waits for them, and re-layouts  3.64 us (2%)
    ppermute x16, starting transfers between devices, send(): return lax.ppermute(values, 'shard', [(i, i ^ bits) for i in range(shards)])  83.2 us
    ppermute x16, waiting for transfers between devices, send(): return lax.ppermute(values, 'shard', [(i, i ^ bits) for i in range(shards)])  27.6 us
    all_to_all x3, starting transfers between devices, exchange(): return lax.all_to_all(blocks, axis, split_axis=0, concat_axis=0, tiled=True)  25.2 us
    all_to_all x3, waiting for transfers between devices, exchange(): return lax.all_to_all(blocks, axis, split_axis=0, concat_axis=0, tiled=True)  3.55 us
    pallas_call x1, Pallas kernels, flip(): pl.pallas_call(flip_kernel, grid=(depth // rows,), in_specs=[pl.BlockSpec...  3.53 us
  transfers between devices with their start and end apart: 19, of which 6 were waited for; matrix products, arithmetic and copies ran while one was open for 2% of the time, Pallas kernels for 5%

profile of v7, /device:TPU:40, one launch (start us, length us, event | category | flops | bytes accessed | tf_op | source)
XLA Modules:
  0.0 152.8 jit_solution(9723168928084889835)
XLA Ops:
  0.6 0.0 copy-start
  0.7 0.1 xor.18
  0.8 0.8 copy-done
  1.5 0.7 gather_fusion
  2.3 4.9 %collective-permute-start = (bf16[4,4,4,512]{3,2,0,1:T(4,128)(2,1)S(1)}, bf16[4,4,4,512]{3,2,0,1:T(4,128)(2,1)S(1)}, u32[]{:S(2)}, u32[]{:S(2)}) collective-permute-start(bf16[4,4,4,512]{3,2,0,1:T(4,128)(2,1)S(1)} %copy.19), channel_id=1, source_target_pairs={{0,1},{1,0},{2,3},{3,2},{4,5},{5,4},{6,7},{7,6},{8,9},{9,8},{10,11... | collective-permute-start | bytes 196616 | tf_op jit(solution)/shard_map/ppermute | solution.py:28
  7.2 3.5 %flip.1 = bf16[32,8,2048]{2,1,0:T(8,128)(2,1)} custom-call(f32[1,512,1024]{2,1,0:T(8,128)} %weights_ref.1), custom_call_target="tpu_custom_call" | custom-call | flops 2000000 | bytes 3000000 | tf_op jit(solution)/shard_map/flip/pallas_call | solution.py:89
  10.7 5.1 %all-to-all-start = ((bf16[16,16,2048]{2,1,0:T(8,128)(2,1)}), bf16[16,16,2048]{2,1,0:T(8,128)(2,1)S(1)}, u32[]{:S(2)}, u32[]{:S(2)}) async-start(bf16[16,16,2048]{2,1,0:T(8,128)(2,1)} %bitcast.126), calls=%async_computation | async-start | bytes 2097152 | tf_op jit(solution)/shard_map/all_to_all | solution.py:20
  15.9 0.0 collective-permute-done
  15.9 3.3 %collective-permute-start.1 = (bf16[2,4,4,512]{3,2,0,1:T(4,128)(2,1)S(1)}, bf16[2,4,4,512]{3,2,0,1:T(4,128)(2,1)S(1)}, u32[]{:S(2)}, u32[]{:S(2)}) collective-permute-start(bf16[2,4,4,512]{3,2,0,1:T(4,128)(2,1)S(1)} %pad_maximum_fusion), channel_id=1, source_target_pairs={{0,2},{1,3},{2,0},{3,1},{4,6},{5,7},{6,4},{7,5},{8,10},{9,11},{10,... | collective-permute-start | bytes 98312 | tf_op jit(solution)/shard_map/ppermute | solution.py:28
  19.3 3.9 %collective-permute-start.2 = (bf16[2,4,4,512]{3,2,1,0:T(4,128)(2,1)S(1)}, bf16[2,4,4,512]{3,2,1,0:T(4,128)(2,1)S(1)}, u32[]{:S(2)}, u32[]{:S(2)}) collective-permute-start(bf16[2,4,4,512]{3,2,1,0:T(4,128)(2,1)S(1)} %pad_maximum_fusion.1), channel_id=1, source_target_pairs={{0,4},{1,5},{2,6},{3,7},{4,0},{5,1},{6,2},{7,3},{8,12},{9,13},{10,... | collective-permute-start | bytes 98312 | tf_op jit(solution)/shard_map/ppermute | solution.py:28
  23.3 2.4 %collective-permute-start.3 = (bf16[2,4,4,512]{3,2,0,1:T(4,128)(2,1)S(1)}, bf16[2,4,4,512]{3,2,0,1:T(4,128)(2,1)S(1)}, u32[]{:S(2)}, u32[]{:S(2)}) collective-permute-start(bf16[2,4,4,512]{3,2,0,1:T(4,128)(2,1)S(1)} %pad_maximum_fusion.2), channel_id=1, source_target_pairs={{0,6},{1,7},{2,4},{3,5},{4,2},{5,3},{6,0},{7,1},{8,14},{9,15},{10,... | collective-permute-start | bytes 98312 | tf_op jit(solution)/shard_map/ppermute | solution.py:28
  25.7 0.0 collective-permute-done.1
  25.7 3.5 %all-to-all-done.spread_ref = bf16[16,16,2048]{2,1,0:T(8,128)(2,1)S(1)} async-done(((bf16[16,16,2048]{2,1,0:T(8,128)(2,1)}), bf16[16,16,2048]{2,1,0:T(8,128)(2,1)S(1)}, u32[]{:S(2)}, u32[]{:S(2)}) %all-to-all-start) | async-done | bytes 1048608 | tf_op jit(solution)/shard_map/all_to_all | solution.py:20
  29.2 1.7 %pick.1 = bf16[16,16,2048]{2,1,0:T(8,128)(2,1)} custom-call(s32[16]{0:T(128)S(1)} %copy-done.1, bf16[16,16,2048]{2,1,0:T(8,128)(2,1)S(1)} %all-to-all-done.spread_ref), custom_call_target="tpu_custom_call" | custom-call | flops 1000000 | bytes 2000000 | tf_op jit(solution)/shard_map/pick/pallas_call | solution.py:110
  30.9 7.3 %all-to-all-start.1 = ((bf16[16,16,2048]{2,1,0:T(8,128)(2,1)}), bf16[16,16,2048]{2,1,0:T(8,128)(2,1)}, u32[]{:S(2)}, u32[]{:S(2)}) async-start(bf16[16,16,2048]{2,1,0:T(8,128)(2,1)} %pick.1), calls=%async_computation.1 | async-start | bytes 2097152 | tf_op jit(solution)/shard_map/all_to_all | solution.py:20
  38.2 0.0 collective-permute-done.2
  38.2 0.0 collective-permute-done.3
  38.3 9.1 %collective-permute-start.4 = (bf16[4,2,4,512]{3,2,1,0:T(4,128)(2,1)S(1)}, bf16[4,2,4,512]{3,2,1,0:T(4,128)(2,1)S(1)}, u32[]{:S(2)}, u32[]{:S(2)}) collective-permute-start(bf16[4,2,4,512]{3,2,1,0:T(4,128)(2,1)S(1)} %pad_maximum_fusion.3), channel_id=1, source_target_pairs={{0,8},{1,9},{2,10},{3,11},{4,12},{5,13},{6,14},{7,15},{8,0},{9,1},... | collective-permute-start | bytes 98312 | tf_op jit(solution)/shard_map/ppermute | solution.py:28
  47.4 10.0 %collective-permute-start.5 = (bf16[4,2,4,512]{3,2,1,0:T(4,128)(2,1)S(1)}, bf16[4,2,4,512]{3,2,1,0:T(4,128)(2,1)S(1)}, u32[]{:S(2)}, u32[]{:S(2)}) collective-permute-start(bf16[4,2,4,512]{3,2,1,0:T(4,128)(2,1)S(1)} %pad_maximum_fusion.4), channel_id=1, source_target_pairs={{0,16},{1,17},{2,18},{3,19},{4,20},{5,21},{6,22},{7,23},{8,24},{9,... | collective-permute-start | bytes 98312 | tf_op jit(solution)/shard_map/ppermute | solution.py:28
  57.5 1.9 %collective-permute-start.6 = (bf16[4,2,4,512]{3,2,1,0:T(4,128)(2,1)S(1)}, bf16[4,2,4,512]{3,2,1,0:T(4,128)(2,1)S(1)}, u32[]{:S(2)}, u32[]{:S(2)}) collective-permute-start(bf16[4,2,4,512]{3,2,1,0:T(4,128)(2,1)S(1)} %pad_maximum_fusion.5), channel_id=1, source_target_pairs={{0,24},{1,25},{2,26},{3,27},{4,28},{5,29},{6,30},{7,31},{8,16},{9,... | collective-permute-start | bytes 98312 | tf_op jit(solution)/shard_map/ppermute | solution.py:28
  59.5 0.0 all-to-all-done.1
  59.5 12.8 %all-to-all-start.2 = ((bf16[32,8,2048]{2,1,0:T(8,128)(2,1)}), bf16[32,8,2048]{2,1,0:T(8,128)(2,1)S(1)}, u32[]{:S(2)}, u32[]{:S(2)}) async-start(bf16[32,8,2048]{2,1,0:T(8,128)(2,1)} %bitcast.28.routed_ref), calls=%async_computation.2 | async-start | bytes 2097152 | tf_op jit(solution)/shard_map/all_to_all | solution.py:20
  72.3 0.0 copy-start.4
  72.3 0.0 copy-start.3
  72.3 0.0 copy-start.2
  72.5 1.8 %multiply.23 = f32[2,8,2,16,256]{4,3,2,1,0:T(8,128)S(1)} custom-call(s32[1]{0:T(128)} %bitcast.me_ref, bf16[32,4,512]{2,1,0:T(4,128)(2,1)S(1)} %bitcast.125, bf16[32,8,2048]{2,1,0:T(8,128)(2,1)} %bitcast.28.routed_ref), custom_call_target="tpu_custom_call" | custom-call | flops 134217728 | bytes 3000000 | tf_op jit(solution)/shard_map/multiply/pallas_call | solution.py:146
  74.3 4.9 %collective-permute-start.7 = (f32[8,2,16,256]{3,2,1,0:T(8,128)S(1)}, f32[8,2,16,256]{3,2,1,0:T(8,128)S(1)}, u32[]{:S(2)}, u32[]{:S(2)}) collective-permute-start(f32[8,2,16,256]{3,2,1,0:T(8,128)S(1)} %slice_bitcast_fusion), channel_id=1, source_target_pairs={{0,1},{1,0},{2,3},{3,2},{4,5},{5,4},{6,7},{7,6},{8,9},{9,8},{10,11... | collective-permute-start | bytes 786440 | tf_op jit(solution)/shard_map/ppermute | solution.py:164
  79.2 7.1 %collective-permute-done.7 = f32[8,2,16,256]{3,2,1,0:T(8,128)S(1)} collective-permute-done((f32[8,2,16,256]{3,2,1,0:T(8,128)S(1)}, f32[8,2,16,256]{3,2,1,0:T(8,128)S(1)}, u32[]{:S(2)}, u32[]{:S(2)}) %collective-permute-start.7) | collective-permute-done | bytes 262176 | tf_op jit(solution)/shard_map/ppermute | solution.py:164
  86.3 10.2 %collective-permute-start.10 = (f32[2,16,256]{2,1,0:T(8,128)S(1)}, f32[2,16,256]{2,1,0:T(8,128)S(1)}, u32[]{:S(2)}, u32[]{:S(2)}) collective-permute-start(f32[2,16,256]{2,1,0:T(8,128)S(1)} %get-tuple-element.7), channel_id=1, source_target_pairs={{0,12},{1,13},{2,14},{3,15},{4,8},{5,9},{6,10},{7,11},{8,4},{9,5},... | collective-permute-start | bytes 98312 | tf_op jit(solution)/shard_map/ppermute | solution.py:164
  96.5 4.6 %collective-permute-start.11 = (f32[2,16,256]{2,1,0:T(8,128)S(1)}, f32[2,16,256]{2,1,0:T(8,128)S(1)}, u32[]{:S(2)}, u32[]{:S(2)}) collective-permute-start(f32[2,16,256]{2,1,0:T(8,128)S(1)} %get-tuple-element.6), channel_id=1, source_target_pairs={{0,16},{1,17},{2,18},{3,19},{4,20},{5,21},{6,22},{7,23},{8,24},{9,... | collective-permute-start | bytes 98312 | tf_op jit(solution)/shard_map/ppermute | solution.py:164
  101.2 0.1 dynamic_slice.3
  101.3 5.8 %collective-permute-start.12 = (f32[2,16,256]{2,1,0:T(8,128)S(1)}, f32[2,16,256]{2,1,0:T(8,128)S(1)}, u32[]{:S(2)}, u32[]{:S(2)}) collective-permute-start(f32[2,16,256]{2,1,0:T(8,128)S(1)} %get-tuple-element.5), channel_id=1, source_target_pairs={{0,20},{1,21},{2,22},{3,23},{4,16},{5,17},{6,18},{7,19},{8,28},{9,... | collective-permute-start | bytes 98312 | tf_op jit(solution)/shard_map/ppermute | solution.py:164
  107.1 9.3 %collective-permute-start.13 = (f32[2,16,256]{2,1,0:T(8,128)S(1)}, f32[2,16,256]{2,1,0:T(8,128)S(1)}, u32[]{:S(2)}, u32[]{:S(2)}) collective-permute-start(f32[2,16,256]{2,1,0:T(8,128)S(1)} %get-tuple-element.4), channel_id=1, source_target_pairs={{0,24},{1,25},{2,26},{3,27},{4,28},{5,29},{6,30},{7,31},{8,16},{9,... | collective-permute-start | bytes 98312 | tf_op jit(solution)/shard_map/ppermute | solution.py:164
  116.4 2.8 %collective-permute-start.14 = (f32[2,16,256]{2,1,0:T(8,128)S(1)}, f32[2,16,256]{2,1,0:T(8,128)S(1)}, u32[]{:S(2)}, u32[]{:S(2)}) collective-permute-start(f32[2,16,256]{2,1,0:T(8,128)S(1)} %get-tuple-element.3), channel_id=1, source_target_pairs={{0,28},{1,29},{2,30},{3,31},{4,24},{5,25},{6,26},{7,27},{8,20},{9,... | collective-permute-start | bytes 98312 | tf_op jit(solution)/shard_map/ppermute | solution.py:164
  119.2 3.8 %collective-permute-done.10 = f32[2,16,256]{2,1,0:T(8,128)S(1)} collective-permute-done((f32[2,16,256]{2,1,0:T(8,128)S(1)}, f32[2,16,256]{2,1,0:T(8,128)S(1)}, u32[]{:S(2)}, u32[]{:S(2)}) %collective-permute-start.10) | collective-permute-done | bytes 32800 | tf_op jit(solution)/shard_map/ppermute | solution.py:164
  123.0 6.3 %collective-permute-start.8 = (f32[2,16,256]{2,1,0:T(8,128)S(1)}, f32[2,16,256]{2,1,0:T(8,128)S(1)}, u32[]{:S(2)}, u32[]{:S(2)}) collective-permute-start(f32[2,16,256]{2,1,0:T(8,128)S(1)} %get-tuple-element.2), channel_id=1, source_target_pairs={{0,4},{1,5},{2,6},{3,7},{4,0},{5,1},{6,2},{7,3},{8,12},{9,13},{10,... | collective-permute-start | bytes 98312 | tf_op jit(solution)/shard_map/ppermute | solution.py:164
  129.2 5.7 %collective-permute-done.11 = f32[2,16,256]{2,1,0:T(8,128)S(1)} collective-permute-done((f32[2,16,256]{2,1,0:T(8,128)S(1)}, f32[2,16,256]{2,1,0:T(8,128)S(1)}, u32[]{:S(2)}, u32[]{:S(2)}) %collective-permute-start.11) | collective-permute-done | bytes 32800 | tf_op jit(solution)/shard_map/ppermute | solution.py:164
  135.0 1.9 %collective-permute-start.9 = (f32[2,16,256]{2,1,0:T(8,128)S(1)}, f32[2,16,256]{2,1,0:T(8,128)S(1)}, u32[]{:S(2)}, u32[]{:S(2)}) collective-permute-start(f32[2,16,256]{2,1,0:T(8,128)S(1)} %get-tuple-element.8), channel_id=1, source_target_pairs={{0,8},{1,9},{2,10},{3,11},{4,12},{5,13},{6,14},{7,15},{8,0},{9,1},... | collective-permute-start | bytes 98312 | tf_op jit(solution)/shard_map/ppermute | solution.py:164
  136.9 0.1 iota_compare_fusion
  137.0 7.7 %collective-permute-done.9 = f32[2,16,256]{2,1,0:T(8,128)S(1)} collective-permute-done((f32[2,16,256]{2,1,0:T(8,128)S(1)}, f32[2,16,256]{2,1,0:T(8,128)S(1)}, u32[]{:S(2)}, u32[]{:S(2)}) %collective-permute-start.9) | collective-permute-done | bytes 32800 | tf_op jit(solution)/shard_map/ppermute | solution.py:164
  144.7 1.9 %collective-permute-start.15 = (f32[16,256]{1,0:T(8,128)S(1)}, f32[16,256]{1,0:T(8,128)S(1)}, u32[]{:S(2)}, u32[]{:S(2)}) collective-permute-start(f32[16,256]{1,0:T(8,128)S(1)} %slice_bitcast_fusion.10), channel_id=1, source_target_pairs={{0,2},{1,3},{2,0},{3,1},{4,6},{5,7},{6,4},{7,5},{8,10},{9,11},{10,... | collective-permute-start | bytes 49160 | tf_op jit(solution)/shard_map/ppermute | solution.py:164
  146.6 0.5 fusion.32
  147.1 3.2 %collective-permute-done.15 = f32[16,256]{1,0:T(8,128)S(1)} collective-permute-done((f32[16,256]{1,0:T(8,128)S(1)}, f32[16,256]{1,0:T(8,128)S(1)}, u32[]{:S(2)}, u32[]{:S(2)}) %collective-permute-start.15) | collective-permute-done | bytes 16416 | tf_op jit(solution)/shard_map/ppermute | solution.py:164
  150.3 0.1 fusion.23
  150.5 0.2 fusion.5
  150.7 0.3 fusion.1
  151.0 0.7 copy.35
  151.7 1.1 copy.24
  (47 shorter events, 0.6 us)
Async XLA Ops:
  0.6 0.9 copy-start
  2.3 13.6 %collective-permute-start = (bf16[4,4,4,512]{3,2,0,1:T(4,128)(2,1)S(1)}, bf16[4,4,4,512]{3,2,0,1:T(4,128)(2,1)S(1)}, u32[]{:S(2)}, u32[]{:S(2)}) collective-permute-start(bf16[4,4,4,512]{3,2,0,1:T(4,128)(2,1)S(1)} %copy.19), channel_id=1, source_target_pairs={{0,1},{1,0},{2,3},{3,2},{4,5},{5,4},{6,7},{7,6},{8,9},{9,8},{10,11... | collective-permute-start | bytes 196616 | tf_op jit(solution)/shard_map/ppermute | solution.py:28
  10.7 18.5 %copy-start.1 = (s32[16]{0:T(128)S(1)}, s32[16]{0:T(128)}, u32[]{:S(2)}) copy-start(s32[16]{0:T(128)} %group_ref.1) | copy-start | bytes 196
  10.7 18.5 %all-to-all-start = ((bf16[16,16,2048]{2,1,0:T(8,128)(2,1)}), bf16[16,16,2048]{2,1,0:T(8,128)(2,1)S(1)}, u32[]{:S(2)}, u32[]{:S(2)}) async-start(bf16[16,16,2048]{2,1,0:T(8,128)(2,1)} %bitcast.126), calls=%async_computation | async-start | bytes 2097152 | tf_op jit(solution)/shard_map/all_to_all | solution.py:20
  15.9 9.7 %collective-permute-start.1 = (bf16[2,4,4,512]{3,2,0,1:T(4,128)(2,1)S(1)}, bf16[2,4,4,512]{3,2,0,1:T(4,128)(2,1)S(1)}, u32[]{:S(2)}, u32[]{:S(2)}) collective-permute-start(bf16[2,4,4,512]{3,2,0,1:T(4,128)(2,1)S(1)} %pad_maximum_fusion), channel_id=1, source_target_pairs={{0,2},{1,3},{2,0},{3,1},{4,6},{5,7},{6,4},{7,5},{8,10},{9,11},{10,... | collective-permute-start | bytes 98312 | tf_op jit(solution)/shard_map/ppermute | solution.py:28
  19.3 18.9 %collective-permute-start.2 = (bf16[2,4,4,512]{3,2,1,0:T(4,128)(2,1)S(1)}, bf16[2,4,4,512]{3,2,1,0:T(4,128)(2,1)S(1)}, u32[]{:S(2)}, u32[]{:S(2)}) collective-permute-start(bf16[2,4,4,512]{3,2,1,0:T(4,128)(2,1)S(1)} %pad_maximum_fusion.1), channel_id=1, source_target_pairs={{0,4},{1,5},{2,6},{3,7},{4,0},{5,1},{6,2},{7,3},{8,12},{9,13},{10,... | collective-permute-start | bytes 98312 | tf_op jit(solution)/shard_map/ppermute | solution.py:28
  23.3 15.0 %collective-permute-start.3 = (bf16[2,4,4,512]{3,2,0,1:T(4,128)(2,1)S(1)}, bf16[2,4,4,512]{3,2,0,1:T(4,128)(2,1)S(1)}, u32[]{:S(2)}, u32[]{:S(2)}) collective-permute-start(bf16[2,4,4,512]{3,2,0,1:T(4,128)(2,1)S(1)} %pad_maximum_fusion.2), channel_id=1, source_target_pairs={{0,6},{1,7},{2,4},{3,5},{4,2},{5,3},{6,0},{7,1},{8,14},{9,15},{10,... | collective-permute-start | bytes 98312 | tf_op jit(solution)/shard_map/ppermute | solution.py:28
  30.9 28.6 %all-to-all-start.1 = ((bf16[16,16,2048]{2,1,0:T(8,128)(2,1)}), bf16[16,16,2048]{2,1,0:T(8,128)(2,1)}, u32[]{:S(2)}, u32[]{:S(2)}) async-start(bf16[16,16,2048]{2,1,0:T(8,128)(2,1)} %pick.1), calls=%async_computation.1 | async-start | bytes 2097152 | tf_op jit(solution)/shard_map/all_to_all | solution.py:20
  38.3 34.0 %collective-permute-start.4 = (bf16[4,2,4,512]{3,2,1,0:T(4,128)(2,1)S(1)}, bf16[4,2,4,512]{3,2,1,0:T(4,128)(2,1)S(1)}, u32[]{:S(2)}, u32[]{:S(2)}) collective-permute-start(bf16[4,2,4,512]{3,2,1,0:T(4,128)(2,1)S(1)} %pad_maximum_fusion.3), channel_id=1, source_target_pairs={{0,8},{1,9},{2,10},{3,11},{4,12},{5,13},{6,14},{7,15},{8,0},{9,1},... | collective-permute-start | bytes 98312 | tf_op jit(solution)/shard_map/ppermute | solution.py:28
  47.4 24.9 %collective-permute-start.5 = (bf16[4,2,4,512]{3,2,1,0:T(4,128)(2,1)S(1)}, bf16[4,2,4,512]{3,2,1,0:T(4,128)(2,1)S(1)}, u32[]{:S(2)}, u32[]{:S(2)}) collective-permute-start(bf16[4,2,4,512]{3,2,1,0:T(4,128)(2,1)S(1)} %pad_maximum_fusion.4), channel_id=1, source_target_pairs={{0,16},{1,17},{2,18},{3,19},{4,20},{5,21},{6,22},{7,23},{8,24},{9,... | collective-permute-start | bytes 98312 | tf_op jit(solution)/shard_map/ppermute | solution.py:28
  57.5 14.9 %collective-permute-start.6 = (bf16[4,2,4,512]{3,2,1,0:T(4,128)(2,1)S(1)}, bf16[4,2,4,512]{3,2,1,0:T(4,128)(2,1)S(1)}, u32[]{:S(2)}, u32[]{:S(2)}) collective-permute-start(bf16[4,2,4,512]{3,2,1,0:T(4,128)(2,1)S(1)} %pad_maximum_fusion.5), channel_id=1, source_target_pairs={{0,24},{1,25},{2,26},{3,27},{4,28},{5,29},{6,30},{7,31},{8,16},{9,... | collective-permute-start | bytes 98312 | tf_op jit(solution)/shard_map/ppermute | solution.py:28
  59.5 92.2 %all-to-all-start.2 = ((bf16[32,8,2048]{2,1,0:T(8,128)(2,1)}), bf16[32,8,2048]{2,1,0:T(8,128)(2,1)S(1)}, u32[]{:S(2)}, u32[]{:S(2)}) async-start(bf16[32,8,2048]{2,1,0:T(8,128)(2,1)} %bitcast.28.routed_ref), calls=%async_computation.2 | async-start | bytes 2097152 | tf_op jit(solution)/shard_map/all_to_all | solution.py:20
  72.3 28.9 %copy-start.4 = (s32[128]{0:T(128)S(1)}, s32[128]{0:T(128)}, u32[]{:S(2)}) copy-start(s32[128]{0:T(128)} %param.11) | copy-start | bytes 1540
  72.3 64.7 %copy-start.3 = (bf16[16,2048]{1,0:T(8,128)(2,1)S(1)}, bf16[16,2048]{1,0:T(8,128)(2,1)}, u32[]{:S(2)}) copy-start(bf16[16,2048]{1,0:T(8,128)(2,1)} %param.9) | copy-start | bytes 196612
  72.3 74.3 %copy-start.2 = (bf16[16,128,256]{2,1,0:T(8,128)(2,1)S(1)}, bf16[16,128,256]{2,1,0:T(8,128)(2,1)}, u32[]{:S(2)}) copy-start(bf16[16,128,256]{2,1,0:T(8,128)(2,1)} %param.10) | copy-start | bytes 3145732
  74.3 12.0 %collective-permute-start.7 = (f32[8,2,16,256]{3,2,1,0:T(8,128)S(1)}, f32[8,2,16,256]{3,2,1,0:T(8,128)S(1)}, u32[]{:S(2)}, u32[]{:S(2)}) collective-permute-start(f32[8,2,16,256]{3,2,1,0:T(8,128)S(1)} %slice_bitcast_fusion), channel_id=1, source_target_pairs={{0,1},{1,0},{2,3},{3,2},{4,5},{5,4},{6,7},{7,6},{8,9},{9,8},{10,11... | collective-permute-start | bytes 786440 | tf_op jit(solution)/shard_map/ppermute | solution.py:164
  86.3 36.6 %collective-permute-start.10 = (f32[2,16,256]{2,1,0:T(8,128)S(1)}, f32[2,16,256]{2,1,0:T(8,128)S(1)}, u32[]{:S(2)}, u32[]{:S(2)}) collective-permute-start(f32[2,16,256]{2,1,0:T(8,128)S(1)} %get-tuple-element.7), channel_id=1, source_target_pairs={{0,12},{1,13},{2,14},{3,15},{4,8},{5,9},{6,10},{7,11},{8,4},{9,5},... | collective-permute-start | bytes 98312 | tf_op jit(solution)/shard_map/ppermute | solution.py:164
  96.5 38.4 %collective-permute-start.11 = (f32[2,16,256]{2,1,0:T(8,128)S(1)}, f32[2,16,256]{2,1,0:T(8,128)S(1)}, u32[]{:S(2)}, u32[]{:S(2)}) collective-permute-start(f32[2,16,256]{2,1,0:T(8,128)S(1)} %get-tuple-element.6), channel_id=1, source_target_pairs={{0,16},{1,17},{2,18},{3,19},{4,20},{5,21},{6,22},{7,23},{8,24},{9,... | collective-permute-start | bytes 98312 | tf_op jit(solution)/shard_map/ppermute | solution.py:164
  101.3 35.7 %collective-permute-start.12 = (f32[2,16,256]{2,1,0:T(8,128)S(1)}, f32[2,16,256]{2,1,0:T(8,128)S(1)}, u32[]{:S(2)}, u32[]{:S(2)}) collective-permute-start(f32[2,16,256]{2,1,0:T(8,128)S(1)} %get-tuple-element.5), channel_id=1, source_target_pairs={{0,20},{1,21},{2,22},{3,23},{4,16},{5,17},{6,18},{7,19},{8,28},{9,... | collective-permute-start | bytes 98312 | tf_op jit(solution)/shard_map/ppermute | solution.py:164
  107.1 29.9 %collective-permute-start.13 = (f32[2,16,256]{2,1,0:T(8,128)S(1)}, f32[2,16,256]{2,1,0:T(8,128)S(1)}, u32[]{:S(2)}, u32[]{:S(2)}) collective-permute-start(f32[2,16,256]{2,1,0:T(8,128)S(1)} %get-tuple-element.4), channel_id=1, source_target_pairs={{0,24},{1,25},{2,26},{3,27},{4,28},{5,29},{6,30},{7,31},{8,16},{9,... | collective-permute-start | bytes 98312 | tf_op jit(solution)/shard_map/ppermute | solution.py:164
  116.4 20.6 %collective-permute-start.14 = (f32[2,16,256]{2,1,0:T(8,128)S(1)}, f32[2,16,256]{2,1,0:T(8,128)S(1)}, u32[]{:S(2)}, u32[]{:S(2)}) collective-permute-start(f32[2,16,256]{2,1,0:T(8,128)S(1)} %get-tuple-element.3), channel_id=1, source_target_pairs={{0,28},{1,29},{2,30},{3,31},{4,24},{5,25},{6,26},{7,27},{8,20},{9,... | collective-permute-start | bytes 98312 | tf_op jit(solution)/shard_map/ppermute | solution.py:164
  123.0 14.0 %collective-permute-start.8 = (f32[2,16,256]{2,1,0:T(8,128)S(1)}, f32[2,16,256]{2,1,0:T(8,128)S(1)}, u32[]{:S(2)}, u32[]{:S(2)}) collective-permute-start(f32[2,16,256]{2,1,0:T(8,128)S(1)} %get-tuple-element.2), channel_id=1, source_target_pairs={{0,4},{1,5},{2,6},{3,7},{4,0},{5,1},{6,2},{7,3},{8,12},{9,13},{10,... | collective-permute-start | bytes 98312 | tf_op jit(solution)/shard_map/ppermute | solution.py:164
  135.0 9.7 %collective-permute-start.9 = (f32[2,16,256]{2,1,0:T(8,128)S(1)}, f32[2,16,256]{2,1,0:T(8,128)S(1)}, u32[]{:S(2)}, u32[]{:S(2)}) collective-permute-start(f32[2,16,256]{2,1,0:T(8,128)S(1)} %get-tuple-element.8), channel_id=1, source_target_pairs={{0,8},{1,9},{2,10},{3,11},{4,12},{5,13},{6,14},{7,15},{8,0},{9,1},... | collective-permute-start | bytes 98312 | tf_op jit(solution)/shard_map/ppermute | solution.py:164
  144.7 5.6 %collective-permute-start.15 = (f32[16,256]{1,0:T(8,128)S(1)}, f32[16,256]{1,0:T(8,128)S(1)}, u32[]{:S(2)}, u32[]{:S(2)}) collective-permute-start(f32[16,256]{1,0:T(8,128)S(1)} %slice_bitcast_fusion.10), channel_id=1, source_target_pairs={{0,2},{1,3},{2,0},{3,1},{4,6},{5,7},{6,4},{7,5},{8,10},{9,11},{10,... | collective-permute-start | bytes 49160 | tf_op jit(solution)/shard_map/ppermute | solution.py:164

commit v8 on v7

--- a/solution.py
+++ b/solution.py
@@ -34,7 +34,8 @@
     near = [jnp.stack([v[k] for v in side]) for k in range(4)]
     near = [near[0]] + [send(near[k], k << 1) for k in range(1, 4)]
     far = [jnp.stack([v[:, k] for v in near]) for k in range(4)]
-    far = [far[0]] + [send(far[k], k << 3) for k in range(1, 4)]
+    for k in (2, 1, 3):
+        far[k] = send(far[k], k << 3)
     return jnp.concatenate(far).reshape((shards,) + blocks.shape[1:])
 
 
@@ -164,8 +165,15 @@
         return lax.ppermute(values, "shard", [(i, i ^ bits) for i in range(shards)])
 
     partial = partial[0] + send(partial[1], 1)
-    arrived = [send(partial[k], k << 2) for k in range(1, 8)]
-    partial = sum(arrived, partial[0])
+    head = lax.reduce_precision(partial[1:], 8, 7)
+    rest = partial[1:, :, :, :HD] - head[:, :, :, :HD]
+    halves = jnp.concatenate([head, rest], axis=-1).astype(jnp.bfloat16)
+    arrived = {}
+    for k in (4, 5, 3, 6, 2, 7, 1):
+        arrived[k] = send(halves[k - 1], k << 2)
+    total = sum(v.astype(jnp.float32) for v in arrived.values())
+    keys = total[:, :, :HD] + total[:, :, 2 * HD :]
+    partial = partial[0] + jnp.concatenate([keys, total[:, :, HD : 2 * HD]], axis=-1)
     partial = partial[0] + send(partial[1], 1 << 1)
     return partial
 

time: 154 us -> 171 us (1.11)
  the two profiles are of different devices: /device:TPU:40 before, /device:TPU:24 now
where the time goes in v8:
time: 171 us; the launch traced here: 170 us
  starting transfers between devices  102 us (60%)
  waiting for transfers between devices  54.8 us (32%)
  Pallas kernels  6.97 us (4%)
  local copies, waits for them, and re-layouts  3.62 us (2%)
    ppermute x16, starting transfers between devices, send(): return lax.ppermute(values, 'shard', [(i, i ^ bits) for i in range(shards)])  77.7 us
    ppermute x16, waiting for transfers between devices, send(): return lax.ppermute(values, 'shard', [(i, i ^ bits) for i in range(shards)])  40.4 us
    all_to_all x3, starting transfers between devices, exchange(): return lax.all_to_all(blocks, axis, split_axis=0, concat_axis=0, tiled=True)  23.9 us
    all_to_all x3, waiting for transfers between devices, exchange(): return lax.all_to_all(blocks, axis, split_axis=0, concat_axis=0, tiled=True)  14.4 us
    pallas_call x1, Pallas kernels, flip(): pl.pallas_call(flip_kernel, grid=(depth // rows,), in_specs=[pl.BlockSpec...  3.53 us
  transfers between devices with their start and end apart: 19, of which 8 were waited for; matrix products, arithmetic and copies ran while one was open for 1% of the time, Pallas kernels for 4%

profile of v8, /device:TPU:24, one launch (start us, length us, event | category | flops | bytes accessed | tf_op | source)
XLA Modules:
  0.0 169.7 jit_solution(1526246768939374832)
XLA Ops:
  0.6 0.0 copy-start
  0.7 0.1 xor.18
  0.8 0.8 copy-done
  1.5 0.7 gather_fusion
  2.3 4.9 %collective-permute-start = (bf16[4,4,4,512]{3,2,0,1:T(4,128)(2,1)S(1)}, bf16[4,4,4,512]{3,2,0,1:T(4,128)(2,1)S(1)}, u32[]{:S(2)}, u32[]{:S(2)}) collective-permute-start(bf16[4,4,4,512]{3,2,0,1:T(4,128)(2,1)S(1)} %copy.19), channel_id=1, source_target_pairs={{0,1},{1,0},{2,3},{3,2},{4,5},{5,4},{6,7},{7,6},{8,9},{9,8},{10,11... | collective-permute-start | bytes 196616 | tf_op jit(solution)/shard_map/ppermute | solution.py:28
  7.2 3.5 %flip.1 = bf16[32,8,2048]{2,1,0:T(8,128)(2,1)} custom-call(f32[1,512,1024]{2,1,0:T(8,128)} %weights_ref.1), custom_call_target="tpu_custom_call" | custom-call | flops 2000000 | bytes 3000000 | tf_op jit(solution)/shard_map/flip/pallas_call | solution.py:90
  10.8 6.2 %all-to-all-start = ((bf16[16,16,2048]{2,1,0:T(8,128)(2,1)}), bf16[16,16,2048]{2,1,0:T(8,128)(2,1)S(1)}, u32[]{:S(2)}, u32[]{:S(2)}) async-start(bf16[16,16,2048]{2,1,0:T(8,128)(2,1)} %bitcast.114), calls=%async_computation | async-start | bytes 2097152 | tf_op jit(solution)/shard_map/all_to_all | solution.py:20
  16.9 0.0 collective-permute-done
  17.1 2.5 %collective-permute-start.1 = (bf16[2,4,4,512]{3,2,0,1:T(4,128)(2,1)S(1)}, bf16[2,4,4,512]{3,2,0,1:T(4,128)(2,1)S(1)}, u32[]{:S(2)}, u32[]{:S(2)}) collective-permute-start(bf16[2,4,4,512]{3,2,0,1:T(4,128)(2,1)S(1)} %pad_maximum_fusion), channel_id=1, source_target_pairs={{0,2},{1,3},{2,0},{3,1},{4,6},{5,7},{6,4},{7,5},{8,10},{9,11},{10,... | collective-permute-start | bytes 98312 | tf_op jit(solution)/shard_map/ppermute | solution.py:28
  19.6 5.2 %collective-permute-start.2 = (bf16[2,4,4,512]{3,2,1,0:T(4,128)(2,1)S(1)}, bf16[2,4,4,512]{3,2,1,0:T(4,128)(2,1)S(1)}, u32[]{:S(2)}, u32[]{:S(2)}) collective-permute-start(bf16[2,4,4,512]{3,2,1,0:T(4,128)(2,1)S(1)} %pad_maximum_fusion.1), channel_id=1, source_target_pairs={{0,4},{1,5},{2,6},{3,7},{4,0},{5,1},{6,2},{7,3},{8,12},{9,13},{10,... | collective-permute-start | bytes 98312 | tf_op jit(solution)/shard_map/ppermute | solution.py:28
  24.9 2.4 %collective-permute-start.3 = (bf16[2,4,4,512]{3,2,0,1:T(4,128)(2,1)S(1)}, bf16[2,4,4,512]{3,2,0,1:T(4,128)(2,1)S(1)}, u32[]{:S(2)}, u32[]{:S(2)}) collective-permute-start(bf16[2,4,4,512]{3,2,0,1:T(4,128)(2,1)S(1)} %pad_maximum_fusion.2), channel_id=1, source_target_pairs={{0,6},{1,7},{2,4},{3,5},{4,2},{5,3},{6,0},{7,1},{8,14},{9,15},{10,... | collective-permute-start | bytes 98312 | tf_op jit(solution)/shard_map/ppermute | solution.py:28
  27.3 5.1 %collective-permute-done.3 = bf16[2,4,4,512]{3,2,0,1:T(4,128)(2,1)S(1)} collective-permute-done((bf16[2,4,4,512]{3,2,0,1:T(4,128)(2,1)S(1)}, bf16[2,4,4,512]{3,2,0,1:T(4,128)(2,1)S(1)}, u32[]{:S(2)}, u32[]{:S(2)}) %collective-permute-start.3) | collective-permute-done | bytes 32800 | tf_op jit(solution)/shard_map/ppermute | solution.py:28
  32.5 9.1 %collective-permute-start.4 = (bf16[4,2,4,512]{3,2,1,0:T(4,128)(2,1)S(1)}, bf16[4,2,4,512]{3,2,1,0:T(4,128)(2,1)S(1)}, u32[]{:S(2)}, u32[]{:S(2)}) collective-permute-start(bf16[4,2,4,512]{3,2,1,0:T(4,128)(2,1)S(1)} %pad_maximum_fusion.3), channel_id=1, source_target_pairs={{0,8},{1,9},{2,10},{3,11},{4,12},{5,13},{6,14},{7,15},{8,0},{9,1},... | collective-permute-start | bytes 98312 | tf_op jit(solution)/shard_map/ppermute | solution.py:28
  41.7 8.2 %collective-permute-start.5 = (bf16[4,2,4,512]{3,2,1,0:T(4,128)(2,1)S(1)}, bf16[4,2,4,512]{3,2,1,0:T(4,128)(2,1)S(1)}, u32[]{:S(2)}, u32[]{:S(2)}) collective-permute-start(bf16[4,2,4,512]{3,2,1,0:T(4,128)(2,1)S(1)} %pad_maximum_fusion.4), channel_id=1, source_target_pairs={{0,16},{1,17},{2,18},{3,19},{4,20},{5,21},{6,22},{7,23},{8,24},{9,... | collective-permute-start | bytes 98312 | tf_op jit(solution)/shard_map/ppermute | solution.py:28
  49.9 1.9 %collective-permute-start.6 = (bf16[4,2,4,512]{3,2,1,0:T(4,128)(2,1)S(1)}, bf16[4,2,4,512]{3,2,1,0:T(4,128)(2,1)S(1)}, u32[]{:S(2)}, u32[]{:S(2)}) collective-permute-start(bf16[4,2,4,512]{3,2,1,0:T(4,128)(2,1)S(1)} %pad_maximum_fusion.5), channel_id=1, source_target_pairs={{0,24},{1,25},{2,26},{3,27},{4,28},{5,29},{6,30},{7,31},{8,16},{9,... | collective-permute-start | bytes 98312 | tf_op jit(solution)/shard_map/ppermute | solution.py:28
  51.9 1.7 pick.1
  53.5 5.7 %all-to-all-start.1 = ((bf16[16,16,2048]{2,1,0:T(8,128)(2,1)}), bf16[16,16,2048]{2,1,0:T(8,128)(2,1)}, u32[]{:S(2)}, u32[]{:S(2)}) async-start(bf16[16,16,2048]{2,1,0:T(8,128)(2,1)} %pick.1), calls=%async_computation.1 | async-start | bytes 2097152 | tf_op jit(solution)/shard_map/all_to_all | solution.py:20
  59.4 0.3 collective-permute-done.6
  59.7 14.4 %all-to-all-done.1 = bf16[16,16,2048]{2,1,0:T(8,128)(2,1)} async-done(((bf16[16,16,2048]{2,1,0:T(8,128)(2,1)}), bf16[16,16,2048]{2,1,0:T(8,128)(2,1)}, u32[]{:S(2)}, u32[]{:S(2)}) %all-to-all-start.1) | async-done | bytes 1048608 | tf_op jit(solution)/shard_map/all_to_all | solution.py:20
  74.0 12.0 %all-to-all-start.2 = ((bf16[32,8,2048]{2,1,0:T(8,128)(2,1)}), bf16[32,8,2048]{2,1,0:T(8,128)(2,1)S(1)}, u32[]{:S(2)}, u32[]{:S(2)}) async-start(bf16[32,8,2048]{2,1,0:T(8,128)(2,1)} %bitcast.28.routed_ref), calls=%async_computation.2 | async-start | bytes 2097152 | tf_op jit(solution)/shard_map/all_to_all | solution.py:20
  86.1 0.0 copy-start.4
  86.1 0.0 copy-start.3
  86.1 0.0 copy-start.2
  86.1 1.8 %multiply.23 = f32[2,8,2,16,256]{4,3,2,1,0:T(8,128)S(1)} custom-call(s32[1]{0:T(128)} %bitcast.me_ref, bf16[32,4,512]{2,1,0:T(4,128)(2,1)S(1)} %bitcast.113, bf16[32,8,2048]{2,1,0:T(8,128)(2,1)} %bitcast.28.routed_ref), custom_call_target="tpu_custom_call" | custom-call | flops 134217728 | bytes 3000000 | tf_op jit(solution)/shard_map/multiply/pallas_call | solution.py:147
  87.9 5.2 %collective-permute-start.7 = (f32[8,2,16,256]{3,2,1,0:T(8,128)S(1)}, f32[8,2,16,256]{3,2,1,0:T(8,128)S(1)}, u32[]{:S(2)}, u32[]{:S(2)}) collective-permute-start(f32[8,2,16,256]{3,2,1,0:T(8,128)S(1)} %slice_bitcast_fusion), channel_id=1, source_target_pairs={{0,1},{1,0},{2,3},{3,2},{4,5},{5,4},{6,7},{7,6},{8,9},{9,8},{10,11... | collective-permute-start | bytes 786440 | tf_op jit(solution)/shard_map/ppermute | solution.py:165
  93.1 8.1 %collective-permute-done.7 = f32[8,2,16,256]{3,2,1,0:T(8,128)S(1)} collective-permute-done((f32[8,2,16,256]{3,2,1,0:T(8,128)S(1)}, f32[8,2,16,256]{3,2,1,0:T(8,128)S(1)}, u32[]{:S(2)}, u32[]{:S(2)}) %collective-permute-start.7) | collective-permute-done | bytes 262176 | tf_op jit(solution)/shard_map/ppermute | solution.py:165
  101.4 9.2 %collective-permute-start.10 = (bf16[2,16,384]{2,1,0:T(8,128)(2,1)S(1)}, bf16[2,16,384]{2,1,0:T(8,128)(2,1)S(1)}, u32[]{:S(2)}, u32[]{:S(2)}) collective-permute-start(bf16[2,16,384]{2,1,0:T(8,128)(2,1)S(1)} %get-tuple-element.6), channel_id=1, source_target_pairs={{0,12},{1,13},{2,14},{3,15},{4,8},{5,9},{6,10},{7,11},{8,4},{9,5},... | collective-permute-start | bytes 73736 | tf_op jit(solution)/shard_map/ppermute | solution.py:165
  110.5 4.4 %collective-permute-start.11 = (bf16[2,16,384]{2,1,0:T(8,128)(2,1)S(1)}, bf16[2,16,384]{2,1,0:T(8,128)(2,1)S(1)}, u32[]{:S(2)}, u32[]{:S(2)}) collective-permute-start(bf16[2,16,384]{2,1,0:T(8,128)(2,1)S(1)} %get-tuple-element.7), channel_id=1, source_target_pairs={{0,24},{1,25},{2,26},{3,27},{4,28},{5,29},{6,30},{7,31},{8,16},{9,... | collective-permute-start | bytes 73736 | tf_op jit(solution)/shard_map/ppermute | solution.py:165
  115.0 0.1 dynamic_slice.3
  115.0 3.8 %collective-permute-start.12 = (bf16[2,16,384]{2,1,0:T(8,128)(2,1)S(1)}, bf16[2,16,384]{2,1,0:T(8,128)(2,1)S(1)}, u32[]{:S(2)}, u32[]{:S(2)}) collective-permute-start(bf16[2,16,384]{2,1,0:T(8,128)(2,1)S(1)} %get-tuple-element.8), channel_id=1, source_target_pairs={{0,8},{1,9},{2,10},{3,11},{4,12},{5,13},{6,14},{7,15},{8,0},{9,1},... | collective-permute-start | bytes 73736 | tf_op jit(solution)/shard_map/ppermute | solution.py:165
  118.9 2.1 %collective-permute-start.13 = (bf16[2,16,384]{2,1,0:T(8,128)(2,1)S(1)}, bf16[2,16,384]{2,1,0:T(8,128)(2,1)S(1)}, u32[]{:S(2)}, u32[]{:S(2)}) collective-permute-start(bf16[2,16,384]{2,1,0:T(8,128)(2,1)S(1)} %get-tuple-element.10), channel_id=1, source_target_pairs={{0,28},{1,29},{2,30},{3,31},{4,24},{5,25},{6,26},{7,27},{8,20},{9,... | collective-permute-start | bytes 73736 | tf_op jit(solution)/shard_map/ppermute | solution.py:165
  121.0 5.6 %collective-permute-start.14 = (bf16[2,16,384]{2,1,0:T(8,128)(2,1)S(1)}, bf16[2,16,384]{2,1,0:T(8,128)(2,1)S(1)}, u32[]{:S(2)}, u32[]{:S(2)}) collective-permute-start(bf16[2,16,384]{2,1,0:T(8,128)(2,1)S(1)} %get-tuple-element.9), channel_id=1, source_target_pairs={{0,4},{1,5},{2,6},{3,7},{4,0},{5,1},{6,2},{7,3},{8,12},{9,13},{10,... | collective-permute-start | bytes 73736 | tf_op jit(solution)/shard_map/ppermute | solution.py:165
  126.6 13.0 %collective-permute-done.10 = bf16[2,16,384]{2,1,0:T(8,128)(2,1)S(1)} collective-permute-done((bf16[2,16,384]{2,1,0:T(8,128)(2,1)S(1)}, bf16[2,16,384]{2,1,0:T(8,128)(2,1)S(1)}, u32[]{:S(2)}, u32[]{:S(2)}) %collective-permute-start.10) | collective-permute-done | bytes 24608 | tf_op jit(solution)/shard_map/ppermute | solution.py:165
  139.6 9.3 %collective-permute-start.8 = (bf16[2,16,384]{2,1,0:T(8,128)(2,1)S(1)}, bf16[2,16,384]{2,1,0:T(8,128)(2,1)S(1)}, u32[]{:S(2)}, u32[]{:S(2)}) collective-permute-start(bf16[2,16,384]{2,1,0:T(8,128)(2,1)S(1)} %get-tuple-element.4), channel_id=1, source_target_pairs={{0,16},{1,17},{2,18},{3,19},{4,20},{5,21},{6,22},{7,23},{8,24},{9,... | collective-permute-start | bytes 73736 | tf_op jit(solution)/shard_map/ppermute | solution.py:165
  148.9 1.9 %collective-permute-start.9 = (bf16[2,16,384]{2,1,0:T(8,128)(2,1)S(1)}, bf16[2,16,384]{2,1,0:T(8,128)(2,1)S(1)}, u32[]{:S(2)}, u32[]{:S(2)}) collective-permute-start(bf16[2,16,384]{2,1,0:T(8,128)(2,1)S(1)} %get-tuple-element.5), channel_id=1, source_target_pairs={{0,20},{1,21},{2,22},{3,23},{4,16},{5,17},{6,18},{7,19},{8,28},{9,... | collective-permute-start | bytes 73736 | tf_op jit(solution)/shard_map/ppermute | solution.py:165
  150.9 0.1 iota_compare_fusion
  151.0 0.0 collective-permute-done.12
  151.0 0.0 collective-permute-done.13
  151.0 3.1 %collective-permute-done.8 = bf16[2,16,384]{2,1,0:T(8,128)(2,1)S(1)} collective-permute-done((bf16[2,16,384]{2,1,0:T(8,128)(2,1)S(1)}, bf16[2,16,384]{2,1,0:T(8,128)(2,1)S(1)}, u32[]{:S(2)}, u32[]{:S(2)}) %collective-permute-start.8) | collective-permute-done | bytes 24608 | tf_op jit(solution)/shard_map/ppermute | solution.py:165
  154.1 7.5 %collective-permute-done.9 = bf16[2,16,384]{2,1,0:T(8,128)(2,1)S(1)} collective-permute-done((bf16[2,16,384]{2,1,0:T(8,128)(2,1)S(1)}, bf16[2,16,384]{2,1,0:T(8,128)(2,1)S(1)}, u32[]{:S(2)}, u32[]{:S(2)}) %collective-permute-start.9) | collective-permute-done | bytes 24608 | tf_op jit(solution)/shard_map/ppermute | solution.py:165
  161.6 1.9 %collective-permute-start.15 = (f32[16,256]{1,0:T(8,128)S(1)}, f32[16,256]{1,0:T(8,128)S(1)}, u32[]{:S(2)}, u32[]{:S(2)}) collective-permute-start(f32[16,256]{1,0:T(8,128)S(1)} %slice_bitcast_fusion.3), channel_id=1, source_target_pairs={{0,2},{1,3},{2,0},{3,1},{4,6},{5,7},{6,4},{7,5},{8,10},{9,11},{10,... | collective-permute-start | bytes 49160 | tf_op jit(solution)/shard_map/ppermute | solution.py:165
  163.6 0.5 fusion.41
  164.0 3.2 %collective-permute-done.15 = f32[16,256]{1,0:T(8,128)S(1)} collective-permute-done((f32[16,256]{1,0:T(8,128)S(1)}, f32[16,256]{1,0:T(8,128)S(1)}, u32[]{:S(2)}, u32[]{:S(2)}) %collective-permute-start.15) | collective-permute-done | bytes 16416 | tf_op jit(solution)/shard_map/ppermute | solution.py:165
  167.3 0.1 fusion.31
  167.4 0.2 fusion.6
  167.7 0.3 fusion.1
  168.0 0.7 copy.35
  168.6 1.1 copy.24
  (51 shorter events, 0.7 us)
Async XLA Ops:
  0.6 0.9 copy-start
  2.3 14.7 %collective-permute-start = (bf16[4,4,4,512]{3,2,0,1:T(4,128)(2,1)S(1)}, bf16[4,4,4,512]{3,2,0,1:T(4,128)(2,1)S(1)}, u32[]{:S(2)}, u32[]{:S(2)}) collective-permute-start(bf16[4,4,4,512]{3,2,0,1:T(4,128)(2,1)S(1)} %copy.19), channel_id=1, source_target_pairs={{0,1},{1,0},{2,3},{3,2},{4,5},{5,4},{6,7},{7,6},{8,9},{9,8},{10,11... | collective-permute-start | bytes 196616 | tf_op jit(solution)/shard_map/ppermute | solution.py:28
  10.7 41.1 %copy-start.1 = (s32[16]{0:T(128)S(1)}, s32[16]{0:T(128)}, u32[]{:S(2)}) copy-start(s32[16]{0:T(128)} %group_ref.1) | copy-start | bytes 196
  10.8 41.1 %all-to-all-start = ((bf16[16,16,2048]{2,1,0:T(8,128)(2,1)}), bf16[16,16,2048]{2,1,0:T(8,128)(2,1)S(1)}, u32[]{:S(2)}, u32[]{:S(2)}) async-start(bf16[16,16,2048]{2,1,0:T(8,128)(2,1)} %bitcast.114), calls=%async_computation | async-start | bytes 2097152 | tf_op jit(solution)/shard_map/all_to_all | solution.py:20
  17.1 10.2 %collective-permute-start.1 = (bf16[2,4,4,512]{3,2,0,1:T(4,128)(2,1)S(1)}, bf16[2,4,4,512]{3,2,0,1:T(4,128)(2,1)S(1)}, u32[]{:S(2)}, u32[]{:S(2)}) collective-permute-start(bf16[2,4,4,512]{3,2,0,1:T(4,128)(2,1)S(1)} %pad_maximum_fusion), channel_id=1, source_target_pairs={{0,2},{1,3},{2,0},{3,1},{4,6},{5,7},{6,4},{7,5},{8,10},{9,11},{10,... | collective-permute-start | bytes 98312 | tf_op jit(solution)/shard_map/ppermute | solution.py:28
  19.6 7.7 %collective-permute-start.2 = (bf16[2,4,4,512]{3,2,1,0:T(4,128)(2,1)S(1)}, bf16[2,4,4,512]{3,2,1,0:T(4,128)(2,1)S(1)}, u32[]{:S(2)}, u32[]{:S(2)}) collective-permute-start(bf16[2,4,4,512]{3,2,1,0:T(4,128)(2,1)S(1)} %pad_maximum_fusion.1), channel_id=1, source_target_pairs={{0,4},{1,5},{2,6},{3,7},{4,0},{5,1},{6,2},{7,3},{8,12},{9,13},{10,... | collective-permute-start | bytes 98312 | tf_op jit(solution)/shard_map/ppermute | solution.py:28
  24.9 7.6 %collective-permute-start.3 = (bf16[2,4,4,512]{3,2,0,1:T(4,128)(2,1)S(1)}, bf16[2,4,4,512]{3,2,0,1:T(4,128)(2,1)S(1)}, u32[]{:S(2)}, u32[]{:S(2)}) collective-permute-start(bf16[2,4,4,512]{3,2,0,1:T(4,128)(2,1)S(1)} %pad_maximum_fusion.2), channel_id=1, source_target_pairs={{0,6},{1,7},{2,4},{3,5},{4,2},{5,3},{6,0},{7,1},{8,14},{9,15},{10,... | collective-permute-start | bytes 98312 | tf_op jit(solution)/shard_map/ppermute | solution.py:28
  32.5 26.8 %collective-permute-start.4 = (bf16[4,2,4,512]{3,2,1,0:T(4,128)(2,1)S(1)}, bf16[4,2,4,512]{3,2,1,0:T(4,128)(2,1)S(1)}, u32[]{:S(2)}, u32[]{:S(2)}) collective-permute-start(bf16[4,2,4,512]{3,2,1,0:T(4,128)(2,1)S(1)} %pad_maximum_fusion.3), channel_id=1, source_target_pairs={{0,8},{1,9},{2,10},{3,11},{4,12},{5,13},{6,14},{7,15},{8,0},{9,1},... | collective-permute-start | bytes 98312 | tf_op jit(solution)/shard_map/ppermute | solution.py:28
  41.7 17.7 %collective-permute-start.5 = (bf16[4,2,4,512]{3,2,1,0:T(4,128)(2,1)S(1)}, bf16[4,2,4,512]{3,2,1,0:T(4,128)(2,1)S(1)}, u32[]{:S(2)}, u32[]{:S(2)}) collective-permute-start(bf16[4,2,4,512]{3,2,1,0:T(4,128)(2,1)S(1)} %pad_maximum_fusion.4), channel_id=1, source_target_pairs={{0,16},{1,17},{2,18},{3,19},{4,20},{5,21},{6,22},{7,23},{8,24},{9,... | collective-permute-start | bytes 98312 | tf_op jit(solution)/shard_map/ppermute | solution.py:28
  49.9 9.7 %collective-permute-start.6 = (bf16[4,2,4,512]{3,2,1,0:T(4,128)(2,1)S(1)}, bf16[4,2,4,512]{3,2,1,0:T(4,128)(2,1)S(1)}, u32[]{:S(2)}, u32[]{:S(2)}) collective-permute-start(bf16[4,2,4,512]{3,2,1,0:T(4,128)(2,1)S(1)} %pad_maximum_fusion.5), channel_id=1, source_target_pairs={{0,24},{1,25},{2,26},{3,27},{4,28},{5,29},{6,30},{7,31},{8,16},{9,... | collective-permute-start | bytes 98312 | tf_op jit(solution)/shard_map/ppermute | solution.py:28
  53.5 20.5 %all-to-all-start.1 = ((bf16[16,16,2048]{2,1,0:T(8,128)(2,1)}), bf16[16,16,2048]{2,1,0:T(8,128)(2,1)}, u32[]{:S(2)}, u32[]{:S(2)}) async-start(bf16[16,16,2048]{2,1,0:T(8,128)(2,1)} %pick.1), calls=%async_computation.1 | async-start | bytes 2097152 | tf_op jit(solution)/shard_map/all_to_all | solution.py:20
  74.0 94.6 %all-to-all-start.2 = ((bf16[32,8,2048]{2,1,0:T(8,128)(2,1)}), bf16[32,8,2048]{2,1,0:T(8,128)(2,1)S(1)}, u32[]{:S(2)}, u32[]{:S(2)}) async-start(bf16[32,8,2048]{2,1,0:T(8,128)(2,1)} %bitcast.28.routed_ref), calls=%async_computation.2 | async-start | bytes 2097152 | tf_op jit(solution)/shard_map/all_to_all | solution.py:20
  86.1 28.9 %copy-start.4 = (s32[128]{0:T(128)S(1)}, s32[128]{0:T(128)}, u32[]{:S(2)}) copy-start(s32[128]{0:T(128)} %param.11) | copy-start | bytes 1540
  86.1 64.9 %copy-start.3 = (bf16[16,2048]{1,0:T(8,128)(2,1)S(1)}, bf16[16,2048]{1,0:T(8,128)(2,1)}, u32[]{:S(2)}) copy-start(bf16[16,2048]{1,0:T(8,128)(2,1)} %param.9) | copy-start | bytes 196612
  86.1 77.5 %copy-start.2 = (bf16[16,128,256]{2,1,0:T(8,128)(2,1)S(1)}, bf16[16,128,256]{2,1,0:T(8,128)(2,1)}, u32[]{:S(2)}) copy-start(bf16[16,128,256]{2,1,0:T(8,128)(2,1)} %param.10) | copy-start | bytes 3145732
  87.9 13.3 %collective-permute-start.7 = (f32[8,2,16,256]{3,2,1,0:T(8,128)S(1)}, f32[8,2,16,256]{3,2,1,0:T(8,128)S(1)}, u32[]{:S(2)}, u32[]{:S(2)}) collective-permute-start(f32[8,2,16,256]{3,2,1,0:T(8,128)S(1)} %slice_bitcast_fusion), channel_id=1, source_target_pairs={{0,1},{1,0},{2,3},{3,2},{4,5},{5,4},{6,7},{7,6},{8,9},{9,8},{10,11... | collective-permute-start | bytes 786440 | tf_op jit(solution)/shard_map/ppermute | solution.py:165
  101.4 38.3 %collective-permute-start.10 = (bf16[2,16,384]{2,1,0:T(8,128)(2,1)S(1)}, bf16[2,16,384]{2,1,0:T(8,128)(2,1)S(1)}, u32[]{:S(2)}, u32[]{:S(2)}) collective-permute-start(bf16[2,16,384]{2,1,0:T(8,128)(2,1)S(1)} %get-tuple-element.6), channel_id=1, source_target_pairs={{0,12},{1,13},{2,14},{3,15},{4,8},{5,9},{6,10},{7,11},{8,4},{9,5},... | collective-permute-start | bytes 73736 | tf_op jit(solution)/shard_map/ppermute | solution.py:165
  110.5 38.4 %collective-permute-start.11 = (bf16[2,16,384]{2,1,0:T(8,128)(2,1)S(1)}, bf16[2,16,384]{2,1,0:T(8,128)(2,1)S(1)}, u32[]{:S(2)}, u32[]{:S(2)}) collective-permute-start(bf16[2,16,384]{2,1,0:T(8,128)(2,1)S(1)} %get-tuple-element.7), channel_id=1, source_target_pairs={{0,24},{1,25},{2,26},{3,27},{4,28},{5,29},{6,30},{7,31},{8,16},{9,... | collective-permute-start | bytes 73736 | tf_op jit(solution)/shard_map/ppermute | solution.py:165
  115.0 35.9 %collective-permute-start.12 = (bf16[2,16,384]{2,1,0:T(8,128)(2,1)S(1)}, bf16[2,16,384]{2,1,0:T(8,128)(2,1)S(1)}, u32[]{:S(2)}, u32[]{:S(2)}) collective-permute-start(bf16[2,16,384]{2,1,0:T(8,128)(2,1)S(1)} %get-tuple-element.8), channel_id=1, source_target_pairs={{0,8},{1,9},{2,10},{3,11},{4,12},{5,13},{6,14},{7,15},{8,0},{9,1},... | collective-permute-start | bytes 73736 | tf_op jit(solution)/shard_map/ppermute | solution.py:165
  118.9 32.1 %collective-permute-start.13 = (bf16[2,16,384]{2,1,0:T(8,128)(2,1)S(1)}, bf16[2,16,384]{2,1,0:T(8,128)(2,1)S(1)}, u32[]{:S(2)}, u32[]{:S(2)}) collective-permute-start(bf16[2,16,384]{2,1,0:T(8,128)(2,1)S(1)} %get-tuple-element.10), channel_id=1, source_target_pairs={{0,28},{1,29},{2,30},{3,31},{4,24},{5,25},{6,26},{7,27},{8,20},{9,... | collective-permute-start | bytes 73736 | tf_op jit(solution)/shard_map/ppermute | solution.py:165
  121.0 30.0 %collective-permute-start.14 = (bf16[2,16,384]{2,1,0:T(8,128)(2,1)S(1)}, bf16[2,16,384]{2,1,0:T(8,128)(2,1)S(1)}, u32[]{:S(2)}, u32[]{:S(2)}) collective-permute-start(bf16[2,16,384]{2,1,0:T(8,128)(2,1)S(1)} %get-tuple-element.9), channel_id=1, source_target_pairs={{0,4},{1,5},{2,6},{3,7},{4,0},{5,1},{6,2},{7,3},{8,12},{9,13},{10,... | collective-permute-start | bytes 73736 | tf_op jit(solution)/shard_map/ppermute | solution.py:165
  139.6 14.4 %collective-permute-start.8 = (bf16[2,16,384]{2,1,0:T(8,128)(2,1)S(1)}, bf16[2,16,384]{2,1,0:T(8,128)(2,1)S(1)}, u32[]{:S(2)}, u32[]{:S(2)}) collective-permute-start(bf16[2,16,384]{2,1,0:T(8,128)(2,1)S(1)} %get-tuple-element.4), channel_id=1, source_target_pairs={{0,16},{1,17},{2,18},{3,19},{4,20},{5,21},{6,22},{7,23},{8,24},{9,... | collective-permute-start | bytes 73736 | tf_op jit(solution)/shard_map/ppermute | solution.py:165
  148.9 12.6 %collective-permute-start.9 = (bf16[2,16,384]{2,1,0:T(8,128)(2,1)S(1)}, bf16[2,16,384]{2,1,0:T(8,128)(2,1)S(1)}, u32[]{:S(2)}, u32[]{:S(2)}) collective-permute-start(bf16[2,16,384]{2,1,0:T(8,128)(2,1)S(1)} %get-tuple-element.5), channel_id=1, source_target_pairs={{0,20},{1,21},{2,22},{3,23},{4,16},{5,17},{6,18},{7,19},{8,28},{9,... | collective-permute-start | bytes 73736 | tf_op jit(solution)/shard_map/ppermute | solution.py:165
  161.6 5.6 %collective-permute-start.15 = (f32[16,256]{1,0:T(8,128)S(1)}, f32[16,256]{1,0:T(8,128)S(1)}, u32[]{:S(2)}, u32[]{:S(2)}) collective-permute-start(f32[16,256]{1,0:T(8,128)S(1)} %slice_bitcast_fusion.3), channel_id=1, source_target_pairs={{0,2},{1,3},{2,0},{3,1},{4,6},{5,7},{6,4},{7,5},{8,10},{9,11},{10,... | collective-permute-start | bytes 49160 | tf_op jit(solution)/shard_map/ppermute | solution.py:165

commit v9 on v8

--- a/solution.py
+++ b/solution.py
@@ -14,6 +14,7 @@
 KVH = 4
 LEN = 128
 ROWS = 128
+ROW_TILE = 128
 
 
 def exchange(blocks, axis):
@@ -73,25 +74,22 @@
 
 
 def flip_kernel(weights_ref, out_ref):
-    step = pl.program_id(0)
     shards, piece, width = out_ref.shape
-    rows = weights_ref.shape[1]
+    rows = width // KVH
+    columns = shards * piece
     for h in range(KVH):
-        lanes = pl.ds(pl.multiple_of(h * (width // KVH) + step * rows, rows), rows)
-        columns = shards * piece
         block = weights_ref[0, :, h * columns : (h + 1) * columns].astype(jnp.bfloat16)
-        out_ref[:, :, lanes] = block.T.reshape(shards, piece, rows)
+        out_ref[:, :, h * rows : (h + 1) * rows] = block.T.reshape(shards, piece, rows)
 
 
 def flip(weights, shards):
     _, depth, columns = weights.shape
     piece = columns // KVH // shards
-    rows = 128
     return pl.pallas_call(
         flip_kernel,
-        grid=(depth // rows,),
-        in_specs=[pl.BlockSpec((1, rows, columns), lambda i: (0, i, 0))],
-        out_specs=VMEM,
+        grid=(depth // ROW_TILE,),
+        in_specs=[pl.BlockSpec((1, ROW_TILE, columns), lambda i: (0, i, 0))],
+        out_specs=pl.BlockSpec((shards, piece, KVH * ROW_TILE), lambda i: (0, 0, i)),
         out_shape=jax.ShapeDtypeStruct((shards, piece, KVH * depth), jnp.bfloat16),
         cost_estimate=pl.CostEstimate(flops=2_000_000, bytes_accessed=3_000_000, transcendentals=0),
         compiler_params=pltpu.CompilerParams(vmem_limit_bytes=62 * 1024 * 1024),
@@ -99,22 +97,26 @@
     )(weights)
 
 
-def pick_kernel(group_ref, spread_ref, out_ref):
-    def move(s, carry):
-        out_ref[group_ref[s]] = spread_ref[s]
-        return carry
-
-    lax.fori_loop(0, spread_ref.shape[0], move, 0)
+def pick_kernel(group_ref, spread_ref, out_ref, sems):
+    copies = [
+        pltpu.make_async_copy(spread_ref.at[s], out_ref.at[group_ref[s]], sems.at[s])
+        for s in range(spread_ref.shape[0])
+    ]
+    for copy in copies:
+        copy.start()
+    for copy in copies:
+        copy.wait()
 
 
 def pick(section_to_group, spread):
     return pl.pallas_call(
         pick_kernel,
         in_specs=[pl.BlockSpec(memory_space=pltpu.SMEM), VMEM],
-        out_specs=VMEM,
+        out_specs=pl.BlockSpec(memory_space=pltpu.HBM),
         out_shape=jax.ShapeDtypeStruct(spread.shape, spread.dtype),
+        scratch_shapes=[pltpu.SemaphoreType.DMA((spread.shape[0],))],
+        compiler_params=pltpu.CompilerParams(vmem_limit_bytes=12 * 1024 * 1024),
         cost_estimate=pl.CostEstimate(flops=1_000_000, bytes_accessed=2_000_000, transcendentals=0),
-        compiler_params=pltpu.CompilerParams(vmem_limit_bytes=12 * 1024 * 1024),
         name="pick",
     )(section_to_group, spread)
 
@@ -130,9 +132,13 @@
         rows_ref[d * own : (d + 1) * own, :] = inputs_ref[me ^ d].astype(jnp.float32)
     inputs = rows_ref[...].astype(jnp.bfloat16)
     for h in range(heads):
+        tiles = [
+            routed_ref[:, :, (i * heads + h) * ROW_TILE : (i * heads + h + 1) * ROW_TILE]
+            for i in range(depth // ROW_TILE)
+        ]
         product = lax.dot_general(
             inputs,
-            routed_ref[:, :, h * depth : (h + 1) * depth].reshape(shards * piece, depth),
+            jnp.concatenate(tiles, axis=-1).reshape(shards * piece, depth),
             (((1,), (1,)), ((), ())),
             preferred_element_type=jnp.float32,
         )
@@ -194,8 +200,8 @@
     routed = exchange(picked, "section").reshape(shards, piece_cols, KVH * slice_rows)
     me = lax.axis_index("shard").astype(jnp.int32).reshape(1)
     received = exchange(routed, "shard")
-    layer_out = received.reshape(shards, piece_cols, KVH, slice_rows)
-    layer_out = layer_out.transpose(2, 1, 0, 3).reshape(1, KVH, piece_cols, D)
+    layer_out = received.reshape(shards, piece_cols, -1, KVH, ROW_TILE)
+    layer_out = layer_out.transpose(3, 1, 0, 2, 4).reshape(1, KVH, piece_cols, D)
     fresh = reduce_rows(multiply(me, inputs, routed)).astype(jnp.bfloat16)
     block_index = lax.axis_index("shard") % per_head
     row_lengths = lax.dynamic_slice_in_dim(lengths, block_index * row_block, row_block, 0)

time: 171 us -> 171 us (level)
  no operation moved by 1% of the time
where the time goes in v9:
time: 171 us; the launch traced here: 170 us
  starting transfers between devices  102 us (60%)
  waiting for transfers between devices  54.7 us (32%)
  Pallas kernels  7.22 us (4%)
  local copies, waits for them, and re-layouts  3.73 us (2%)
    ppermute x16, starting transfers between devices, send(): return lax.ppermute(values, 'shard', [(i, i ^ bits) for i in range(shards)])  77.7 us
    ppermute x16, waiting for transfers between devices, send(): return lax.ppermute(values, 'shard', [(i, i ^ bits) for i in range(shards)])  40.4 us
    all_to_all x3, starting transfers between devices, exchange(): return lax.all_to_all(blocks, axis, split_axis=0, concat_axis=0, tiled=True)  23.9 us
    all_to_all x3, waiting for transfers between devices, exchange(): return lax.all_to_all(blocks, axis, split_axis=0, concat_axis=0, tiled=True)  14.4 us
    pallas_call x1, Pallas kernels, flip(): pl.pallas_call(flip_kernel, grid=(depth // ROW_TILE,), in_specs=[pl.Block...  3.78 us
  transfers between devices with their start and end apart: 19, of which 8 were waited for; matrix products, arithmetic and copies ran while one was open for 1% of the time, Pallas kernels for 4%

profile of v9, /device:TPU:24, one launch (start us, length us, event | category | flops | bytes accessed | tf_op | source)
XLA Modules:
  0.0 170.1 jit_solution(939323438239965818)
XLA Ops:
  0.6 0.0 copy-start
  0.7 0.1 xor.18
  0.8 0.8 copy-done
  1.5 0.7 gather_fusion
  2.3 4.9 %collective-permute-start = (bf16[4,4,4,512]{3,2,0,1:T(4,128)(2,1)S(1)}, bf16[4,4,4,512]{3,2,0,1:T(4,128)(2,1)S(1)}, u32[]{:S(2)}, u32[]{:S(2)}) collective-permute-start(bf16[4,4,4,512]{3,2,0,1:T(4,128)(2,1)S(1)} %copy.19), channel_id=1, source_target_pairs={{0,1},{1,0},{2,3},{3,2},{4,5},{5,4},{6,7},{7,6},{8,9},{9,8},{10,11... | collective-permute-start | bytes 196616 | tf_op jit(solution)/shard_map/ppermute | solution.py:29
  7.2 3.8 %flip.1 = bf16[32,8,2048]{2,1,0:T(8,128)(2,1)} custom-call(f32[1,512,1024]{2,1,0:T(8,128)} %weights_ref.1), custom_call_target="tpu_custom_call" | custom-call | flops 2000000 | bytes 3000000 | tf_op jit(solution)/shard_map/flip/pallas_call | solution.py:88
  11.0 6.2 %all-to-all-start = ((bf16[16,16,2048]{2,1,0:T(8,128)(2,1)}), bf16[16,16,2048]{2,1,0:T(8,128)(2,1)S(1)}, u32[]{:S(2)}, u32[]{:S(2)}) async-start(bf16[16,16,2048]{2,1,0:T(8,128)(2,1)} %bitcast.114), calls=%async_computation | async-start | bytes 2097152 | tf_op jit(solution)/shard_map/all_to_all | solution.py:21
  17.3 2.5 %collective-permute-start.1 = (bf16[2,4,4,512]{3,2,0,1:T(4,128)(2,1)S(1)}, bf16[2,4,4,512]{3,2,0,1:T(4,128)(2,1)S(1)}, u32[]{:S(2)}, u32[]{:S(2)}) collective-permute-start(bf16[2,4,4,512]{3,2,0,1:T(4,128)(2,1)S(1)} %pad_maximum_fusion), channel_id=1, source_target_pairs={{0,2},{1,3},{2,0},{3,1},{4,6},{5,7},{6,4},{7,5},{8,10},{9,11},{10,... | collective-permute-start | bytes 98312 | tf_op jit(solution)/shard_map/ppermute | solution.py:29
  19.9 5.2 %collective-permute-start.2 = (bf16[2,4,4,512]{3,2,1,0:T(4,128)(2,1)S(1)}, bf16[2,4,4,512]{3,2,1,0:T(4,128)(2,1)S(1)}, u32[]{:S(2)}, u32[]{:S(2)}) collective-permute-start(bf16[2,4,4,512]{3,2,1,0:T(4,128)(2,1)S(1)} %pad_maximum_fusion.1), channel_id=1, source_target_pairs={{0,4},{1,5},{2,6},{3,7},{4,0},{5,1},{6,2},{7,3},{8,12},{9,13},{10,... | collective-permute-start | bytes 98312 | tf_op jit(solution)/shard_map/ppermute | solution.py:29
  25.1 2.4 %collective-permute-start.3 = (bf16[2,4,4,512]{3,2,0,1:T(4,128)(2,1)S(1)}, bf16[2,4,4,512]{3,2,0,1:T(4,128)(2,1)S(1)}, u32[]{:S(2)}, u32[]{:S(2)}) collective-permute-start(bf16[2,4,4,512]{3,2,0,1:T(4,128)(2,1)S(1)} %pad_maximum_fusion.2), channel_id=1, source_target_pairs={{0,6},{1,7},{2,4},{3,5},{4,2},{5,3},{6,0},{7,1},{8,14},{9,15},{10,... | collective-permute-start | bytes 98312 | tf_op jit(solution)/shard_map/ppermute | solution.py:29
  27.5 0.0 collective-permute-done.1
  27.6 0.0 collective-permute-done.2
  27.6 5.1 %collective-permute-done.3 = bf16[2,4,4,512]{3,2,0,1:T(4,128)(2,1)S(1)} collective-permute-done((bf16[2,4,4,512]{3,2,0,1:T(4,128)(2,1)S(1)}, bf16[2,4,4,512]{3,2,0,1:T(4,128)(2,1)S(1)}, u32[]{:S(2)}, u32[]{:S(2)}) %collective-permute-start.3) | collective-permute-done | bytes 32800 | tf_op jit(solution)/shard_map/ppermute | solution.py:29
  32.8 9.1 %collective-permute-start.4 = (bf16[4,2,4,512]{3,2,1,0:T(4,128)(2,1)S(1)}, bf16[4,2,4,512]{3,2,1,0:T(4,128)(2,1)S(1)}, u32[]{:S(2)}, u32[]{:S(2)}) collective-permute-start(bf16[4,2,4,512]{3,2,1,0:T(4,128)(2,1)S(1)} %pad_maximum_fusion.3), channel_id=1, source_target_pairs={{0,8},{1,9},{2,10},{3,11},{4,12},{5,13},{6,14},{7,15},{8,0},{9,1},... | collective-permute-start | bytes 98312 | tf_op jit(solution)/shard_map/ppermute | solution.py:29
  41.9 8.2 %collective-permute-start.5 = (bf16[4,2,4,512]{3,2,1,0:T(4,128)(2,1)S(1)}, bf16[4,2,4,512]{3,2,1,0:T(4,128)(2,1)S(1)}, u32[]{:S(2)}, u32[]{:S(2)}) collective-permute-start(bf16[4,2,4,512]{3,2,1,0:T(4,128)(2,1)S(1)} %pad_maximum_fusion.4), channel_id=1, source_target_pairs={{0,16},{1,17},{2,18},{3,19},{4,20},{5,21},{6,22},{7,23},{8,24},{9,... | collective-permute-start | bytes 98312 | tf_op jit(solution)/shard_map/ppermute | solution.py:29
  50.2 1.9 %collective-permute-start.6 = (bf16[4,2,4,512]{3,2,1,0:T(4,128)(2,1)S(1)}, bf16[4,2,4,512]{3,2,1,0:T(4,128)(2,1)S(1)}, u32[]{:S(2)}, u32[]{:S(2)}) collective-permute-start(bf16[4,2,4,512]{3,2,1,0:T(4,128)(2,1)S(1)} %pad_maximum_fusion.5), channel_id=1, source_target_pairs={{0,24},{1,25},{2,26},{3,27},{4,28},{5,29},{6,30},{7,31},{8,16},{9,... | collective-permute-start | bytes 98312 | tf_op jit(solution)/shard_map/ppermute | solution.py:29
  52.1 0.0 all-to-all-done.spread_ref
  52.1 1.6 pick.1
  53.8 5.7 %all-to-all-start.1 = ((bf16[16,16,2048]{2,1,0:T(8,128)(2,1)}), bf16[16,16,2048]{2,1,0:T(8,128)(2,1)}, u32[]{:S(2)}, u32[]{:S(2)}) async-start(bf16[16,16,2048]{2,1,0:T(8,128)(2,1)} %pick.1), calls=%async_computation.1 | async-start | bytes 2097152 | tf_op jit(solution)/shard_map/all_to_all | solution.py:21
  59.6 0.3 collective-permute-done.6
  59.9 14.4 %all-to-all-done.1 = bf16[16,16,2048]{2,1,0:T(8,128)(2,1)} async-done(((bf16[16,16,2048]{2,1,0:T(8,128)(2,1)}), bf16[16,16,2048]{2,1,0:T(8,128)(2,1)}, u32[]{:S(2)}, u32[]{:S(2)}) %all-to-all-start.1) | async-done | bytes 1048608 | tf_op jit(solution)/shard_map/all_to_all | solution.py:21
  74.3 12.0 %all-to-all-start.2 = ((bf16[32,8,2048]{2,1,0:T(8,128)(2,1)}), bf16[32,8,2048]{2,1,0:T(8,128)(2,1)S(1)}, u32[]{:S(2)}, u32[]{:S(2)}) async-start(bf16[32,8,2048]{2,1,0:T(8,128)(2,1)} %bitcast.28.routed_ref), calls=%async_computation.2 | async-start | bytes 2097152 | tf_op jit(solution)/shard_map/all_to_all | solution.py:21
  86.3 0.0 copy-start.4
  86.3 0.0 copy-start.3
  86.3 0.0 copy-start.2
  86.3 1.8 %multiply.23 = f32[2,8,2,16,256]{4,3,2,1,0:T(8,128)S(1)} custom-call(s32[1]{0:T(128)} %bitcast.me_ref, bf16[32,4,512]{2,1,0:T(4,128)(2,1)S(1)} %bitcast.113, bf16[32,8,2048]{2,1,0:T(8,128)(2,1)} %bitcast.28.routed_ref), custom_call_target="tpu_custom_call" | custom-call | flops 134217728 | bytes 3000000 | tf_op jit(solution)/shard_map/multiply/pallas_call | solution.py:153
  88.2 5.2 %collective-permute-start.7 = (f32[8,2,16,256]{3,2,1,0:T(8,128)S(1)}, f32[8,2,16,256]{3,2,1,0:T(8,128)S(1)}, u32[]{:S(2)}, u32[]{:S(2)}) collective-permute-start(f32[8,2,16,256]{3,2,1,0:T(8,128)S(1)} %slice_bitcast_fusion), channel_id=1, source_target_pairs={{0,1},{1,0},{2,3},{3,2},{4,5},{5,4},{6,7},{7,6},{8,9},{9,8},{10,11... | collective-permute-start | bytes 786440 | tf_op jit(solution)/shard_map/ppermute | solution.py:171
  93.4 8.1 %collective-permute-done.7 = f32[8,2,16,256]{3,2,1,0:T(8,128)S(1)} collective-permute-done((f32[8,2,16,256]{3,2,1,0:T(8,128)S(1)}, f32[8,2,16,256]{3,2,1,0:T(8,128)S(1)}, u32[]{:S(2)}, u32[]{:S(2)}) %collective-permute-start.7) | collective-permute-done | bytes 262176 | tf_op jit(solution)/shard_map/ppermute | solution.py:171
  101.6 9.2 %collective-permute-start.10 = (bf16[2,16,384]{2,1,0:T(8,128)(2,1)S(1)}, bf16[2,16,384]{2,1,0:T(8,128)(2,1)S(1)}, u32[]{:S(2)}, u32[]{:S(2)}) collective-permute-start(bf16[2,16,384]{2,1,0:T(8,128)(2,1)S(1)} %get-tuple-element.6), channel_id=1, source_target_pairs={{0,12},{1,13},{2,14},{3,15},{4,8},{5,9},{6,10},{7,11},{8,4},{9,5},... | collective-permute-start | bytes 73736 | tf_op jit(solution)/shard_map/ppermute | solution.py:171
  110.8 4.4 %collective-permute-start.11 = (bf16[2,16,384]{2,1,0:T(8,128)(2,1)S(1)}, bf16[2,16,384]{2,1,0:T(8,128)(2,1)S(1)}, u32[]{:S(2)}, u32[]{:S(2)}) collective-permute-start(bf16[2,16,384]{2,1,0:T(8,128)(2,1)S(1)} %get-tuple-element.7), channel_id=1, source_target_pairs={{0,24},{1,25},{2,26},{3,27},{4,28},{5,29},{6,30},{7,31},{8,16},{9,... | collective-permute-start | bytes 73736 | tf_op jit(solution)/shard_map/ppermute | solution.py:171
  115.2 0.1 dynamic_slice.3
  115.3 3.8 %collective-permute-start.12 = (bf16[2,16,384]{2,1,0:T(8,128)(2,1)S(1)}, bf16[2,16,384]{2,1,0:T(8,128)(2,1)S(1)}, u32[]{:S(2)}, u32[]{:S(2)}) collective-permute-start(bf16[2,16,384]{2,1,0:T(8,128)(2,1)S(1)} %get-tuple-element.8), channel_id=1, source_target_pairs={{0,8},{1,9},{2,10},{3,11},{4,12},{5,13},{6,14},{7,15},{8,0},{9,1},... | collective-permute-start | bytes 73736 | tf_op jit(solution)/shard_map/ppermute | solution.py:171
  119.1 2.1 %collective-permute-start.13 = (bf16[2,16,384]{2,1,0:T(8,128)(2,1)S(1)}, bf16[2,16,384]{2,1,0:T(8,128)(2,1)S(1)}, u32[]{:S(2)}, u32[]{:S(2)}) collective-permute-start(bf16[2,16,384]{2,1,0:T(8,128)(2,1)S(1)} %get-tuple-element.10), channel_id=1, source_target_pairs={{0,28},{1,29},{2,30},{3,31},{4,24},{5,25},{6,26},{7,27},{8,20},{9,... | collective-permute-start | bytes 73736 | tf_op jit(solution)/shard_map/ppermute | solution.py:171
  121.2 5.6 %collective-permute-start.14 = (bf16[2,16,384]{2,1,0:T(8,128)(2,1)S(1)}, bf16[2,16,384]{2,1,0:T(8,128)(2,1)S(1)}, u32[]{:S(2)}, u32[]{:S(2)}) collective-permute-start(bf16[2,16,384]{2,1,0:T(8,128)(2,1)S(1)} %get-tuple-element.9), channel_id=1, source_target_pairs={{0,4},{1,5},{2,6},{3,7},{4,0},{5,1},{6,2},{7,3},{8,12},{9,13},{10,... | collective-permute-start | bytes 73736 | tf_op jit(solution)/shard_map/ppermute | solution.py:171
  126.9 13.0 %collective-permute-done.10 = bf16[2,16,384]{2,1,0:T(8,128)(2,1)S(1)} collective-permute-done((bf16[2,16,384]{2,1,0:T(8,128)(2,1)S(1)}, bf16[2,16,384]{2,1,0:T(8,128)(2,1)S(1)}, u32[]{:S(2)}, u32[]{:S(2)}) %collective-permute-start.10) | collective-permute-done | bytes 24608 | tf_op jit(solution)/shard_map/ppermute | solution.py:171
  139.9 9.3 %collective-permute-start.8 = (bf16[2,16,384]{2,1,0:T(8,128)(2,1)S(1)}, bf16[2,16,384]{2,1,0:T(8,128)(2,1)S(1)}, u32[]{:S(2)}, u32[]{:S(2)}) collective-permute-start(bf16[2,16,384]{2,1,0:T(8,128)(2,1)S(1)} %get-tuple-element.4), channel_id=1, source_target_pairs={{0,16},{1,17},{2,18},{3,19},{4,20},{5,21},{6,22},{7,23},{8,24},{9,... | collective-permute-start | bytes 73736 | tf_op jit(solution)/shard_map/ppermute | solution.py:171
  149.2 1.9 %collective-permute-start.9 = (bf16[2,16,384]{2,1,0:T(8,128)(2,1)S(1)}, bf16[2,16,384]{2,1,0:T(8,128)(2,1)S(1)}, u32[]{:S(2)}, u32[]{:S(2)}) collective-permute-start(bf16[2,16,384]{2,1,0:T(8,128)(2,1)S(1)} %get-tuple-element.5), channel_id=1, source_target_pairs={{0,20},{1,21},{2,22},{3,23},{4,16},{5,17},{6,18},{7,19},{8,28},{9,... | collective-permute-start | bytes 73736 | tf_op jit(solution)/shard_map/ppermute | solution.py:171
  151.1 0.1 iota_compare_fusion
  151.2 3.1 %collective-permute-done.8 = bf16[2,16,384]{2,1,0:T(8,128)(2,1)S(1)} collective-permute-done((bf16[2,16,384]{2,1,0:T(8,128)(2,1)S(1)}, bf16[2,16,384]{2,1,0:T(8,128)(2,1)S(1)}, u32[]{:S(2)}, u32[]{:S(2)}) %collective-permute-start.8) | collective-permute-done | bytes 24608 | tf_op jit(solution)/shard_map/ppermute | solution.py:171
  154.3 7.5 %collective-permute-done.9 = bf16[2,16,384]{2,1,0:T(8,128)(2,1)S(1)} collective-permute-done((bf16[2,16,384]{2,1,0:T(8,128)(2,1)S(1)}, bf16[2,16,384]{2,1,0:T(8,128)(2,1)S(1)}, u32[]{:S(2)}, u32[]{:S(2)}) %collective-permute-start.9) | collective-permute-done | bytes 24608 | tf_op jit(solution)/shard_map/ppermute | solution.py:171
  161.9 1.9 %collective-permute-start.15 = (f32[16,256]{1,0:T(8,128)S(1)}, f32[16,256]{1,0:T(8,128)S(1)}, u32[]{:S(2)}, u32[]{:S(2)}) collective-permute-start(f32[16,256]{1,0:T(8,128)S(1)} %slice_bitcast_fusion.3), channel_id=1, source_target_pairs={{0,2},{1,3},{2,0},{3,1},{4,6},{5,7},{6,4},{7,5},{8,10},{9,11},{10,... | collective-permute-start | bytes 49160 | tf_op jit(solution)/shard_map/ppermute | solution.py:171
  163.8 0.5 fusion.41
  164.3 3.2 %collective-permute-done.15 = f32[16,256]{1,0:T(8,128)S(1)} collective-permute-done((f32[16,256]{1,0:T(8,128)S(1)}, f32[16,256]{1,0:T(8,128)S(1)}, u32[]{:S(2)}, u32[]{:S(2)}) %collective-permute-start.15) | collective-permute-done | bytes 16416 | tf_op jit(solution)/shard_map/ppermute | solution.py:171
  167.5 0.1 fusion.31
  167.7 0.2 fusion.6
  167.9 0.3 fusion.1
  168.2 0.7 copy.35
  168.9 1.2 copy.24
  (51 shorter events, 0.7 us)
Async XLA Ops:
  0.6 0.9 copy-start
  2.3 14.9 %collective-permute-start = (bf16[4,4,4,512]{3,2,0,1:T(4,128)(2,1)S(1)}, bf16[4,4,4,512]{3,2,0,1:T(4,128)(2,1)S(1)}, u32[]{:S(2)}, u32[]{:S(2)}) collective-permute-start(bf16[4,4,4,512]{3,2,0,1:T(4,128)(2,1)S(1)} %copy.19), channel_id=1, source_target_pairs={{0,1},{1,0},{2,3},{3,2},{4,5},{5,4},{6,7},{7,6},{8,9},{9,8},{10,11... | collective-permute-start | bytes 196616 | tf_op jit(solution)/shard_map/ppermute | solution.py:29
  11.0 41.1 %copy-start.1 = (s32[16]{0:T(128)S(1)}, s32[16]{0:T(128)}, u32[]{:S(2)}) copy-start(s32[16]{0:T(128)} %group_ref.1) | copy-start | bytes 196
  11.0 41.1 %all-to-all-start = ((bf16[16,16,2048]{2,1,0:T(8,128)(2,1)}), bf16[16,16,2048]{2,1,0:T(8,128)(2,1)S(1)}, u32[]{:S(2)}, u32[]{:S(2)}) async-start(bf16[16,16,2048]{2,1,0:T(8,128)(2,1)} %bitcast.114), calls=%async_computation | async-start | bytes 2097152 | tf_op jit(solution)/shard_map/all_to_all | solution.py:21
  17.3 10.2 %collective-permute-start.1 = (bf16[2,4,4,512]{3,2,0,1:T(4,128)(2,1)S(1)}, bf16[2,4,4,512]{3,2,0,1:T(4,128)(2,1)S(1)}, u32[]{:S(2)}, u32[]{:S(2)}) collective-permute-start(bf16[2,4,4,512]{3,2,0,1:T(4,128)(2,1)S(1)} %pad_maximum_fusion), channel_id=1, source_target_pairs={{0,2},{1,3},{2,0},{3,1},{4,6},{5,7},{6,4},{7,5},{8,10},{9,11},{10,... | collective-permute-start | bytes 98312 | tf_op jit(solution)/shard_map/ppermute | solution.py:29
  19.9 7.7 %collective-permute-start.2 = (bf16[2,4,4,512]{3,2,1,0:T(4,128)(2,1)S(1)}, bf16[2,4,4,512]{3,2,1,0:T(4,128)(2,1)S(1)}, u32[]{:S(2)}, u32[]{:S(2)}) collective-permute-start(bf16[2,4,4,512]{3,2,1,0:T(4,128)(2,1)S(1)} %pad_maximum_fusion.1), channel_id=1, source_target_pairs={{0,4},{1,5},{2,6},{3,7},{4,0},{5,1},{6,2},{7,3},{8,12},{9,13},{10,... | collective-permute-start | bytes 98312 | tf_op jit(solution)/shard_map/ppermute | solution.py:29
  25.1 7.6 %collective-permute-start.3 = (bf16[2,4,4,512]{3,2,0,1:T(4,128)(2,1)S(1)}, bf16[2,4,4,512]{3,2,0,1:T(4,128)(2,1)S(1)}, u32[]{:S(2)}, u32[]{:S(2)}) collective-permute-start(bf16[2,4,4,512]{3,2,0,1:T(4,128)(2,1)S(1)} %pad_maximum_fusion.2), channel_id=1, source_target_pairs={{0,6},{1,7},{2,4},{3,5},{4,2},{5,3},{6,0},{7,1},{8,14},{9,15},{10,... | collective-permute-start | bytes 98312 | tf_op jit(solution)/shard_map/ppermute | solution.py:29
  32.8 26.8 %collective-permute-start.4 = (bf16[4,2,4,512]{3,2,1,0:T(4,128)(2,1)S(1)}, bf16[4,2,4,512]{3,2,1,0:T(4,128)(2,1)S(1)}, u32[]{:S(2)}, u32[]{:S(2)}) collective-permute-start(bf16[4,2,4,512]{3,2,1,0:T(4,128)(2,1)S(1)} %pad_maximum_fusion.3), channel_id=1, source_target_pairs={{0,8},{1,9},{2,10},{3,11},{4,12},{5,13},{6,14},{7,15},{8,0},{9,1},... | collective-permute-start | bytes 98312 | tf_op jit(solution)/shard_map/ppermute | solution.py:29
  41.9 17.7 %collective-permute-start.5 = (bf16[4,2,4,512]{3,2,1,0:T(4,128)(2,1)S(1)}, bf16[4,2,4,512]{3,2,1,0:T(4,128)(2,1)S(1)}, u32[]{:S(2)}, u32[]{:S(2)}) collective-permute-start(bf16[4,2,4,512]{3,2,1,0:T(4,128)(2,1)S(1)} %pad_maximum_fusion.4), channel_id=1, source_target_pairs={{0,16},{1,17},{2,18},{3,19},{4,20},{5,21},{6,22},{7,23},{8,24},{9,... | collective-permute-start | bytes 98312 | tf_op jit(solution)/shard_map/ppermute | solution.py:29
  50.2 9.7 %collective-permute-start.6 = (bf16[4,2,4,512]{3,2,1,0:T(4,128)(2,1)S(1)}, bf16[4,2,4,512]{3,2,1,0:T(4,128)(2,1)S(1)}, u32[]{:S(2)}, u32[]{:S(2)}) collective-permute-start(bf16[4,2,4,512]{3,2,1,0:T(4,128)(2,1)S(1)} %pad_maximum_fusion.5), channel_id=1, source_target_pairs={{0,24},{1,25},{2,26},{3,27},{4,28},{5,29},{6,30},{7,31},{8,16},{9,... | collective-permute-start | bytes 98312 | tf_op jit(solution)/shard_map/ppermute | solution.py:29
  53.8 20.5 %all-to-all-start.1 = ((bf16[16,16,2048]{2,1,0:T(8,128)(2,1)}), bf16[16,16,2048]{2,1,0:T(8,128)(2,1)}, u32[]{:S(2)}, u32[]{:S(2)}) async-start(bf16[16,16,2048]{2,1,0:T(8,128)(2,1)} %pick.1), calls=%async_computation.1 | async-start | bytes 2097152 | tf_op jit(solution)/shard_map/all_to_all | solution.py:21
  74.3 94.6 %all-to-all-start.2 = ((bf16[32,8,2048]{2,1,0:T(8,128)(2,1)}), bf16[32,8,2048]{2,1,0:T(8,128)(2,1)S(1)}, u32[]{:S(2)}, u32[]{:S(2)}) async-start(bf16[32,8,2048]{2,1,0:T(8,128)(2,1)} %bitcast.28.routed_ref), calls=%async_computation.2 | async-start | bytes 2097152 | tf_op jit(solution)/shard_map/all_to_all | solution.py:21
  86.3 28.9 %copy-start.4 = (s32[128]{0:T(128)S(1)}, s32[128]{0:T(128)}, u32[]{:S(2)}) copy-start(s32[128]{0:T(128)} %param.11) | copy-start | bytes 1540
  86.3 64.9 %copy-start.3 = (bf16[16,2048]{1,0:T(8,128)(2,1)S(1)}, bf16[16,2048]{1,0:T(8,128)(2,1)}, u32[]{:S(2)}) copy-start(bf16[16,2048]{1,0:T(8,128)(2,1)} %param.9) | copy-start | bytes 196612
  86.3 77.5 %copy-start.2 = (bf16[16,128,256]{2,1,0:T(8,128)(2,1)S(1)}, bf16[16,128,256]{2,1,0:T(8,128)(2,1)}, u32[]{:S(2)}) copy-start(bf16[16,128,256]{2,1,0:T(8,128)(2,1)} %param.10) | copy-start | bytes 3145732
  88.2 13.3 %collective-permute-start.7 = (f32[8,2,16,256]{3,2,1,0:T(8,128)S(1)}, f32[8,2,16,256]{3,2,1,0:T(8,128)S(1)}, u32[]{:S(2)}, u32[]{:S(2)}) collective-permute-start(f32[8,2,16,256]{3,2,1,0:T(8,128)S(1)} %slice_bitcast_fusion), channel_id=1, source_target_pairs={{0,1},{1,0},{2,3},{3,2},{4,5},{5,4},{6,7},{7,6},{8,9},{9,8},{10,11... | collective-permute-start | bytes 786440 | tf_op jit(solution)/shard_map/ppermute | solution.py:171
  101.6 38.3 %collective-permute-start.10 = (bf16[2,16,384]{2,1,0:T(8,128)(2,1)S(1)}, bf16[2,16,384]{2,1,0:T(8,128)(2,1)S(1)}, u32[]{:S(2)}, u32[]{:S(2)}) collective-permute-start(bf16[2,16,384]{2,1,0:T(8,128)(2,1)S(1)} %get-tuple-element.6), channel_id=1, source_target_pairs={{0,12},{1,13},{2,14},{3,15},{4,8},{5,9},{6,10},{7,11},{8,4},{9,5},... | collective-permute-start | bytes 73736 | tf_op jit(solution)/shard_map/ppermute | solution.py:171
  110.8 38.4 %collective-permute-start.11 = (bf16[2,16,384]{2,1,0:T(8,128)(2,1)S(1)}, bf16[2,16,384]{2,1,0:T(8,128)(2,1)S(1)}, u32[]{:S(2)}, u32[]{:S(2)}) collective-permute-start(bf16[2,16,384]{2,1,0:T(8,128)(2,1)S(1)} %get-tuple-element.7), channel_id=1, source_target_pairs={{0,24},{1,25},{2,26},{3,27},{4,28},{5,29},{6,30},{7,31},{8,16},{9,... | collective-permute-start | bytes 73736 | tf_op jit(solution)/shard_map/ppermute | solution.py:171
  115.3 35.9 %collective-permute-start.12 = (bf16[2,16,384]{2,1,0:T(8,128)(2,1)S(1)}, bf16[2,16,384]{2,1,0:T(8,128)(2,1)S(1)}, u32[]{:S(2)}, u32[]{:S(2)}) collective-permute-start(bf16[2,16,384]{2,1,0:T(8,128)(2,1)S(1)} %get-tuple-element.8), channel_id=1, source_target_pairs={{0,8},{1,9},{2,10},{3,11},{4,12},{5,13},{6,14},{7,15},{8,0},{9,1},... | collective-permute-start | bytes 73736 | tf_op jit(solution)/shard_map/ppermute | solution.py:171
  119.1 32.1 %collective-permute-start.13 = (bf16[2,16,384]{2,1,0:T(8,128)(2,1)S(1)}, bf16[2,16,384]{2,1,0:T(8,128)(2,1)S(1)}, u32[]{:S(2)}, u32[]{:S(2)}) collective-permute-start(bf16[2,16,384]{2,1,0:T(8,128)(2,1)S(1)} %get-tuple-element.10), channel_id=1, source_target_pairs={{0,28},{1,29},{2,30},{3,31},{4,24},{5,25},{6,26},{7,27},{8,20},{9,... | collective-permute-start | bytes 73736 | tf_op jit(solution)/shard_map/ppermute | solution.py:171
  121.2 30.0 %collective-permute-start.14 = (bf16[2,16,384]{2,1,0:T(8,128)(2,1)S(1)}, bf16[2,16,384]{2,1,0:T(8,128)(2,1)S(1)}, u32[]{:S(2)}, u32[]{:S(2)}) collective-permute-start(bf16[2,16,384]{2,1,0:T(8,128)(2,1)S(1)} %get-tuple-element.9), channel_id=1, source_target_pairs={{0,4},{1,5},{2,6},{3,7},{4,0},{5,1},{6,2},{7,3},{8,12},{9,13},{10,... | collective-permute-start | bytes 73736 | tf_op jit(solution)/shard_map/ppermute | solution.py:171
  139.9 14.4 %collective-permute-start.8 = (bf16[2,16,384]{2,1,0:T(8,128)(2,1)S(1)}, bf16[2,16,384]{2,1,0:T(8,128)(2,1)S(1)}, u32[]{:S(2)}, u32[]{:S(2)}) collective-permute-start(bf16[2,16,384]{2,1,0:T(8,128)(2,1)S(1)} %get-tuple-element.4), channel_id=1, source_target_pairs={{0,16},{1,17},{2,18},{3,19},{4,20},{5,21},{6,22},{7,23},{8,24},{9,... | collective-permute-start | bytes 73736 | tf_op jit(solution)/shard_map/ppermute | solution.py:171
  149.2 12.6 %collective-permute-start.9 = (bf16[2,16,384]{2,1,0:T(8,128)(2,1)S(1)}, bf16[2,16,384]{2,1,0:T(8,128)(2,1)S(1)}, u32[]{:S(2)}, u32[]{:S(2)}) collective-permute-start(bf16[2,16,384]{2,1,0:T(8,128)(2,1)S(1)} %get-tuple-element.5), channel_id=1, source_target_pairs={{0,20},{1,21},{2,22},{3,23},{4,16},{5,17},{6,18},{7,19},{8,28},{9,... | collective-permute-start | bytes 73736 | tf_op jit(solution)/shard_map/ppermute | solution.py:171
  161.9 5.6 %collective-permute-start.15 = (f32[16,256]{1,0:T(8,128)S(1)}, f32[16,256]{1,0:T(8,128)S(1)}, u32[]{:S(2)}, u32[]{:S(2)}) collective-permute-start(f32[16,256]{1,0:T(8,128)S(1)} %slice_bitcast_fusion.3), channel_id=1, source_target_pairs={{0,2},{1,3},{2,0},{3,1},{4,6},{5,7},{6,4},{7,5},{8,10},{9,11},{10,... | collective-permute-start | bytes 49160 | tf_op jit(solution)/shard_map/ppermute | solution.py:171

commit v10 on v8

--- a/solution.py
+++ b/solution.py
@@ -27,16 +27,16 @@
     def send(values, bits):
         return lax.ppermute(values, "shard", [(i, i ^ bits) for i in range(shards)])
 
-    order = jnp.arange(shards, dtype=jnp.int32).reshape(4, 4, 2).transpose(2, 1, 0).reshape(-1)
+    order = jnp.arange(shards, dtype=jnp.int32).reshape(4, 4, 2).transpose(2, 0, 1).reshape(-1)
     start = blocks.at[me ^ order].get(mode="promise_in_bounds")
     start = start.reshape((2, 4, 4) + blocks.shape[1:])
     side = [start[0], send(start[1], 1)]
-    near = [jnp.stack([v[k] for v in side]) for k in range(4)]
-    near = [near[0]] + [send(near[k], k << 1) for k in range(1, 4)]
-    far = [jnp.stack([v[:, k] for v in near]) for k in range(4)]
+    far = [jnp.stack([v[k] for v in side]) for k in range(4)]
     for k in (2, 1, 3):
         far[k] = send(far[k], k << 3)
-    return jnp.concatenate(far).reshape((shards,) + blocks.shape[1:])
+    near = [jnp.stack([v[:, k] for v in far]) for k in range(4)]
+    near = [near[0]] + [send(near[k], k << 1) for k in range(1, 4)]
+    return jnp.concatenate(near).reshape((shards,) + blocks.shape[1:])
 
 
 def attend(query_rows, cache_rows, fresh_rows, row_lengths):
@@ -127,7 +127,9 @@
     own = inputs_ref.shape[1]
     block_rows = ROWS // per_head
     for d in range(shards):
-        rows_ref[d * own : (d + 1) * own, :] = inputs_ref[me ^ d].astype(jnp.float32)
+        r = me ^ d
+        place = ((r >> 1) & 3) * (shards // 4) + (r >> 3) * 2 + (r & 1)
+        rows_ref[d * own : (d + 1) * own, :] = inputs_ref[place].astype(jnp.float32)
     inputs = rows_ref[...].astype(jnp.bfloat16)
     for h in range(heads):
         product = lax.dot_general(

time: 171 us -> 171 us (level)
  starting transfers between devices: 102 us -> 99.2 us
  waiting for transfers between devices: 54.8 us -> 57.2 us
    all_to_all x3, starting transfers between devices: 23.9 us -> 20 us  [exchange(): return lax.all_to_all(blocks, axis, split_axis=0, concat_axis=0, tiled=True)]
    ppermute x16, waiting for transfers between devices: 40.4 us -> 42.6 us  [send(): return lax.ppermute(values, 'shard', [(i, i ^ bits) for i in range(shards)])]
where the time goes in v10:
time: 171 us; the launch traced here: 170 us
  starting transfers between devices  99.2 us (58%)
  waiting for transfers between devices  57.2 us (33%)
  Pallas kernels  7.02 us (4%)
  local copies, waits for them, and re-layouts  3.62 us (2%)
    ppermute x16, starting transfers between devices, send(): return lax.ppermute(values, 'shard', [(i, i ^ bits) for i in range(shards)])  79.2 us
    ppermute x16, waiting for transfers between devices, send(): return lax.ppermute(values, 'shard', [(i, i ^ bits) for i in range(shards)])  42.6 us
    all_to_all x3, starting transfers between devices, exchange(): return lax.all_to_all(blocks, axis, split_axis=0, concat_axis=0, tiled=True)  20 us
    all_to_all x3, waiting for transfers between devices, exchange(): return lax.all_to_all(blocks, axis, split_axis=0, concat_axis=0, tiled=True)  14.6 us
    pallas_call x1, Pallas kernels, flip(): pl.pallas_call(flip_kernel, grid=(depth // rows,), in_specs=[pl.BlockSpec...  3.53 us
  transfers between devices with their start and end apart: 19, of which 8 were waited for; matrix products, arithmetic and copies ran while one was open for 1% of the time, Pallas kernels for 4%

profile of v10, /device:TPU:24, one launch (start us, length us, event | category | flops | bytes accessed | tf_op | source)
XLA Modules:
  0.0 169.8 jit_solution(2590050159538504199)
XLA Ops:
  0.6 0.0 copy-start
  0.7 0.1 xor.18
  0.8 0.8 copy-done
  1.5 0.7 gather_fusion
  2.3 4.9 %collective-permute-start = (bf16[4,4,4,512]{3,2,0,1:T(4,128)(2,1)S(1)}, bf16[4,4,4,512]{3,2,0,1:T(4,128)(2,1)S(1)}, u32[]{:S(2)}, u32[]{:S(2)}) collective-permute-start(bf16[4,4,4,512]{3,2,0,1:T(4,128)(2,1)S(1)} %copy.19), channel_id=1, source_target_pairs={{0,1},{1,0},{2,3},{3,2},{4,5},{5,4},{6,7},{7,6},{8,9},{9,8},{10,11... | collective-permute-start | bytes 196616 | tf_op jit(solution)/shard_map/ppermute | solution.py:28
  7.2 3.5 %flip.1 = bf16[32,8,2048]{2,1,0:T(8,128)(2,1)} custom-call(f32[1,512,1024]{2,1,0:T(8,128)} %weights_ref.1), custom_call_target="tpu_custom_call" | custom-call | flops 2000000 | bytes 3000000 | tf_op jit(solution)/shard_map/flip/pallas_call | solution.py:90
  10.8 6.2 %all-to-all-start = ((bf16[16,16,2048]{2,1,0:T(8,128)(2,1)}), bf16[16,16,2048]{2,1,0:T(8,128)(2,1)S(1)}, u32[]{:S(2)}, u32[]{:S(2)}) async-start(bf16[16,16,2048]{2,1,0:T(8,128)(2,1)} %bitcast.114), calls=%async_computation | async-start | bytes 2097152 | tf_op jit(solution)/shard_map/all_to_all | solution.py:20
  16.9 0.0 collective-permute-done
  17.1 7.8 %collective-permute-start.1 = (bf16[2,4,4,512]{3,2,0,1:T(4,128)(2,1)S(1)}, bf16[2,4,4,512]{3,2,0,1:T(4,128)(2,1)S(1)}, u32[]{:S(2)}, u32[]{:S(2)}) collective-permute-start(bf16[2,4,4,512]{3,2,0,1:T(4,128)(2,1)S(1)} %pad_maximum_fusion), channel_id=1, source_target_pairs={{0,8},{1,9},{2,10},{3,11},{4,12},{5,13},{6,14},{7,15},{8,0},{9,1},... | collective-permute-start | bytes 98312 | tf_op jit(solution)/shard_map/ppermute | solution.py:28
  24.9 10.9 %collective-permute-start.2 = (bf16[2,4,4,512]{3,2,1,0:T(4,128)(2,1)S(1)}, bf16[2,4,4,512]{3,2,1,0:T(4,128)(2,1)S(1)}, u32[]{:S(2)}, u32[]{:S(2)}) collective-permute-start(bf16[2,4,4,512]{3,2,1,0:T(4,128)(2,1)S(1)} %pad_maximum_fusion.1), channel_id=1, source_target_pairs={{0,16},{1,17},{2,18},{3,19},{4,20},{5,21},{6,22},{7,23},{8,24},{9,... | collective-permute-start | bytes 98312 | tf_op jit(solution)/shard_map/ppermute | solution.py:28
  35.9 1.9 %collective-permute-start.3 = (bf16[2,4,4,512]{3,2,0,1:T(4,128)(2,1)S(1)}, bf16[2,4,4,512]{3,2,0,1:T(4,128)(2,1)S(1)}, u32[]{:S(2)}, u32[]{:S(2)}) collective-permute-start(bf16[2,4,4,512]{3,2,0,1:T(4,128)(2,1)S(1)} %pad_maximum_fusion.2), channel_id=1, source_target_pairs={{0,24},{1,25},{2,26},{3,27},{4,28},{5,29},{6,30},{7,31},{8,16},{9,... | collective-permute-start | bytes 98312 | tf_op jit(solution)/shard_map/ppermute | solution.py:28
  37.8 0.0 collective-permute-done.1
  37.8 1.7 %collective-permute-done.2 = bf16[2,4,4,512]{3,2,1,0:T(4,128)(2,1)S(1)} collective-permute-done((bf16[2,4,4,512]{3,2,1,0:T(4,128)(2,1)S(1)}, bf16[2,4,4,512]{3,2,1,0:T(4,128)(2,1)S(1)}, u32[]{:S(2)}, u32[]{:S(2)}) %collective-permute-start.2) | collective-permute-done | bytes 32800 | tf_op jit(solution)/shard_map/ppermute | solution.py:28
  39.5 6.0 %collective-permute-done.3 = bf16[2,4,4,512]{3,2,0,1:T(4,128)(2,1)S(1)} collective-permute-done((bf16[2,4,4,512]{3,2,0,1:T(4,128)(2,1)S(1)}, bf16[2,4,4,512]{3,2,0,1:T(4,128)(2,1)S(1)}, u32[]{:S(2)}, u32[]{:S(2)}) %collective-permute-start.3) | collective-permute-done | bytes 32800 | tf_op jit(solution)/shard_map/ppermute | solution.py:28
  45.6 3.6 %collective-permute-start.4 = (bf16[4,2,4,512]{3,2,1,0:T(4,128)(2,1)S(1)}, bf16[4,2,4,512]{3,2,1,0:T(4,128)(2,1)S(1)}, u32[]{:S(2)}, u32[]{:S(2)}) collective-permute-start(bf16[4,2,4,512]{3,2,1,0:T(4,128)(2,1)S(1)} %pad_maximum_fusion.3), channel_id=1, source_target_pairs={{0,2},{1,3},{2,0},{3,1},{4,6},{5,7},{6,4},{7,5},{8,10},{9,11},{10,... | collective-permute-start | bytes 98312 | tf_op jit(solution)/shard_map/ppermute | solution.py:28
  49.3 3.4 %collective-permute-start.5 = (bf16[4,2,4,512]{3,2,1,0:T(4,128)(2,1)S(1)}, bf16[4,2,4,512]{3,2,1,0:T(4,128)(2,1)S(1)}, u32[]{:S(2)}, u32[]{:S(2)}) collective-permute-start(bf16[4,2,4,512]{3,2,1,0:T(4,128)(2,1)S(1)} %pad_maximum_fusion.4), channel_id=1, source_target_pairs={{0,4},{1,5},{2,6},{3,7},{4,0},{5,1},{6,2},{7,3},{8,12},{9,13},{10,... | collective-permute-start | bytes 98312 | tf_op jit(solution)/shard_map/ppermute | solution.py:28
  52.8 3.1 %collective-permute-start.6 = (bf16[4,2,4,512]{3,2,1,0:T(4,128)(2,1)S(1)}, bf16[4,2,4,512]{3,2,1,0:T(4,128)(2,1)S(1)}, u32[]{:S(2)}, u32[]{:S(2)}) collective-permute-start(bf16[4,2,4,512]{3,2,1,0:T(4,128)(2,1)S(1)} %pad_maximum_fusion.5), channel_id=1, source_target_pairs={{0,6},{1,7},{2,4},{3,5},{4,2},{5,3},{6,0},{7,1},{8,14},{9,15},{10,... | collective-permute-start | bytes 98312 | tf_op jit(solution)/shard_map/ppermute | solution.py:28
  55.9 0.0 all-to-all-done.spread_ref
  55.9 1.7 pick.1
  57.5 5.7 %all-to-all-start.1 = ((bf16[16,16,2048]{2,1,0:T(8,128)(2,1)}), bf16[16,16,2048]{2,1,0:T(8,128)(2,1)}, u32[]{:S(2)}, u32[]{:S(2)}) async-start(bf16[16,16,2048]{2,1,0:T(8,128)(2,1)} %pick.1), calls=%async_computation.1 | async-start | bytes 2097152 | tf_op jit(solution)/shard_map/all_to_all | solution.py:20
  63.4 14.6 %all-to-all-done.1 = bf16[16,16,2048]{2,1,0:T(8,128)(2,1)} async-done(((bf16[16,16,2048]{2,1,0:T(8,128)(2,1)}), bf16[16,16,2048]{2,1,0:T(8,128)(2,1)}, u32[]{:S(2)}, u32[]{:S(2)}) %all-to-all-start.1) | async-done | bytes 1048608 | tf_op jit(solution)/shard_map/all_to_all | solution.py:20
  78.0 8.2 %all-to-all-start.2 = ((bf16[32,8,2048]{2,1,0:T(8,128)(2,1)}), bf16[32,8,2048]{2,1,0:T(8,128)(2,1)S(1)}, u32[]{:S(2)}, u32[]{:S(2)}) async-start(bf16[32,8,2048]{2,1,0:T(8,128)(2,1)} %bitcast.28.routed_ref), calls=%async_computation.2 | async-start | bytes 2097152 | tf_op jit(solution)/shard_map/all_to_all | solution.py:20
  86.2 0.0 copy-start.4
  86.2 0.0 copy-start.3
  86.2 0.0 copy-start.2
  86.2 1.8 %multiply.23 = f32[2,8,2,16,256]{4,3,2,1,0:T(8,128)S(1)} custom-call(s32[1]{0:T(128)} %bitcast.me_ref, bf16[32,4,512]{2,1,0:T(4,128)(2,1)S(1)} %bitcast.113, bf16[32,8,2048]{2,1,0:T(8,128)(2,1)} %bitcast.28.routed_ref), custom_call_target="tpu_custom_call" | custom-call | flops 134217728 | bytes 3000000 | tf_op jit(solution)/shard_map/multiply/pallas_call | solution.py:149
  88.1 5.2 %collective-permute-start.7 = (f32[8,2,16,256]{3,2,1,0:T(8,128)S(1)}, f32[8,2,16,256]{3,2,1,0:T(8,128)S(1)}, u32[]{:S(2)}, u32[]{:S(2)}) collective-permute-start(f32[8,2,16,256]{3,2,1,0:T(8,128)S(1)} %slice_bitcast_fusion), channel_id=1, source_target_pairs={{0,1},{1,0},{2,3},{3,2},{4,5},{5,4},{6,7},{7,6},{8,9},{9,8},{10,11... | collective-permute-start | bytes 786440 | tf_op jit(solution)/shard_map/ppermute | solution.py:167
  93.3 8.1 %collective-permute-done.7 = f32[8,2,16,256]{3,2,1,0:T(8,128)S(1)} collective-permute-done((f32[8,2,16,256]{3,2,1,0:T(8,128)S(1)}, f32[8,2,16,256]{3,2,1,0:T(8,128)S(1)}, u32[]{:S(2)}, u32[]{:S(2)}) %collective-permute-start.7) | collective-permute-done | bytes 262176 | tf_op jit(solution)/shard_map/ppermute | solution.py:167
  101.5 9.2 %collective-permute-start.10 = (bf16[2,16,384]{2,1,0:T(8,128)(2,1)S(1)}, bf16[2,16,384]{2,1,0:T(8,128)(2,1)S(1)}, u32[]{:S(2)}, u32[]{:S(2)}) collective-permute-start(bf16[2,16,384]{2,1,0:T(8,128)(2,1)S(1)} %get-tuple-element.6), channel_id=1, source_target_pairs={{0,12},{1,13},{2,14},{3,15},{4,8},{5,9},{6,10},{7,11},{8,4},{9,5},... | collective-permute-start | bytes 73736 | tf_op jit(solution)/shard_map/ppermute | solution.py:167
  110.7 4.4 %collective-permute-start.11 = (bf16[2,16,384]{2,1,0:T(8,128)(2,1)S(1)}, bf16[2,16,384]{2,1,0:T(8,128)(2,1)S(1)}, u32[]{:S(2)}, u32[]{:S(2)}) collective-permute-start(bf16[2,16,384]{2,1,0:T(8,128)(2,1)S(1)} %get-tuple-element.7), channel_id=1, source_target_pairs={{0,24},{1,25},{2,26},{3,27},{4,28},{5,29},{6,30},{7,31},{8,16},{9,... | collective-permute-start | bytes 73736 | tf_op jit(solution)/shard_map/ppermute | solution.py:167
  115.1 0.1 dynamic_slice.3
  115.2 3.8 %collective-permute-start.12 = (bf16[2,16,384]{2,1,0:T(8,128)(2,1)S(1)}, bf16[2,16,384]{2,1,0:T(8,128)(2,1)S(1)}, u32[]{:S(2)}, u32[]{:S(2)}) collective-permute-start(bf16[2,16,384]{2,1,0:T(8,128)(2,1)S(1)} %get-tuple-element.8), channel_id=1, source_target_pairs={{0,8},{1,9},{2,10},{3,11},{4,12},{5,13},{6,14},{7,15},{8,0},{9,1},... | collective-permute-start | bytes 73736 | tf_op jit(solution)/shard_map/ppermute | solution.py:167
  119.0 2.1 %collective-permute-start.13 = (bf16[2,16,384]{2,1,0:T(8,128)(2,1)S(1)}, bf16[2,16,384]{2,1,0:T(8,128)(2,1)S(1)}, u32[]{:S(2)}, u32[]{:S(2)}) collective-permute-start(bf16[2,16,384]{2,1,0:T(8,128)(2,1)S(1)} %get-tuple-element.10), channel_id=1, source_target_pairs={{0,28},{1,29},{2,30},{3,31},{4,24},{5,25},{6,26},{7,27},{8,20},{9,... | collective-permute-start | bytes 73736 | tf_op jit(solution)/shard_map/ppermute | solution.py:167
  121.1 5.7 %collective-permute-start.14 = (bf16[2,16,384]{2,1,0:T(8,128)(2,1)S(1)}, bf16[2,16,384]{2,1,0:T(8,128)(2,1)S(1)}, u32[]{:S(2)}, u32[]{:S(2)}) collective-permute-start(bf16[2,16,384]{2,1,0:T(8,128)(2,1)S(1)} %get-tuple-element.9), channel_id=1, source_target_pairs={{0,4},{1,5},{2,6},{3,7},{4,0},{5,1},{6,2},{7,3},{8,12},{9,13},{10,... | collective-permute-start | bytes 73736 | tf_op jit(solution)/shard_map/ppermute | solution.py:167
  126.8 13.0 %collective-permute-done.10 = bf16[2,16,384]{2,1,0:T(8,128)(2,1)S(1)} collective-permute-done((bf16[2,16,384]{2,1,0:T(8,128)(2,1)S(1)}, bf16[2,16,384]{2,1,0:T(8,128)(2,1)S(1)}, u32[]{:S(2)}, u32[]{:S(2)}) %collective-permute-start.10) | collective-permute-done | bytes 24608 | tf_op jit(solution)/shard_map/ppermute | solution.py:167
  139.8 9.3 %collective-permute-start.8 = (bf16[2,16,384]{2,1,0:T(8,128)(2,1)S(1)}, bf16[2,16,384]{2,1,0:T(8,128)(2,1)S(1)}, u32[]{:S(2)}, u32[]{:S(2)}) collective-permute-start(bf16[2,16,384]{2,1,0:T(8,128)(2,1)S(1)} %get-tuple-element.4), channel_id=1, source_target_pairs={{0,16},{1,17},{2,18},{3,19},{4,20},{5,21},{6,22},{7,23},{8,24},{9,... | collective-permute-start | bytes 73736 | tf_op jit(solution)/shard_map/ppermute | solution.py:167
  149.1 1.9 %collective-permute-start.9 = (bf16[2,16,384]{2,1,0:T(8,128)(2,1)S(1)}, bf16[2,16,384]{2,1,0:T(8,128)(2,1)S(1)}, u32[]{:S(2)}, u32[]{:S(2)}) collective-permute-start(bf16[2,16,384]{2,1,0:T(8,128)(2,1)S(1)} %get-tuple-element.5), channel_id=1, source_target_pairs={{0,20},{1,21},{2,22},{3,23},{4,16},{5,17},{6,18},{7,19},{8,28},{9,... | collective-permute-start | bytes 73736 | tf_op jit(solution)/shard_map/ppermute | solution.py:167
  151.0 0.1 iota_compare_fusion
  151.1 3.1 %collective-permute-done.8 = bf16[2,16,384]{2,1,0:T(8,128)(2,1)S(1)} collective-permute-done((bf16[2,16,384]{2,1,0:T(8,128)(2,1)S(1)}, bf16[2,16,384]{2,1,0:T(8,128)(2,1)S(1)}, u32[]{:S(2)}, u32[]{:S(2)}) %collective-permute-start.8) | collective-permute-done | bytes 24608 | tf_op jit(solution)/shard_map/ppermute | solution.py:167
  154.2 7.5 %collective-permute-done.9 = bf16[2,16,384]{2,1,0:T(8,128)(2,1)S(1)} collective-permute-done((bf16[2,16,384]{2,1,0:T(8,128)(2,1)S(1)}, bf16[2,16,384]{2,1,0:T(8,128)(2,1)S(1)}, u32[]{:S(2)}, u32[]{:S(2)}) %collective-permute-start.9) | collective-permute-done | bytes 24608 | tf_op jit(solution)/shard_map/ppermute | solution.py:167
  161.8 1.9 %collective-permute-start.15 = (f32[16,256]{1,0:T(8,128)S(1)}, f32[16,256]{1,0:T(8,128)S(1)}, u32[]{:S(2)}, u32[]{:S(2)}) collective-permute-start(f32[16,256]{1,0:T(8,128)S(1)} %slice_bitcast_fusion.3), channel_id=1, source_target_pairs={{0,2},{1,3},{2,0},{3,1},{4,6},{5,7},{6,4},{7,5},{8,10},{9,11},{10,... | collective-permute-start | bytes 49160 | tf_op jit(solution)/shard_map/ppermute | solution.py:167
  163.7 0.5 fusion.41
  164.2 3.2 %collective-permute-done.15 = f32[16,256]{1,0:T(8,128)S(1)} collective-permute-done((f32[16,256]{1,0:T(8,128)S(1)}, f32[16,256]{1,0:T(8,128)S(1)}, u32[]{:S(2)}, u32[]{:S(2)}) %collective-permute-start.15) | collective-permute-done | bytes 16416 | tf_op jit(solution)/shard_map/ppermute | solution.py:167
  167.4 0.1 fusion.31
  167.6 0.2 fusion.6
  167.8 0.3 fusion.1
  168.1 0.7 copy.35
  168.8 1.1 copy.24
  (51 shorter events, 0.7 us)
Async XLA Ops:
  0.6 0.9 copy-start
  2.3 14.7 %collective-permute-start = (bf16[4,4,4,512]{3,2,0,1:T(4,128)(2,1)S(1)}, bf16[4,4,4,512]{3,2,0,1:T(4,128)(2,1)S(1)}, u32[]{:S(2)}, u32[]{:S(2)}) collective-permute-start(bf16[4,4,4,512]{3,2,0,1:T(4,128)(2,1)S(1)} %copy.19), channel_id=1, source_target_pairs={{0,1},{1,0},{2,3},{3,2},{4,5},{5,4},{6,7},{7,6},{8,9},{9,8},{10,11... | collective-permute-start | bytes 196616 | tf_op jit(solution)/shard_map/ppermute | solution.py:28
  10.7 45.1 %copy-start.1 = (s32[16]{0:T(128)S(1)}, s32[16]{0:T(128)}, u32[]{:S(2)}) copy-start(s32[16]{0:T(128)} %group_ref.1) | copy-start | bytes 196
  10.8 45.1 %all-to-all-start = ((bf16[16,16,2048]{2,1,0:T(8,128)(2,1)}), bf16[16,16,2048]{2,1,0:T(8,128)(2,1)S(1)}, u32[]{:S(2)}, u32[]{:S(2)}) async-start(bf16[16,16,2048]{2,1,0:T(8,128)(2,1)} %bitcast.114), calls=%async_computation | async-start | bytes 2097152 | tf_op jit(solution)/shard_map/all_to_all | solution.py:20
  17.1 20.7 %collective-permute-start.1 = (bf16[2,4,4,512]{3,2,0,1:T(4,128)(2,1)S(1)}, bf16[2,4,4,512]{3,2,0,1:T(4,128)(2,1)S(1)}, u32[]{:S(2)}, u32[]{:S(2)}) collective-permute-start(bf16[2,4,4,512]{3,2,0,1:T(4,128)(2,1)S(1)} %pad_maximum_fusion), channel_id=1, source_target_pairs={{0,8},{1,9},{2,10},{3,11},{4,12},{5,13},{6,14},{7,15},{8,0},{9,1},... | collective-permute-start | bytes 98312 | tf_op jit(solution)/shard_map/ppermute | solution.py:28
  24.9 14.6 %collective-permute-start.2 = (bf16[2,4,4,512]{3,2,1,0:T(4,128)(2,1)S(1)}, bf16[2,4,4,512]{3,2,1,0:T(4,128)(2,1)S(1)}, u32[]{:S(2)}, u32[]{:S(2)}) collective-permute-start(bf16[2,4,4,512]{3,2,1,0:T(4,128)(2,1)S(1)} %pad_maximum_fusion.1), channel_id=1, source_target_pairs={{0,16},{1,17},{2,18},{3,19},{4,20},{5,21},{6,22},{7,23},{8,24},{9,... | collective-permute-start | bytes 98312 | tf_op jit(solution)/shard_map/ppermute | solution.py:28
  35.9 9.7 %collective-permute-start.3 = (bf16[2,4,4,512]{3,2,0,1:T(4,128)(2,1)S(1)}, bf16[2,4,4,512]{3,2,0,1:T(4,128)(2,1)S(1)}, u32[]{:S(2)}, u32[]{:S(2)}) collective-permute-start(bf16[2,4,4,512]{3,2,0,1:T(4,128)(2,1)S(1)} %pad_maximum_fusion.2), channel_id=1, source_target_pairs={{0,24},{1,25},{2,26},{3,27},{4,28},{5,29},{6,30},{7,31},{8,16},{9,... | collective-permute-start | bytes 98312 | tf_op jit(solution)/shard_map/ppermute | solution.py:28
  45.6 17.7 %collective-permute-start.4 = (bf16[4,2,4,512]{3,2,1,0:T(4,128)(2,1)S(1)}, bf16[4,2,4,512]{3,2,1,0:T(4,128)(2,1)S(1)}, u32[]{:S(2)}, u32[]{:S(2)}) collective-permute-start(bf16[4,2,4,512]{3,2,1,0:T(4,128)(2,1)S(1)} %pad_maximum_fusion.3), channel_id=1, source_target_pairs={{0,2},{1,3},{2,0},{3,1},{4,6},{5,7},{6,4},{7,5},{8,10},{9,11},{10,... | collective-permute-start | bytes 98312 | tf_op jit(solution)/shard_map/ppermute | solution.py:28
  49.3 14.0 %collective-permute-start.5 = (bf16[4,2,4,512]{3,2,1,0:T(4,128)(2,1)S(1)}, bf16[4,2,4,512]{3,2,1,0:T(4,128)(2,1)S(1)}, u32[]{:S(2)}, u32[]{:S(2)}) collective-permute-start(bf16[4,2,4,512]{3,2,1,0:T(4,128)(2,1)S(1)} %pad_maximum_fusion.4), channel_id=1, source_target_pairs={{0,4},{1,5},{2,6},{3,7},{4,0},{5,1},{6,2},{7,3},{8,12},{9,13},{10,... | collective-permute-start | bytes 98312 | tf_op jit(solution)/shard_map/ppermute | solution.py:28
  52.8 10.6 %collective-permute-start.6 = (bf16[4,2,4,512]{3,2,1,0:T(4,128)(2,1)S(1)}, bf16[4,2,4,512]{3,2,1,0:T(4,128)(2,1)S(1)}, u32[]{:S(2)}, u32[]{:S(2)}) collective-permute-start(bf16[4,2,4,512]{3,2,1,0:T(4,128)(2,1)S(1)} %pad_maximum_fusion.5), channel_id=1, source_target_pairs={{0,6},{1,7},{2,4},{3,5},{4,2},{5,3},{6,0},{7,1},{8,14},{9,15},{10,... | collective-permute-start | bytes 98312 | tf_op jit(solution)/shard_map/ppermute | solution.py:28
  57.5 20.5 %all-to-all-start.1 = ((bf16[16,16,2048]{2,1,0:T(8,128)(2,1)}), bf16[16,16,2048]{2,1,0:T(8,128)(2,1)}, u32[]{:S(2)}, u32[]{:S(2)}) async-start(bf16[16,16,2048]{2,1,0:T(8,128)(2,1)} %pick.1), calls=%async_computation.1 | async-start | bytes 2097152 | tf_op jit(solution)/shard_map/all_to_all | solution.py:20
  78.0 90.8 %all-to-all-start.2 = ((bf16[32,8,2048]{2,1,0:T(8,128)(2,1)}), bf16[32,8,2048]{2,1,0:T(8,128)(2,1)S(1)}, u32[]{:S(2)}, u32[]{:S(2)}) async-start(bf16[32,8,2048]{2,1,0:T(8,128)(2,1)} %bitcast.28.routed_ref), calls=%async_computation.2 | async-start | bytes 2097152 | tf_op jit(solution)/shard_map/all_to_all | solution.py:20
  86.2 28.9 %copy-start.4 = (s32[128]{0:T(128)S(1)}, s32[128]{0:T(128)}, u32[]{:S(2)}) copy-start(s32[128]{0:T(128)} %param.11) | copy-start | bytes 1540
  86.2 64.9 %copy-start.3 = (bf16[16,2048]{1,0:T(8,128)(2,1)S(1)}, bf16[16,2048]{1,0:T(8,128)(2,1)}, u32[]{:S(2)}) copy-start(bf16[16,2048]{1,0:T(8,128)(2,1)} %param.9) | copy-start | bytes 196612
  86.2 77.5 %copy-start.2 = (bf16[16,128,256]{2,1,0:T(8,128)(2,1)S(1)}, bf16[16,128,256]{2,1,0:T(8,128)(2,1)}, u32[]{:S(2)}) copy-start(bf16[16,128,256]{2,1,0:T(8,128)(2,1)} %param.10) | copy-start | bytes 3145732
  88.1 13.3 %collective-permute-start.7 = (f32[8,2,16,256]{3,2,1,0:T(8,128)S(1)}, f32[8,2,16,256]{3,2,1,0:T(8,128)S(1)}, u32[]{:S(2)}, u32[]{:S(2)}) collective-permute-start(f32[8,2,16,256]{3,2,1,0:T(8,128)S(1)} %slice_bitcast_fusion), channel_id=1, source_target_pairs={{0,1},{1,0},{2,3},{3,2},{4,5},{5,4},{6,7},{7,6},{8,9},{9,8},{10,11... | collective-permute-start | bytes 786440 | tf_op jit(solution)/shard_map/ppermute | solution.py:167
  101.5 38.3 %collective-permute-start.10 = (bf16[2,16,384]{2,1,0:T(8,128)(2,1)S(1)}, bf16[2,16,384]{2,1,0:T(8,128)(2,1)S(1)}, u32[]{:S(2)}, u32[]{:S(2)}) collective-permute-start(bf16[2,16,384]{2,1,0:T(8,128)(2,1)S(1)} %get-tuple-element.6), channel_id=1, source_target_pairs={{0,12},{1,13},{2,14},{3,15},{4,8},{5,9},{6,10},{7,11},{8,4},{9,5},... | collective-permute-start | bytes 73736 | tf_op jit(solution)/shard_map/ppermute | solution.py:167
  110.7 38.3 %collective-permute-start.11 = (bf16[2,16,384]{2,1,0:T(8,128)(2,1)S(1)}, bf16[2,16,384]{2,1,0:T(8,128)(2,1)S(1)}, u32[]{:S(2)}, u32[]{:S(2)}) collective-permute-start(bf16[2,16,384]{2,1,0:T(8,128)(2,1)S(1)} %get-tuple-element.7), channel_id=1, source_target_pairs={{0,24},{1,25},{2,26},{3,27},{4,28},{5,29},{6,30},{7,31},{8,16},{9,... | collective-permute-start | bytes 73736 | tf_op jit(solution)/shard_map/ppermute | solution.py:167
  115.2 35.9 %collective-permute-start.12 = (bf16[2,16,384]{2,1,0:T(8,128)(2,1)S(1)}, bf16[2,16,384]{2,1,0:T(8,128)(2,1)S(1)}, u32[]{:S(2)}, u32[]{:S(2)}) collective-permute-start(bf16[2,16,384]{2,1,0:T(8,128)(2,1)S(1)} %get-tuple-element.8), channel_id=1, source_target_pairs={{0,8},{1,9},{2,10},{3,11},{4,12},{5,13},{6,14},{7,15},{8,0},{9,1},... | collective-permute-start | bytes 73736 | tf_op jit(solution)/shard_map/ppermute | solution.py:167
  119.0 32.0 %collective-permute-start.13 = (bf16[2,16,384]{2,1,0:T(8,128)(2,1)S(1)}, bf16[2,16,384]{2,1,0:T(8,128)(2,1)S(1)}, u32[]{:S(2)}, u32[]{:S(2)}) collective-permute-start(bf16[2,16,384]{2,1,0:T(8,128)(2,1)S(1)} %get-tuple-element.10), channel_id=1, source_target_pairs={{0,28},{1,29},{2,30},{3,31},{4,24},{5,25},{6,26},{7,27},{8,20},{9,... | collective-permute-start | bytes 73736 | tf_op jit(solution)/shard_map/ppermute | solution.py:167
  121.1 30.0 %collective-permute-start.14 = (bf16[2,16,384]{2,1,0:T(8,128)(2,1)S(1)}, bf16[2,16,384]{2,1,0:T(8,128)(2,1)S(1)}, u32[]{:S(2)}, u32[]{:S(2)}) collective-permute-start(bf16[2,16,384]{2,1,0:T(8,128)(2,1)S(1)} %get-tuple-element.9), channel_id=1, source_target_pairs={{0,4},{1,5},{2,6},{3,7},{4,0},{5,1},{6,2},{7,3},{8,12},{9,13},{10,... | collective-permute-start | bytes 73736 | tf_op jit(solution)/shard_map/ppermute | solution.py:167
  139.8 14.4 %collective-permute-start.8 = (bf16[2,16,384]{2,1,0:T(8,128)(2,1)S(1)}, bf16[2,16,384]{2,1,0:T(8,128)(2,1)S(1)}, u32[]{:S(2)}, u32[]{:S(2)}) collective-permute-start(bf16[2,16,384]{2,1,0:T(8,128)(2,1)S(1)} %get-tuple-element.4), channel_id=1, source_target_pairs={{0,16},{1,17},{2,18},{3,19},{4,20},{5,21},{6,22},{7,23},{8,24},{9,... | collective-permute-start | bytes 73736 | tf_op jit(solution)/shard_map/ppermute | solution.py:167
  149.1 12.6 %collective-permute-start.9 = (bf16[2,16,384]{2,1,0:T(8,128)(2,1)S(1)}, bf16[2,16,384]{2,1,0:T(8,128)(2,1)S(1)}, u32[]{:S(2)}, u32[]{:S(2)}) collective-permute-start(bf16[2,16,384]{2,1,0:T(8,128)(2,1)S(1)} %get-tuple-element.5), channel_id=1, source_target_pairs={{0,20},{1,21},{2,22},{3,23},{4,16},{5,17},{6,18},{7,19},{8,28},{9,... | collective-permute-start | bytes 73736 | tf_op jit(solution)/shard_map/ppermute | solution.py:167
  161.8 5.6 %collective-permute-start.15 = (f32[16,256]{1,0:T(8,128)S(1)}, f32[16,256]{1,0:T(8,128)S(1)}, u32[]{:S(2)}, u32[]{:S(2)}) collective-permute-start(f32[16,256]{1,0:T(8,128)S(1)} %slice_bitcast_fusion.3), channel_id=1, source_target_pairs={{0,2},{1,3},{2,0},{3,1},{4,6},{5,7},{6,4},{7,5},{8,10},{9,11},{10,... | collective-permute-start | bytes 49160 | tf_op jit(solution)/shard_map/ppermute | solution.py:167
